TPU v7x, 32 devices: a whole 2x2x4 slice. The times are simulated.
32 devices in a mesh: dp: 4 (over y, x), expert: 8 (over z, core).
Axes of the slice: x: 2, y: 2, z: 4, core: 2. Of those that a mesh axis runs over, the one named last changes fastest.
Arguments:
- tokens: bfloat16 [4096, 2048], P(('dp', 'expert')), may hold values from -6 to 6
- cotangent: bfloat16 [4096, 2048], P(('dp', 'expert')), may hold values from -6 to 6
- attention_norm_gain: float32 [2048], replicated, may hold values from 0.25 to 1.75
- experts_norm_gain: float32 [2048], replicated, may hold values from 0.25 to 1.75
- attention_query_key_value: bfloat16 [2048, 6144], P(None, 'expert'), may hold values from -0.125 to 0.125
- attention_output_weight: bfloat16 [2048, 2048], P('expert'), may hold values from -2 to 2
- router_projection: bfloat16 [2048, 8], replicated, may hold values from -0.0625 to 0.0625
- shared_gate_up_weight: bfloat16 [2, 2048, 5632], P(None, None, 'expert'), may hold values from -0.125 to 0.125
- shared_down_weight: bfloat16 [5632, 2048], P('expert'), may hold values from -0.078125 to 0.078125
- shared_gate_vector: bfloat16 [2048], replicated, may hold values from -0.125 to 0.125
- expert_gate_up_weight: bfloat16 [8, 2, 2048, 1408], P('expert'), may hold values from -0.125 to 0.125
- expert_down_weight: bfloat16 [8, 1408, 2048], P('expert'), may hold values from -0.15625 to 0.15625
- routes: int32 [4096, 4], P(('dp', 'expert')), may hold values from 0 to 7, all different within a row; in each aligned block of 128 rows (0 to 127, 128 to 255, ...) at most 72 rows name the same one
- lengths: int32 [4], P('dp'), may hold values from 256 to 1024, as said below
- adapter_slot_index: int32 [4], P('dp'), may hold values from 0 to 7
- attention_adapter_first: bfloat16 [4, 2048, 128], replicated, may hold values from -0.125 to 0.125
- attention_adapter_second: bfloat16 [4, 128, 2048], replicated, may hold values from -0.75 to 0.75
- router_adapter_first: bfloat16 [2048, 128], replicated, may hold values from -0.125 to 0.125
- router_adapter_second: bfloat16 [128, 8], replicated, may hold values from -0.375 to 0.375
- shared_adapter_first: bfloat16 [2, 2048, 128], replicated, may hold values from -0.125 to 0.125
- shared_adapter_second: bfloat16 [2, 128, 5632], replicated, may hold values from -0.75 to 0.75
- shared_down_adapter_first: bfloat16 [5632, 128], replicated, may hold values from -0.078125 to 0.078125
- shared_down_adapter_second: bfloat16 [128, 2048], replicated, may hold values from -0.75 to 0.75
- expert_adapter_first: bfloat16 [8, 2, 2048, 128], P('expert'), may hold values from -0.125 to 0.125
- expert_adapter_second: bfloat16 [8, 2, 128, 1408], P('expert'), may hold values from -0.75 to 0.75
- expert_down_adapter_first: bfloat16 [8, 1408, 128], P('expert'), may hold values from -0.15625 to 0.15625
- expert_down_adapter_second: bfloat16 [8, 128, 2048], P('expert'), may hold values from -0.75 to 0.75
Outputs:
- layer_out: bfloat16 [4096, 2048], P(('dp', 'expert'))
- tokens_grad: float32 [4096, 2048], P(('dp', 'expert'))
- grad_attn_lora_a: float32 [4, 2048, 128], P(None, None, ('dp', 'expert'))
- grad_attn_lora_b: float32 [4, 128, 2048], P(None, ('dp', 'expert'))
- grad_router_lora_a: float32 [2048, 128], P(None, ('dp', 'expert'))
- grad_router_lora_b: float32 [128, 8], P(('dp', 'expert'))
- grad_shared_lora_a: float32 [2, 2048, 128], P(None, None, ('dp', 'expert'))
- grad_shared_lora_b: float32 [2, 128, 5632], P(None, ('dp', 'expert'))
- grad_shared_down_lora_a: float32 [5632, 128], P(None, ('dp', 'expert'))
- grad_shared_down_lora_b: float32 [128, 2048], P(('dp', 'expert'))
- grad_expert_lora_a: float32 [8, 2, 2048, 128], P('expert')
- grad_expert_lora_b: float32 [8, 2, 128, 1408], P('expert')
- grad_expert_down_lora_a: float32 [8, 1408, 128], P('expert')
- grad_expert_down_lora_b: float32 [8, 128, 2048], P('expert')
Inputs may be any that keep to these rules, and one draw needn't show every extreme that they name: `routes`: each row names 4 different experts. Among the rows of one device no expert is named more than 72 times, and in some device's rows one expert is named exactly 72 times. `lengths`: one sequence slot keeps all 1024 tokens in every draw.
All inputs are finite; a program needn't handle non-finite values.
Results may differ from a plain program's by a relative error of at most 0.02.
Values may be sent and summed in bfloat16 or wider, within the bound.
A program may use at most 512 MiB of HBM per device.

v0:
```python
import math

import jax
import jax.numpy as jnp
from jax import lax
from jax.sharding import PartitionSpec as P

HEADS = 16
HEAD_DIM = 128
ADAPTER_RANK = 16
ADAPTER_COUNT = 8
BLOCK = 256
SEQ_MAX = 2048


NORM_EPS = 1e-06
ROPE_BASE = 1000000.0
MASKED = -1e30


def narrow_product(left_side, right_side):
    return jnp.dot(left_side, right_side, preferred_element_type=jnp.float32)


def rms_forward(values, gain_vector):
    factor = lax.rsqrt(jnp.mean(values * values, axis=-1, keepdims=True) + NORM_EPS)
    return (values * factor * gain_vector, factor)


def rms_backward(values, factor, gain_vector, upstream):
    weighted = upstream * gain_vector
    return factor * weighted - values * (factor * factor * factor) * jnp.mean(
        values * weighted, axis=-1, keepdims=True
    )


def rope_tables(positions, head_width):
    half_width = head_width // 2
    inverse = ROPE_BASE ** (-(jnp.arange(half_width).astype(jnp.float32) * 2.0 / head_width))
    angles = positions.astype(jnp.float32)[:, None] * inverse[None, :]
    return (jnp.cos(angles), jnp.sin(angles))


def rotate(values, cosine_table, sine_table, direction):
    half_width = values.shape[-1] // 2
    first_half = values[..., :half_width]
    second_half = values[..., half_width:]
    cosine_part = cosine_table[:, None, :]
    sine_part = sine_table[:, None, :] * direction
    return jnp.concatenate(
        [
            first_half * cosine_part - second_half * sine_part,
            second_half * cosine_part + first_half * sine_part,
        ],
        axis=-1,
    )


def adapter_middle(input_rows, down_maps, slot_picker):
    product = jnp.einsum("nd,jdr->jnr", input_rows, down_maps, preferred_element_type=jnp.float32)
    return (product * slot_picker[None]).astype(jnp.bfloat16)


def adapter_wrapper(inner_value, up_maps):
    return jnp.einsum("jnr,jro->jno", inner_value, up_maps, preferred_element_type=jnp.float32)


def adapter_back(input_rows, inner_value, down_maps, up_maps, upstream, slot_picker_narrow):
    grad_inner = (
        jnp.einsum("jno,jro->jnr", upstream, up_maps, preferred_element_type=jnp.float32).astype(
            jnp.bfloat16
        )
        * slot_picker_narrow[None]
    )
    grad_down = jnp.einsum(
        "nd,jnr->jdr", input_rows, grad_inner, preferred_element_type=jnp.float32
    )
    grad_up = jnp.einsum("jnr,jno->jro", inner_value, upstream, preferred_element_type=jnp.float32)
    grad_inputs = jnp.einsum(
        "jnr,jdr->nd", grad_inner, down_maps, preferred_element_type=jnp.float32
    )
    return (grad_inputs, grad_down, grad_up)


def gated_back(gate_value, up_value, grad_hidden):
    sigmoid_gate = jax.nn.sigmoid(gate_value)
    grad_gate = grad_hidden * up_value * sigmoid_gate * (1.0 + gate_value * (1.0 - sigmoid_gate))
    grad_up = grad_hidden * gate_value * sigmoid_gate
    return jnp.stack([grad_gate, grad_up]).astype(jnp.bfloat16)


def on_device(
    tokens,
    cotangent,
    attention_norm_gain,
    experts_norm_gain,
    attention_query_key_value,
    attention_output_weight,
    router_projection,
    shared_gate_up_weight,
    shared_down_weight,
    shared_gate_vector,
    expert_gate_up_weight,
    expert_down_weight,
    routes,
    lengths,
    adapter_slot_index,
    attention_adapter_first,
    attention_adapter_second,
    router_adapter_first,
    router_adapter_second,
    shared_adapter_first,
    shared_adapter_second,
    shared_down_adapter_first,
    shared_down_adapter_second,
    expert_adapter_first,
    expert_adapter_second,
    expert_down_adapter_first,
    expert_down_adapter_second,
):
    count_rows, model_width_size = tokens.shape
    head_width = HEAD_DIM
    head_count = HEADS
    owners = lax.axis_size("expert")
    owner_index = lax.axis_index("expert")
    experts = router_projection.shape[1]
    top_count = routes.shape[1]
    capacity = (count_rows * top_count * 9 + 8 * experts - 1) // (8 * experts)
    seq_length = min(SEQ_MAX, count_rows * owners)
    key_step = min(512, seq_length)
    slot_count = lengths.shape[0]
    score_scale = 1.0 / math.sqrt(head_width)
    slot_range = jnp.arange(slot_count, dtype=jnp.int32)

    def slot_lookup(slot_values, lookup_table):
        return jnp.sum(
            jnp.where(slot_values[:, None] == slot_range[None, :], lookup_table[None, :], 0), axis=1
        )

    own_index = owner_index * count_rows + jnp.arange(count_rows, dtype=jnp.int32)
    query_slot = own_index // seq_length
    query_pos = own_index % seq_length
    query_block = query_pos // BLOCK
    slot_start = owner_index * count_rows // seq_length * seq_length
    chosen = slot_lookup(query_slot, adapter_slot_index)
    adapter_hot = chosen[:, None] == jnp.arange(ADAPTER_COUNT, dtype=jnp.int32)[None, :]
    slot_picker = jnp.repeat(adapter_hot.astype(jnp.float32), ADAPTER_RANK, axis=1)
    slot_picker_narrow = slot_picker.astype(jnp.bfloat16)
    cosine_table, sine_table = rope_tables(query_pos, head_width)
    shaped = (count_rows, head_count, head_width)

    def key_allowed(start_row, row_count):
        key_index = start_row + jnp.arange(row_count, dtype=jnp.int32)
        key_slot = key_index // seq_length
        key_pos = key_index % seq_length
        key_live = key_pos < slot_lookup(key_slot, lengths)
        return (
            (query_slot[:, None] == key_slot[None, :])
            & ((key_pos // BLOCK)[None, :] <= query_block[:, None])
            & key_live[None, :]
        )

    def scores_for(query_values, key_rows, allowed):
        raw_scores = (
            jnp.einsum("qhd,khd->hqk", query_values, key_rows, preferred_element_type=jnp.float32)
            * score_scale
        )
        return jnp.where(allowed[None], raw_scores, MASKED)

    def block_rows(source_table, start_row):
        return lax.dynamic_slice_in_dim(source_table, start_row, key_step, 0).reshape(
            key_step, head_count, head_width
        )

    input_rows = tokens.astype(jnp.float32)
    qkv_full, projection_complete, shared_full, shared_down_full = (
        lax.all_gather(attention_query_key_value, "expert", axis=1, tiled=True),
        lax.all_gather(attention_output_weight, "expert", axis=0, tiled=True),
        lax.all_gather(shared_gate_up_weight, "expert", axis=2, tiled=True),
        lax.all_gather(shared_down_weight, "expert", axis=0, tiled=True),
    )
    normed_first, factor_first = rms_forward(input_rows, attention_norm_gain)
    first_narrow = normed_first.astype(jnp.bfloat16)
    attention_middle = adapter_middle(first_narrow, attention_adapter_first[:3], slot_picker)
    projected = jnp.einsum(
        "nd,djo->jno",
        first_narrow,
        qkv_full.reshape(model_width_size, 3, model_width_size),
        preferred_element_type=jnp.float32,
    ) + adapter_wrapper(attention_middle, attention_adapter_second[:3])
    query_low = rotate(projected[0].reshape(shaped), cosine_table, sine_table, 1.0).astype(
        jnp.bfloat16
    )
    key_low = (
        rotate(projected[1].reshape(shaped), cosine_table, sine_table, 1.0)
        .astype(jnp.bfloat16)
        .reshape(count_rows, model_width_size)
    )
    value_low = projected[2].astype(jnp.bfloat16)
    keys_all, values_all = (
        lax.all_gather(key_low, "expert", axis=0, tiled=True),
        lax.all_gather(value_low, "expert", axis=0, tiled=True),
    )
    starts = slot_start + jnp.arange(seq_length // key_step, dtype=jnp.int32) * key_step

    def max_step(carry_state, start_row):
        running_max, running_sum = carry_state
        allowed = key_allowed(start_row, key_step)
        scores = scores_for(query_low, block_rows(keys_all, start_row), allowed)
        new_max = jnp.maximum(running_max, jnp.max(scores, axis=2))
        new_sum = running_sum * jnp.exp(running_max - new_max) + jnp.sum(
            jnp.exp(scores - new_max[:, :, None]) * allowed[None], axis=2
        )
        return ((new_max, new_sum), None)

    start_carry = (
        jnp.full((head_count, count_rows), MASKED, jnp.float32),
        jnp.zeros((head_count, count_rows), jnp.float32),
    )
    (final_max, final_sum), unused = lax.scan(max_step, start_carry, starts)
    log_total = final_max + jnp.log(final_sum)

    def value_step(total_value, start_row):
        allowed = key_allowed(start_row, key_step)
        scores = scores_for(query_low, block_rows(keys_all, start_row), allowed)
        weights = jnp.exp(scores - log_total[:, :, None]).astype(jnp.bfloat16)
        return (
            total_value
            + jnp.einsum(
                "hqk,khd->qhd",
                weights,
                block_rows(values_all, start_row),
                preferred_element_type=jnp.float32,
            ),
            None,
        )

    attention_result, unused = lax.scan(value_step, jnp.zeros(shaped, jnp.float32), starts)
    attention_result_narrow = attention_result.reshape(count_rows, model_width_size).astype(
        jnp.bfloat16
    )
    output_middle = adapter_middle(
        attention_result_narrow, attention_adapter_first[3:], slot_picker
    )
    attention_output_value = (
        narrow_product(attention_result_narrow, projection_complete)
        + adapter_wrapper(output_middle, attention_adapter_second[3:])[0]
    )
    residual_stream = input_rows + attention_output_value
    normed_second, factor_second = rms_forward(residual_stream, experts_norm_gain)
    second_narrow = normed_second.astype(jnp.bfloat16)
    router_middle = adapter_middle(second_narrow, router_adapter_first[None], slot_picker)
    router_scores = (
        narrow_product(second_narrow, router_projection)
        + adapter_wrapper(router_middle, router_adapter_second[None])[0]
    )
    route_hits = routes[:, :, None] == jnp.arange(experts, dtype=jnp.int32)[None, None, :]
    picked = jnp.sum(jnp.where(route_hits, router_scores[:, None, :], 0.0), axis=2)
    gate_weights = jax.nn.softmax(picked, axis=1)
    flat_routes = routes.reshape(-1)
    flat_hits = (flat_routes[:, None] == jnp.arange(experts, dtype=jnp.int32)[None, :]).astype(
        jnp.int32
    )
    slot_ranks = jnp.sum((jnp.cumsum(flat_hits, axis=0) - 1) * flat_hits, axis=1)
    slot_of = (flat_routes * capacity + slot_ranks).reshape(count_rows, top_count)
    placement_hits = (
        slot_of[:, :, None] == jnp.arange(experts * capacity, dtype=jnp.int32)[None, None, :]
    )
    spread = jnp.sum(placement_hits.astype(jnp.bfloat16), axis=1)
    send_rows = jnp.einsum(
        "ts,td->sd", spread, second_narrow, preferred_element_type=jnp.float32
    ).astype(jnp.bfloat16)
    send_hot = jnp.einsum(
        "ts,ta->sa", spread, adapter_hot.astype(jnp.bfloat16), preferred_element_type=jnp.float32
    ).astype(jnp.bfloat16)
    received_rows, received_hot = (
        lax.all_to_all(
            send_rows.reshape(experts, capacity, model_width_size),
            "expert",
            split_axis=0,
            concat_axis=0,
            tiled=True,
        ),
        lax.all_to_all(
            send_hot.reshape(experts, capacity, ADAPTER_COUNT),
            "expert",
            split_axis=0,
            concat_axis=0,
            tiled=True,
        ),
    )
    expert_input_rows = received_rows.reshape(experts * capacity, model_width_size)
    expert_picker = jnp.repeat(
        received_hot.reshape(experts * capacity, ADAPTER_COUNT).astype(jnp.float32),
        ADAPTER_RANK,
        axis=1,
    )
    expert_selector_low = expert_picker.astype(jnp.bfloat16)
    gate_up_maps = expert_gate_up_weight[0]
    expert_middle = adapter_middle(expert_input_rows, expert_adapter_first[0], expert_picker)
    expert_pre = jnp.einsum(
        "nd,jdf->jnf", expert_input_rows, gate_up_maps, preferred_element_type=jnp.float32
    ) + adapter_wrapper(expert_middle, expert_adapter_second[0])
    expert_hidden_units = (jax.nn.silu(expert_pre[0]) * expert_pre[1]).astype(jnp.bfloat16)
    down_middle = adapter_middle(
        expert_hidden_units, expert_down_adapter_first[0][None], expert_picker
    )
    expert_result = (
        narrow_product(expert_hidden_units, expert_down_weight[0])
        + adapter_wrapper(down_middle, expert_down_adapter_second[0][None])[0]
    ).astype(jnp.bfloat16)
    returned = lax.all_to_all(
        expert_result.reshape(experts, capacity, model_width_size),
        "expert",
        split_axis=0,
        concat_axis=0,
        tiled=True,
    )
    returned_rows = (
        jnp.take(
            returned.reshape(experts * capacity, model_width_size), slot_of.reshape(-1), axis=0
        )
        .reshape(count_rows, top_count, model_width_size)
        .astype(jnp.float32)
    )
    mixture = jnp.sum(gate_weights[:, :, None] * returned_rows, axis=1)
    shared_middle = adapter_middle(second_narrow, shared_adapter_first, slot_picker)
    shared_pre = jnp.einsum(
        "nd,jdf->jnf", second_narrow, shared_full, preferred_element_type=jnp.float32
    ) + adapter_wrapper(shared_middle, shared_adapter_second)
    shared_hidden_units = (jax.nn.silu(shared_pre[0]) * shared_pre[1]).astype(jnp.bfloat16)
    shared_down_middle = adapter_middle(
        shared_hidden_units, shared_down_adapter_first[None], slot_picker
    )
    shared_output_value = (
        narrow_product(shared_hidden_units, shared_down_full)
        + adapter_wrapper(shared_down_middle, shared_down_adapter_second[None])[0]
    )
    shared_weight = jax.nn.sigmoid(
        jnp.dot(second_narrow, shared_gate_vector, preferred_element_type=jnp.float32)
    )
    layer_out = (residual_stream + mixture + shared_weight[:, None] * shared_output_value).astype(
        jnp.bfloat16
    )
    upstream = cotangent.astype(jnp.float32)
    qkv_back, proj_back, shared_back, shared_down_back = (
        qkv_full,
        projection_complete,
        shared_full,
        shared_down_full,
    )
    gate_grads = jnp.sum(upstream[:, None, :] * returned_rows, axis=2)
    weighted_place = jnp.sum(jnp.where(placement_hits, gate_weights[:, :, None], 0.0), axis=1)
    send_grads = jnp.einsum(
        "ts,td->sd",
        weighted_place,
        upstream,
        precision=lax.Precision.HIGHEST,
        preferred_element_type=jnp.float32,
    ).astype(jnp.bfloat16)
    arrived = lax.all_to_all(
        send_grads.reshape(experts, capacity, model_width_size),
        "expert",
        split_axis=0,
        concat_axis=0,
        tiled=True,
    )
    expert_upstream = arrived.reshape(experts * capacity, model_width_size)
    down_grad_inputs, down_grad_a, down_grad_b = adapter_back(
        expert_hidden_units,
        down_middle,
        expert_down_adapter_first[0][None],
        expert_down_adapter_second[0][None],
        expert_upstream[None],
        expert_selector_low,
    )
    expert_grad_hidden = (
        jnp.einsum(
            "nd,fd->nf", expert_upstream, expert_down_weight[0], preferred_element_type=jnp.float32
        )
        + down_grad_inputs
    )
    expert_grad_pre = gated_back(expert_pre[0], expert_pre[1], expert_grad_hidden)
    in_grad_inputs, in_grad_a, in_grad_b = adapter_back(
        expert_input_rows,
        expert_middle,
        expert_adapter_first[0],
        expert_adapter_second[0],
        expert_grad_pre,
        expert_selector_low,
    )
    expert_grad_inputs = (
        jnp.einsum("jnf,jdf->nd", expert_grad_pre, gate_up_maps, preferred_element_type=jnp.float32)
        + in_grad_inputs
    )
    sent_back = lax.all_to_all(
        expert_grad_inputs.astype(jnp.bfloat16).reshape(experts, capacity, model_width_size),
        "expert",
        split_axis=0,
        concat_axis=0,
        tiled=True,
    )
    centered = gate_weights * (
        gate_grads - jnp.sum(gate_weights * gate_grads, axis=1, keepdims=True)
    )
    logit_grads = jnp.sum(jnp.where(route_hits, centered[:, :, None], 0.0), axis=1).astype(
        jnp.bfloat16
    )
    router_grad_inputs, router_grad_a, router_grad_b = adapter_back(
        second_narrow,
        router_middle,
        router_adapter_first[None],
        router_adapter_second[None],
        logit_grads[None],
        slot_picker_narrow,
    )
    second_grad = (
        jnp.einsum("ne,de->nd", logit_grads, router_projection, preferred_element_type=jnp.float32)
        + router_grad_inputs
    )
    value_grads = (shared_weight[:, None] * upstream).astype(jnp.bfloat16)
    weight_grads = (
        jnp.sum(upstream * shared_output_value, axis=1) * shared_weight * (1.0 - shared_weight)
    )
    sdown_grad_inputs, sdown_grad_a, sdown_grad_b = adapter_back(
        shared_hidden_units,
        shared_down_middle,
        shared_down_adapter_first[None],
        shared_down_adapter_second[None],
        value_grads[None],
        slot_picker_narrow,
    )
    shared_grad_hidden = (
        jnp.einsum("nd,fd->nf", value_grads, shared_down_back, preferred_element_type=jnp.float32)
        + sdown_grad_inputs
    )
    shared_preactivation_gradient = gated_back(shared_pre[0], shared_pre[1], shared_grad_hidden)
    sin_grad_inputs, sin_grad_a, sin_grad_b = adapter_back(
        second_narrow,
        shared_middle,
        shared_adapter_first,
        shared_adapter_second,
        shared_preactivation_gradient,
        slot_picker_narrow,
    )
    second_grad = (
        second_grad
        + jnp.einsum(
            "jnf,jdf->nd",
            shared_preactivation_gradient,
            shared_back,
            preferred_element_type=jnp.float32,
        )
        + sin_grad_inputs
        + weight_grads[:, None] * shared_gate_vector.astype(jnp.float32)[None, :]
    )
    second_grad = second_grad + jnp.einsum(
        "ts,sd->td",
        spread,
        sent_back.reshape(experts * capacity, model_width_size),
        preferred_element_type=jnp.float32,
    )
    residual_grad = upstream + rms_backward(
        residual_stream, factor_second, experts_norm_gain, second_grad
    )
    attention_upstream_gradient = residual_grad.astype(jnp.bfloat16)
    out_grad_inputs, out_grad_a, out_grad_b = adapter_back(
        attention_result_narrow,
        output_middle,
        attention_adapter_first[3:],
        attention_adapter_second[3:],
        attention_upstream_gradient[None],
        slot_picker_narrow,
    )
    attended_grad = (
        (
            jnp.einsum(
                "ne,de->nd",
                attention_upstream_gradient,
                proj_back,
                preferred_element_type=jnp.float32,
            )
            + out_grad_inputs
        )
        .astype(jnp.bfloat16)
        .reshape(shaped)
    )
    row_delta = jnp.transpose(jnp.sum(attended_grad.astype(jnp.float32) * attention_result, axis=2))
    keys_back, values_back = (
        lax.all_gather(key_low, "expert", axis=0, tiled=True),
        lax.all_gather(value_low, "expert", axis=0, tiled=True),
    )

    def score_grads(start_row, row_count, key_rows, value_rows):
        allowed = key_allowed(start_row, row_count)
        scores = scores_for(query_low, key_rows, allowed)
        probabilities = jnp.exp(scores - log_total[:, :, None])
        prob_grads = jnp.einsum(
            "qhd,khd->hqk", attended_grad, value_rows, preferred_element_type=jnp.float32
        )
        return (
            probabilities,
            (probabilities * (prob_grads - row_delta[:, :, None])).astype(jnp.bfloat16),
        )

    def query_step(total_grad, start_row):
        key_rows = block_rows(keys_back, start_row)
        probabilities, score_low = score_grads(
            start_row, key_step, key_rows, block_rows(values_back, start_row)
        )
        return (
            total_grad
            + jnp.einsum("hqk,khd->qhd", score_low, key_rows, preferred_element_type=jnp.float32),
            None,
        )

    query_grad, unused = lax.scan(query_step, jnp.zeros(shaped, jnp.float32), starts)
    row_count = count_rows * lax.axis_size("expert")

    def one_piece(begin_row):
        key_rows = lax.dynamic_slice_in_dim(keys_back, begin_row, key_step, 0).reshape(
            key_step, head_count, head_width
        )
        value_rows = lax.dynamic_slice_in_dim(values_back, begin_row, key_step, 0).reshape(
            key_step, head_count, head_width
        )
        probabilities, score_low = score_grads(begin_row, key_step, key_rows, value_rows)
        key_part = (
            jnp.einsum("hqk,qhd->khd", score_low, query_low, preferred_element_type=jnp.float32)
            * score_scale
        )
        value_part = jnp.einsum(
            "hqk,qhd->khd",
            probabilities.astype(jnp.bfloat16),
            attended_grad,
            preferred_element_type=jnp.float32,
        )
        return jnp.concatenate(
            [
                key_part.reshape(key_step, model_width_size),
                value_part.reshape(key_step, model_width_size),
            ],
            axis=1,
        )

    pieces = lax.map(one_piece, key_step * jnp.arange(row_count // key_step, dtype=jnp.int32))
    key_value_grads = lax.psum_scatter(
        pieces.reshape(row_count, 2 * model_width_size).astype(jnp.bfloat16),
        "expert",
        scatter_dimension=0,
        tiled=True,
    ).astype(jnp.float32)
    query_pre_grad = rotate(query_grad * score_scale, cosine_table, sine_table, -1.0).astype(
        jnp.bfloat16
    )
    key_pre_grad = rotate(
        key_value_grads[:, :model_width_size].reshape(shaped), cosine_table, sine_table, -1.0
    ).astype(jnp.bfloat16)
    value_pre_grad = key_value_grads[:, model_width_size:].astype(jnp.bfloat16)
    preactivation_gradients = jnp.stack(
        [
            query_pre_grad.reshape(count_rows, model_width_size),
            key_pre_grad.reshape(count_rows, model_width_size),
            value_pre_grad,
        ]
    )
    qkv_grad_inputs, qkv_grad_a, qkv_grad_b = adapter_back(
        first_narrow,
        attention_middle,
        attention_adapter_first[:3],
        attention_adapter_second[:3],
        preactivation_gradients,
        slot_picker_narrow,
    )
    first_grad = (
        jnp.einsum(
            "jno,djo->nd",
            preactivation_gradients,
            qkv_back.reshape(model_width_size, 3, model_width_size),
            preferred_element_type=jnp.float32,
        )
        + qkv_grad_inputs
    )
    tokens_grad = residual_grad + rms_backward(
        input_rows, factor_first, attention_norm_gain, first_grad
    )
    attn_grad_a = jnp.concatenate([qkv_grad_a, out_grad_a], axis=0)
    attn_grad_b = jnp.concatenate([qkv_grad_b, out_grad_b], axis=0)
    summed = (
        lax.psum_scatter(attn_grad_a, ("dp", "expert"), scatter_dimension=2, tiled=True),
        lax.psum_scatter(attn_grad_b, ("dp", "expert"), scatter_dimension=1, tiled=True),
        lax.psum_scatter(router_grad_a[0], ("dp", "expert"), scatter_dimension=1, tiled=True),
        lax.psum_scatter(router_grad_b[0], ("dp", "expert"), scatter_dimension=0, tiled=True),
        lax.psum_scatter(sin_grad_a, ("dp", "expert"), scatter_dimension=2, tiled=True),
        lax.psum_scatter(sin_grad_b, ("dp", "expert"), scatter_dimension=1, tiled=True),
        lax.psum_scatter(sdown_grad_a[0], ("dp", "expert"), scatter_dimension=1, tiled=True),
        lax.psum_scatter(sdown_grad_b[0], ("dp", "expert"), scatter_dimension=0, tiled=True),
    )
    expert_summed = (
        lax.psum(in_grad_a[None].astype(jnp.bfloat16), "dp").astype(jnp.float32),
        lax.psum(in_grad_b[None].astype(jnp.bfloat16), "dp").astype(jnp.float32),
        lax.psum(down_grad_a.astype(jnp.bfloat16), "dp").astype(jnp.float32),
        lax.psum(down_grad_b.astype(jnp.bfloat16), "dp").astype(jnp.float32),
    )
    return (
        layer_out,
        tokens_grad,
        summed[0],
        summed[1],
        summed[2],
        summed[3],
        summed[4],
        summed[5],
        summed[6],
        summed[7],
        expert_summed[0],
        expert_summed[1],
        expert_summed[2],
        expert_summed[3],
    )


def solution(mesh):
    return jax.shard_map(
        on_device,
        mesh=mesh,
        in_specs=(
            P(("dp", "expert"), None),
            P(("dp", "expert"), None),
            P(),
            P(),
            P(None, "expert"),
            P("expert", None),
            P(),
            P(None, None, "expert"),
            P("expert", None),
            P(),
            P("expert", None, None, None),
            P("expert", None, None),
            P(("dp", "expert"), None),
            P("dp"),
            P("dp"),
            P(),
            P(),
            P(),
            P(),
            P(),
            P(),
            P(),
            P(),
            P("expert", None, None, None),
            P("expert", None, None, None),
            P("expert", None, None),
            P("expert", None, None),
        ),
        out_specs=(
            P(("dp", "expert"), None),
            P(("dp", "expert"), None),
            P(None, None, ("dp", "expert")),
            P(None, ("dp", "expert"), None),
            P(None, ("dp", "expert")),
            P(("dp", "expert"), None),
            P(None, None, ("dp", "expert")),
            P(None, ("dp", "expert"), None),
            P(None, ("dp", "expert")),
            P(("dp", "expert"), None),
            P("expert", None, None, None),
            P("expert", None, None, None),
            P("expert", None, None),
            P("expert", None, None),
        ),
        check_vma=False,
    )
```

profile of v0, /device:TPU:11, one launch (start us, length us, event | category | flops | bytes accessed | tf_op | source)
XLA Modules:
  0.0 1913.3 jit_solution(4166304495779683689)
XLA Ops:
  16.8 214.2 %all-gather.8.cloned.1.call-done = bf16[2048,6144]{0,1:T(8,128)(2,1)} async-done(((bf16[2048,768]{0,1:T(8,128)(2,1)}), bf16[2048,6144]{0,1:T(8,128)(2,1)}) %all-gather.8.cloned.1.call-update) | async-done | bytes 25165840 | tf_op jit(solution)/shard_map/all_gather | solution.py:177
  231.0 14.7 fusion.222
  304.6 40.9 %all-gather.10.cloned.1.call-done = bf16[1024,2048]{0,1:T(8,128)(2,1)} async-done(((bf16[128,2048]{0,1:T(8,128)(2,1)}), bf16[1024,2048]{0,1:T(8,128)(2,1)}) %all-gather.10.cloned.1.call-update) | async-done | bytes 4194320 | tf_op jit(solution)/shard_map/all_gather | solution.py:201
  345.5 32.1 %while.66 = (s32[]{:T(128)}, f32[16,128]{1,0:T(8,128)S(1)}, f32[16,128]{1,0:T(8,128)}, s32[2]{0:T(128)}, s32[1]{0:T(128)}, /*index=5*/bf16[1024,2048]{0,1:T(8,12...) while((s32[]{:T(128)}, f32[16,128]{1,0:T(8,128)S(1)}, ...), condition=%wide.region_4.5_spmd.clone.clone.clone, body=%wide.region_1.4_spmd.clone.clone.clone.sunk | while | flops 277196160 | bytes 16108794 | solution.py:220
  378.3 35.1 %while.67 = (s32[]{:T(128)}, f32[128,16,128]{0,2,1:T(8,128)}, s32[2]{0:T(128)}, bf16[1024,2048]{0,1:T(8,128)(2,1)}, s32[1]{0:T(128)}, /*index=5*/bf16[1024,2048]...) while((s32[]{:T(128)}, f32[128,16,128]{0,2,1:T(8,128)}, ...), condition=%wide.region_6.7_spmd.clone.clone.clone, body=%wide.region_5.6_spmd.clone.clone.clone.sunk | while | flops 541885824 | bytes 15355081 | solution.py:238
  417.2 10.3 all-gather.12.cloned.1.call-done
  450.4 116.1 %all-to-all-done = bf16[8,72,2048]{2,1,0:T(8,128)(2,1)} async-done(((bf16[8,72,2048]{2,1,0:T(8,128)(2,1)}), bf16[8,72,2048]{2,1,0:T(8,128)(2,1)}, u32[]{:S(2)}, u32[]{:S(2)}) %all-to-all-start) | async-done | bytes 2359328 | tf_op jit(solution)/shard_map/all_to_all | solution.py:277
  569.5 11.2 fusion.73
  616.5 106.6 %all-to-all-done.2 = bf16[8,72,2048]{2,1,0:T(8,128)(2,1)} async-done(((bf16[8,72,2048]{2,1,0:T(8,128)(2,1)}), bf16[8,72,2048]{2,1,0:T(8,128)(2,1)}, u32[]{:S(2)}, u32[]{:S(2)}) %all-to-all-start.2) | async-done | bytes 2359328 | tf_op jit(solution)/shard_map/all_to_all | solution.py:312
  775.6 83.6 %all-to-all-done.3 = bf16[8,72,2048]{2,1,0:T(8,128)(2,1)} async-done(((bf16[8,72,2048]{2,1,0:T(8,128)(2,1)}), bf16[8,72,2048]{2,1,0:T(8,128)(2,1)}, u32[]{:S(2)}, u32[]{:S(2)}) %all-to-all-start.3) | async-done | bytes 2359328 | tf_op jit(solution)/shard_map/all_to_all | solution.py:361
  894.3 123.1 %all-gather.14.cloned.1.call-done = bf16[2,2048,5632]{1,2,0:T(8,128)(2,1)} async-done(((bf16[2,2048,704]{1,2,0:T(8,128)(2,1)}), bf16[2,2048,5632]{1,2,0:T(8,128)(2,1)}) %all-gather.14.cloned.1.call-update) | async-done | bytes 46137360 | tf_op jit(solution)/shard_map/all_gather | solution.py:179
  1017.5 24.6 %convolution_bitcast_fusion.2 = f32[2,128,5632]{2,1,0:T(8,128)} fusion(bf16[2,2048,5632]{1,2,0:T(8,128)(2,1)} %all-gather.14.cloned.1.call-done, bf16[128,2048]{1,0:T(8,128)(2,1)S(1)} %multiply_convert_fusion.3), kind=kOutput, calls=%fused_computation.184 | convolution fusion | flops 5905580032 | bytes 52428800 | tf_op jit(solution)/shard_map/nd,jdf->jnf/dot_general | solution.py:328
  1050.4 173.0 %all-gather.16.cloned.1.call-done = bf16[5632,2048]{1,0:T(8,128)(2,1)} async-done(((bf16[704,2048]{1,0:T(8,128)(2,1)}), bf16[5632,2048]{1,0:T(8,128)(2,1)}) %all-gather.16.cloned.1.call-update) | async-done | bytes 23068688 | tf_op jit(solution)/shard_map/all_gather | solution.py:180
  1223.4 12.7 fusion.117
  1238.1 13.9 fusion.249
  1260.4 18.2 convolution_bitcast_fusion.12
  1298.1 56.9 %while.65 = (s32[]{:T(128)}, bf16[2,512,4096]{1,2,0:T(8,128)(2,1)}, s32[2]{0:T(128)S(1)}, s32[1]{0:T(128)}, bf16[1024,2048]{0,1:T(8,128)(2,1)}, /*index=5*/bf16[...) while((s32[]{:T(128)}, bf16[2,512,4096]{1,2,0:T(8,128)(2,1)}, ...), condition=%wide.region_26.27_spmd.clone.clone, body=%wide.region_25.26_spmd.clone.clone.sunk | while | flops 1095009664 | bytes 69438728 | solution.py:546
  1355.0 11.9 copy.288
  1390.2 41.3 %while.68 = (s32[]{:T(128)}, f32[128,16,128]{0,2,1:T(8,128)}, s32[2]{0:T(128)}, bf16[1024,2048]{0,1:T(8,128)(2,1)}, s32[1]{0:T(128)}, /*index=5*/bf16[128,16,128...) while((s32[]{:T(128)}, f32[128,16,128]{0,2,1:T(8,128)}, ...), condition=%wide.region_24.25_spmd.clone.clone.clone, body=%wide.region_23.24_spmd.clone.clone.clone.sunk | while | flops 812418432 | bytes 26373336 | solution.py:517
  1434.2 21.7 %reduce-scatter.6.cloned.1.call-done = bf16[128,4096]{1,0:T(8,128)(2,1)} async-done(((bf16[1024,4096]{1,0:T(8,128)(2,1)}), bf16[128,4096]{1,0:T(8,128)(2,1)}) %reduce-scatter.6.cloned.1.call-update) | async-done | bytes 1048592 | tf_op jit(solution)/shard_map/reduce_scatter | solution.py:547
  1474.0 41.3 %all-reduce.3 = f32[128,8]{1,0:T(8,128)S(1)} all-reduce(f32[128,8]{1,0:T(8,128)S(1)} %fusion.260), channel_id=7, replica_groups=mesh['dp'=4,'expert'=8] {'dp','expert'}, use_global_device_ids=true, to_apply=%region_32.33.clone | all-reduce | flops 1024 | bytes 8192
  1515.9 23.7 %all-reduce.15.cloned.1.call-done = (bf16[1,2,2048,128]{2,3,1,0:T(8,128)(2,1)}, bf16[1,2,128,1408]{3,2,1,0:T(8,128)(2,1)}, bf16[1,1408,128]{1,2,0:T(8,128)(2,1)}, bf16[1,128,2048]{2,1,0:T(8,128)(2,1)}) async-done(((bf16[1,2,2048,128]{2,3,1,0:T(8,128)(2,1)}, bf16[1,2,128,1408]{3,2,1,0:T(8,128)(2,1)}, bf16[1,1408,128]{1,2,0:T(8,128)(2,1)}, bf16[1,128,2048]{2,1,0:T(8,128)(2,1)}), ...) | async-done | bytes 2654224 | tf_op jit(solution)/shard_map/psum | solution.py:600
  1548.2 11.9 fusion.197
  1561.5 334.0 %all-reduce.13.cloned.1.call-done = (f32[4,2048,128]{1,2,0:T(8,128)}, f32[4,128,2048]{2,1,0:T(8,128)}, f32[2048,128]{0,1:T(8,128)}, f32[2,2048,128]{1,2,0:T(8,12...) async-done(((f32[4,2048,128]{1,2,0:T(8,128)}, f32[4,128,2048]{2,1,0:T(8,128)}, f32[2048,128]{0,1:T(8,128)}, f32[2,2048,128]{1,2,0:T(8,128)}, ...) | async-done | bytes 21233680
  (520 shorter events, 473.5 us)
Async XLA Ops:
  7.2 1034.9 %copy-start = (bf16[2,128,5632]{2,1,0:T(8,128)(2,1)S(1)}, bf16[2,128,5632]{2,1,0:T(8,128)(2,1)}, u32[]{:S(2)}) copy-start(bf16[2,128,5632]{2,1,0:T(8,128)(2,1)} %param.55) | copy-start | bytes 8650756
  7.2 223.8 %all-gather.8.cloned.1.call-start = ((), (), s32[]{:S(2)}) async-start(), calls=%async_computation.6 | async-start | bytes 28311552 | tf_op jit(solution)/shard_map/all_gather | solution.py:177
  12.2 286.0 %all-gather.18.cloned.1.call-start = ((), (), s32[]{:S(2)}) async-start(), calls=%async_computation.12 | async-start | bytes 4718592 | tf_op jit(solution)/shard_map/all_gather | solution.py:202
  13.6 232.1 %copy-start.59 = (f32[128,128]{1,0:T(8,128)}, f32[128,128]{1,0:T(8,128)S(1)}, u32[]{:S(2)}) copy-start(f32[128,128]{1,0:T(8,128)S(1)} %copy.253) | copy-start | bytes 196612
  14.3 231.4 %copy-start.106 = (f32[128]{0:T(128)}, f32[128]{0:T(128)S(1)}, u32[]{:S(2)}) copy-start(f32[128]{0:T(128)S(1)} %get-tuple-element.1445) | copy-start | bytes 1540
  251.2 94.3 %all-gather.10.cloned.1.call-start = ((), (), s32[]{:S(2)}) async-start(), calls=%async_computation.7 | async-start | bytes 4718592 | tf_op jit(solution)/shard_map/all_gather | solution.py:201
  263.2 164.2 %all-gather.12.cloned.1.call-start = ((), (), s32[]{:S(2)}) async-start(), calls=%async_computation.8 | async-start | bytes 9437184 | tf_op jit(solution)/shard_map/all_gather | solution.py:178
  263.8 753.6 %all-gather.14.cloned.1.call-start = ((), (), s32[]{:S(2)}) async-start(), calls=%async_computation.9 | async-start | bytes 51904512 | tf_op jit(solution)/shard_map/all_gather | solution.py:179
  264.4 959.0 %all-gather.16.cloned.1.call-start = ((), (), s32[]{:S(2)}) async-start(), calls=%async_computation.10 | async-start | bytes 25952256 | tf_op jit(solution)/shard_map/all_gather | solution.py:180
  280.8 156.4 %all-to-all-start.1 = ((bf16[8,72,8]{1,2,0:T(8,128)(2,1)}), bf16[8,72,8]{1,2,0:T(8,128)(2,1)}, u32[]{:S(2)}, u32[]{:S(2)}) async-start(bf16[8,72,8]{1,2,0:T(8,128)(2,1)} %copy.268), calls=%async_computation.1 | async-start | bytes 32768 | tf_op jit(solution)/shard_map/all_to_all | solution.py:284
  437.2 129.3 %all-to-all-start = ((bf16[8,72,2048]{2,1,0:T(8,128)(2,1)}), bf16[8,72,2048]{2,1,0:T(8,128)(2,1)}, u32[]{:S(2)}, u32[]{:S(2)}) async-start(bf16[8,72,2048]{2,1,0:T(8,128)(2,1)} %bitcast.644), calls=%async_computation | async-start | bytes 4718592 | tf_op jit(solution)/shard_map/all_to_all | solution.py:277
  591.0 132.1 %all-to-all-start.2 = ((bf16[8,72,2048]{2,1,0:T(8,128)(2,1)}), bf16[8,72,2048]{2,1,0:T(8,128)(2,1)}, u32[]{:S(2)}, u32[]{:S(2)}) async-start(bf16[8,72,2048]{2,1,0:T(8,128)(2,1)} %bitcast.646), calls=%async_computation.2 | async-start | bytes 4718592 | tf_op jit(solution)/shard_map/all_to_all | solution.py:312
  615.9 114.3 %copy-start.97 = (f32[128,4]{0,1:T(4,128)}, f32[128,4]{0,1:T(4,128)S(1)}, u32[]{:S(2)}) copy-start(f32[128,4]{0,1:T(4,128)S(1)} %select_reduce_fusion.2) | copy-start | bytes 6148
  615.9 114.3 %copy-start.105 = (f32[128]{0:T(128)}, f32[128]{0:T(128)S(1)}, u32[]{:S(2)}) copy-start(f32[128]{0:T(128)S(1)} %reduce_max.22) | copy-start | bytes 1540
  742.4 116.7 %all-to-all-start.3 = ((bf16[8,72,2048]{2,1,0:T(8,128)(2,1)}), bf16[8,72,2048]{2,1,0:T(8,128)(2,1)}, u32[]{:S(2)}, u32[]{:S(2)}) async-start(bf16[8,72,2048]{2,1,0:T(8,128)(2,1)} %bitcast.643), calls=%async_computation.3 | async-start | bytes 4718592 | tf_op jit(solution)/shard_map/all_to_all | solution.py:361
  885.3 396.3 %all-to-all-start.4 = ((bf16[8,72,2048]{2,1,0:T(8,128)(2,1)}), bf16[8,72,2048]{2,1,0:T(8,128)(2,1)}, u32[]{:S(2)}, u32[]{:S(2)}) async-start(bf16[8,72,2048]{2,1,0:T(8,128)(2,1)} %bitcast.645), calls=%async_computation.4 | async-start | bytes 4718592 | tf_op jit(solution)/shard_map/all_to_all | solution.py:396
  894.3 561.6 %reduce-scatter.6.cloned.1.call-start = ((), (), s32[]{:S(2)}) async-start(), calls=%async_computation.11 | async-start | bytes 9437184 | tf_op jit(solution)/shard_map/reduce_scatter | solution.py:547
  1050.3 185.7 %copy-start.70 = (bf16[128,128]{1,0:T(8,128)(2,1)S(1)}, bf16[128,128]{1,0:T(8,128)(2,1)}, u32[]{:S(2)}) copy-start(bf16[128,128]{1,0:T(8,128)(2,1)} %fusion.184) | copy-start | bytes 98308
  1367.0 172.6 %all-reduce.15.cloned.1.call-start = ((), (), s32[]{:S(2)}) async-start(), calls=%async_computation.14 | async-start | bytes 5308416 | tf_op jit(solution)/shard_map/psum | solution.py:600
  1379.1 516.5 %all-reduce.13.cloned.1.call-start = ((), (), s32[]{:S(2)}) async-start(), calls=%async_computation.13 | async-start | bytes 42467328
  1390.2 42.7 %copy-start.25 = (bf16[128,16,128]{0,2,1:T(8,128)(2,1)S(1)}, bf16[128,16,128]{0,2,1:T(8,128)(2,1)}, u32[]{:S(2)}) copy-start(bf16[128,16,128]{0,2,1:T(8,128)(2,1)} %copy-done.24) | copy-start | bytes 1572868
  1432.9 27.0 %copy-start.67 = (f32[128,64]{0,1:T(8,128)S(1)}, f32[128,64]{0,1:T(8,128)}, u32[]{:S(2)}) copy-start(f32[128,64]{0,1:T(8,128)} %copy-done.66) | copy-start | bytes 98308
  1432.9 27.0 %copy-start.87 = (f32[128,64]{0,1:T(8,128)S(1)}, f32[128,64]{0,1:T(8,128)}, u32[]{:S(2)}) copy-start(f32[128,64]{0,1:T(8,128)} %get-tuple-element.1441) | copy-start | bytes 98308
  1548.2 358.3 %copy-start.1 = (bf16[2,128,5632]{2,1,0:T(8,128)(2,1)S(1)}, bf16[2,128,5632]{2,1,0:T(8,128)(2,1)}, u32[]{:S(2)}) copy-start(bf16[2,128,5632]{2,1,0:T(8,128)(2,1)} %param.55) | copy-start | bytes 8650756
  (118 other events, 597.3 us)
Sparse Core Ops, SparseCore 0:
  12.3 218.6 all-gather.7
  251.3 46.7 all-gather.17
  300.3 45.1 all-gather.9
  346.9 80.4 all-gather.11
  428.9 588.4 all-gather.13
  1018.9 204.3 all-gather.15
  1367.1 88.7 reduce-scatter.5
  1459.9 79.6 all-reduce.14
  1546.0 349.4 all-reduce.12
where the time goes:
time: 1930 us; the launch traced here: 1910 us
  waiting for transfers between devices  1260 us (65%)
  matrix products  284 us (15%)
  local copies, waits for them, and re-layouts  167 us (9%)
  other arithmetic  91 us (5%)
  starting transfers between devices  42.4 us (2%)
  blocking collectives  41.3 us (2%)
    unnamed x10, waiting for transfers between devices  336 us
    all_gather x1, waiting for transfers between devices, on_device(): lax.all_gather(attention_query_key_value, 'expert', axis=1, tiled=True)  214 us
    all_gather x1, waiting for transfers between devices, on_device(): lax.all_gather(shared_down_weight, 'expert', axis=0, tiled=True)  173 us
    all_gather x1, waiting for transfers between devices, on_device(): lax.all_gather(shared_gate_up_weight, 'expert', axis=2, tiled=True)  123 us
    all_to_all x1, waiting for transfers between devices, on_device(): lax.all_to_all(send_rows.reshape(experts, capacity, model_width_size), 'e...  116 us
    all_to_all x1, waiting for transfers between devices, on_device(): lax.all_to_all(expert_result.reshape(experts, capacity, model_width_size)...  107 us
    all_to_all x1, waiting for transfers between devices, on_device(): lax.all_to_all(send_grads.reshape(experts, capacity, model_width_size), '...  83.6 us
    unnamed x257, local copies, waits for them, and re-layouts  45.2 us
  transfers between devices with their start and end apart: 14, of which 12 were waited for; matrix products, arithmetic and copies ran while one was open for 22% of the time, Pallas kernels for 0%

commit v1 on v0

v1 whole, which is shorter than its diff:
```python
import math

import jax
import jax.numpy as jnp
from jax import lax
from jax.sharding import PartitionSpec as P

HEADS = 16
HEAD_DIM = 128
ADAPTER_RANK = 16
ADAPTER_COUNT = 8
BLOCK = 256
SEQ_MAX = 2048


NORM_EPS = 1e-06
ROPE_BASE = 1000000.0
MASKED = -1e30


def narrow_product(left_side, right_side):
    return jnp.dot(left_side, right_side, preferred_element_type=jnp.float32)


def rms_forward(values, gain_vector):
    factor = lax.rsqrt(jnp.mean(values * values, axis=-1, keepdims=True) + NORM_EPS)
    return (values * factor * gain_vector, factor)


def rms_backward(values, factor, gain_vector, upstream):
    weighted = upstream * gain_vector
    return factor * weighted - values * (factor * factor * factor) * jnp.mean(
        values * weighted, axis=-1, keepdims=True
    )


def rope_tables(positions, head_width):
    half_width = head_width // 2
    inverse = ROPE_BASE ** (-(jnp.arange(half_width).astype(jnp.float32) * 2.0 / head_width))
    angles = positions.astype(jnp.float32)[:, None] * inverse[None, :]
    return (jnp.cos(angles), jnp.sin(angles))


def rotate(values, cosine_table, sine_table, direction):
    half_width = values.shape[-1] // 2
    first_half = values[..., :half_width]
    second_half = values[..., half_width:]
    cosine_part = cosine_table[:, None, :]
    sine_part = sine_table[:, None, :] * direction
    return jnp.concatenate(
        [
            first_half * cosine_part - second_half * sine_part,
            second_half * cosine_part + first_half * sine_part,
        ],
        axis=-1,
    )


def rows_product(left_side, right_side):
    return lax.dot_general(
        left_side, right_side, (((1,), (1,)), ((), ())), preferred_element_type=jnp.float32
    )


def token_product(left_side, right_side):
    return lax.dot_general(
        left_side, right_side, (((0,), (0,)), ((), ())), preferred_element_type=jnp.float32
    )


def gated_back(gate_value, up_value, grad_hidden):
    sigmoid_gate = jax.nn.sigmoid(gate_value)
    grad_gate = grad_hidden * up_value * sigmoid_gate * (1.0 + gate_value * (1.0 - sigmoid_gate))
    grad_up = grad_hidden * gate_value * sigmoid_gate
    return (grad_gate.astype(jnp.bfloat16), grad_up.astype(jnp.bfloat16))


def head_weights(columns, owner_index, owners, slot_count, head_start, width):
    model_width_size, held = columns.shape
    if slot_count == 1 and held == 3 * width and owners % 3:
        moved = [
            lax.ppermute(
                columns[:, step * width : (step + 1) * width],
                "expert",
                [(source, (3 * source + step) % owners) for source in range(owners)],
            )
            for step in range(3)
        ]
        stacked = jnp.stack(moved)
        return jnp.stack(
            [
                lax.dynamic_index_in_dim(stacked, (owner_index + owners * kind) % 3, 0, False)
                for kind in range(3)
            ]
        )
    full = lax.all_gather(columns, "expert", axis=1, tiled=True)
    return jnp.stack(
        [
            lax.dynamic_slice_in_dim(full, kind * model_width_size + head_start * HEAD_DIM, width, 1)
            for kind in range(3)
        ]
    )


def spread_adapters(compact, adapter_index):
    ranks = ADAPTER_COUNT * ADAPTER_RANK
    total = jnp.zeros((ranks, compact.shape[1]), compact.dtype)
    for slot in range(adapter_index.shape[0]):
        piece = compact[slot * ADAPTER_RANK : (slot + 1) * ADAPTER_RANK]
        total = total + lax.dynamic_update_slice_in_dim(
            jnp.zeros_like(total), piece, adapter_index[slot] * ADAPTER_RANK, 0
        )
    return total


def reduce_adapters(
    partial, owned, owned_starts, owned_totals, adapter_index, adapter_groups, owner_index, owners
):
    groups = lax.axis_size("dp")
    group_index = lax.axis_index("dp")
    slot_count = adapter_index.shape[0]
    partial_sizes = [value.shape[1] for value in partial]
    owned_sizes = [value.shape[1] for value in owned]
    partial_all = jnp.concatenate(partial, axis=1)
    owned_all = jnp.concatenate(owned, axis=1)

    def cut(values, sizes):
        pieces, at = [], 0
        for size in sizes:
            pieces.append(values[..., at : at + size])
            at += size
        return pieces

    if slot_count > 1 or ADAPTER_RANK % owners or ADAPTER_COUNT % groups or owners % (
        ADAPTER_COUNT // groups
    ):
        wide = [
            lax.dynamic_update_slice_in_dim(
                jnp.zeros((value.shape[0], total), value.dtype), value, start, 1
            )
            for value, start, total in zip(owned, owned_starts, owned_totals)
        ]
        dense = spread_adapters(jnp.concatenate([partial_all] + wide, axis=1), adapter_index)
        summed = lax.psum_scatter(dense, ("dp", "expert"), scatter_dimension=0, tiled=True)
        pieces = cut(summed, partial_sizes + owned_totals)
        return pieces[: len(partial)], pieces[len(partial) :]

    local = ADAPTER_COUNT // groups
    own_rows = ADAPTER_RANK // owners
    held = sum(partial_sizes)
    padded = -(-held // (8 * 128)) * 8 * 128
    tall = jnp.pad(partial_all, ((0, 0), (0, padded - held)))
    tall = tall.reshape(8 * ADAPTER_RANK, padded // 8)
    scattered = lax.psum_scatter(tall, "expert", scatter_dimension=0, tiled=True)
    scattered = scattered.reshape(own_rows, padded)
    moved = lax.all_to_all(owned_all, "expert", split_axis=0, concat_axis=1, tiled=True)
    joined = jnp.concatenate([scattered, moved], axis=1)
    gathered = lax.all_gather(joined, "dp", axis=0)
    sums = []
    for which in range(local):
        mine = (adapter_groups == group_index * local + which).astype(jnp.float32)
        sums.append(jnp.sum(jnp.where(mine[:, None, None] > 0, gathered, 0.0), axis=0))
    sums = jnp.stack(sums)
    arrived = []
    for step in range(local):
        piece = lax.dynamic_index_in_dim(sums, (step + owner_index) % local, 0, False)
        arrived.append(
            lax.ppermute(
                piece,
                "expert",
                [
                    (source, (step + source) % local * (owners // local) + source // local)
                    for source in range(owners)
                ],
            )
        )
    arrived = jnp.stack(arrived)
    place = owner_index // (owners // local)
    rows = jnp.concatenate(
        [
            lax.dynamic_index_in_dim(arrived, (place - which) % local, 0, False)
            for which in range(local)
        ],
        axis=0,
    )
    pieces = cut(rows[:, :held], partial_sizes)
    wide = rows[:, padded:].reshape(local * own_rows, owners, sum(owned_sizes))
    owned_pieces = [
        value.reshape(local * own_rows, owners * size)
        for value, size in zip(cut(wide, owned_sizes), owned_sizes)
    ]
    return pieces, owned_pieces


def on_device(
    tokens,
    cotangent,
    attention_norm_gain,
    experts_norm_gain,
    attention_query_key_value,
    attention_output_weight,
    router_projection,
    shared_gate_up_weight,
    shared_down_weight,
    shared_gate_vector,
    expert_gate_up_weight,
    expert_down_weight,
    routes,
    lengths,
    adapter_slot_index,
    attention_adapter_first,
    attention_adapter_second,
    router_adapter_first,
    router_adapter_second,
    shared_adapter_first,
    shared_adapter_second,
    shared_down_adapter_first,
    shared_down_adapter_second,
    expert_adapter_first,
    expert_adapter_second,
    expert_down_adapter_first,
    expert_down_adapter_second,
):
    count_rows, model_width_size = tokens.shape
    owners = lax.axis_size("expert")
    owner_index = lax.axis_index("expert")
    experts = router_projection.shape[1]
    top_count = routes.shape[1]
    capacity = (count_rows * top_count * 9 + 8 * experts - 1) // (8 * experts)
    group_rows = count_rows * owners
    seq_length = min(SEQ_MAX, group_rows)
    slot_count = lengths.shape[0]
    group_devices = owners // slot_count
    head_count = HEADS // group_devices
    width = head_count * HEAD_DIM
    own_slot = owner_index // group_devices
    head_start = owner_index % group_devices * head_count
    head_column = head_start * HEAD_DIM
    score_scale = 1.0 / math.sqrt(HEAD_DIM)
    half = jnp.bfloat16

    def own_rows(values):
        return lax.dynamic_slice_in_dim(values, owner_index * count_rows, count_rows, 0)

    def slot_rows(values):
        if slot_count == 1:
            return values
        return lax.dynamic_slice_in_dim(values, own_slot * seq_length, seq_length, 0)

    def group_wide(values):
        if slot_count == 1:
            return values
        return lax.dynamic_update_slice_in_dim(
            jnp.zeros((group_rows, values.shape[1]), values.dtype), values, own_slot * seq_length, 0
        )

    def slot_wide(values):
        if slot_count == 1:
            return values
        return lax.dynamic_update_slice_in_dim(
            jnp.zeros((slot_count * ADAPTER_RANK, values.shape[1]), values.dtype),
            values,
            own_slot * ADAPTER_RANK,
            0,
        )

    def slot_value(values):
        return values[0] if slot_count == 1 else lax.dynamic_index_in_dim(values, own_slot, 0, False)

    def picked_maps(maps, axis):
        return jnp.concatenate(
            [
                lax.dynamic_slice_in_dim(
                    maps, adapter_slot_index[slot] * ADAPTER_RANK, ADAPTER_RANK, axis
                )
                for slot in range(slot_count)
            ],
            axis=axis,
        )

    def scatter_rows(values):
        return lax.psum_scatter(values.astype(half), "expert", scatter_dimension=0, tiled=True)

    tokens_all = lax.all_gather(tokens, "expert", axis=0, tiled=True)
    qkv_weights = head_weights(
        attention_query_key_value, owner_index, owners, slot_count, head_start, width
    )
    routes_all = lax.all_gather(routes, "expert", axis=0, tiled=True)
    adapter_groups = lax.all_gather(adapter_slot_index, "dp", axis=0, tiled=True)
    upstream_all = lax.all_gather(cotangent, "expert", axis=0, tiled=True)
    if attention_output_weight.shape[0] == width:
        output_weight = attention_output_weight
    else:
        output_weight = lax.dynamic_slice_in_dim(
            lax.all_gather(attention_output_weight, "expert", axis=0, tiled=True),
            head_column,
            width,
            0,
        )

    if slot_count == 1:
        selector = None
    else:
        row_slot = jnp.arange(group_rows, dtype=jnp.int32) // seq_length
        rank_slot = jnp.arange(slot_count * ADAPTER_RANK, dtype=jnp.int32) // ADAPTER_RANK
        selector = (row_slot[:, None] == rank_slot[None, :]).astype(half)

    def chosen(values, picker):
        narrow = values.astype(half)
        return narrow if picker is None else narrow * picker

    attention_adapter = slot_value(adapter_slot_index) * ADAPTER_RANK
    attention_first = lax.dynamic_slice_in_dim(
        attention_adapter_first, attention_adapter, ADAPTER_RANK, 2
    )
    attention_second = lax.dynamic_slice_in_dim(
        attention_adapter_second, attention_adapter, ADAPTER_RANK, 1
    )
    qkv_second = lax.dynamic_slice_in_dim(attention_second[:3], head_column, width, 2)
    output_first = lax.dynamic_slice_in_dim(attention_first[3], head_column, width, 0)
    output_second = attention_second[3]
    router_first = picked_maps(router_adapter_first, 1)
    router_second = picked_maps(router_adapter_second, 0)
    shared_wide = shared_down_weight.shape[0]
    shared_first = picked_maps(shared_adapter_first, 2)
    shared_second = lax.dynamic_slice_in_dim(
        picked_maps(shared_adapter_second, 1), owner_index * shared_wide, shared_wide, 2
    )
    down_first = lax.dynamic_slice_in_dim(
        picked_maps(shared_down_adapter_first, 1), owner_index * shared_wide, shared_wide, 0
    )
    down_second = picked_maps(shared_down_adapter_second, 0)
    expert_first = picked_maps(expert_adapter_first[0], 2)
    expert_second = picked_maps(expert_adapter_second[0], 1)
    expert_down_first = picked_maps(expert_down_adapter_first[0], 1)
    expert_down_second = picked_maps(expert_down_adapter_second[0], 0)

    expert_range = jnp.arange(experts, dtype=jnp.int32)
    route_hits = jnp.any(routes_all[:, :, None] == expert_range[None, None, :], axis=1)
    own_hits = jnp.any(routes_all == owner_index, axis=1)
    ranks = jnp.cumsum(own_hits.astype(jnp.int32)) - 1
    row_range = jnp.arange(experts * capacity, dtype=jnp.int32)
    placed = (ranks[None, :] == row_range[:, None]) & own_hits[None, :]
    spread = placed.astype(half)
    row_selector = None if selector is None else narrow_product(spread, selector).astype(half)

    slot_tokens = slot_rows(tokens_all).astype(jnp.float32)
    normed_first, unused = rms_forward(slot_tokens, attention_norm_gain)
    first_narrow = normed_first.astype(half)
    positions = jnp.arange(seq_length, dtype=jnp.int32)
    cosine_table, sine_table = rope_tables(positions, HEAD_DIM)
    shaped = (seq_length, head_count, HEAD_DIM)
    attention_middle = [
        narrow_product(first_narrow, attention_first[kind]).astype(half) for kind in range(3)
    ]
    projected = [
        narrow_product(first_narrow, qkv_weights[kind])
        + narrow_product(attention_middle[kind], qkv_second[kind])
        for kind in range(3)
    ]
    query_low = rotate(projected[0].reshape(shaped), cosine_table, sine_table, 1.0).astype(half)
    key_low = rotate(projected[1].reshape(shaped), cosine_table, sine_table, 1.0).astype(half)
    value_low = projected[2].reshape(shaped).astype(half)
    allowed = ((positions // BLOCK)[None, :] <= (positions // BLOCK)[:, None]) & (
        positions < slot_value(lengths)
    )[None, :]
    scores = (
        jnp.einsum("qhd,khd->hqk", query_low, key_low, preferred_element_type=jnp.float32)
        * score_scale
    )
    scores = jnp.where(allowed[None], scores, MASKED)
    exponents = jnp.exp(scores - jnp.max(scores, axis=2, keepdims=True)) * allowed[None]
    probabilities = exponents / jnp.sum(exponents, axis=2, keepdims=True)
    probabilities_low = probabilities.astype(half)
    attended = jnp.einsum(
        "hqk,khd->qhd", probabilities_low, value_low, preferred_element_type=jnp.float32
    )
    attended_low = attended.reshape(seq_length, width).astype(half)
    output_middle = narrow_product(attended_low, output_first).astype(half)
    attention_part = narrow_product(attended_low, output_weight) + narrow_product(
        output_middle, output_second
    )
    input_rows = tokens.astype(jnp.float32)
    residual_stream = input_rows + scatter_rows(group_wide(attention_part)).astype(jnp.float32)
    normed_second, factor_second = rms_forward(residual_stream, experts_norm_gain)
    second_own = normed_second.astype(half)
    second_all = lax.all_gather(second_own, "expert", axis=0, tiled=True)

    router_middle = chosen(narrow_product(second_all, router_first), selector)
    router_scores = narrow_product(second_all, router_projection) + narrow_product(
        router_middle, router_second
    )
    reach = jnp.max(jnp.where(route_hits, router_scores, MASKED), axis=1, keepdims=True)
    gate_exponents = jnp.where(route_hits, jnp.exp(jnp.minimum(router_scores - reach, 0.0)), 0.0)
    gate_weights = gate_exponents / jnp.sum(gate_exponents, axis=1, keepdims=True)
    own_gate = jnp.sum(jnp.where(expert_range[None, :] == owner_index, gate_weights, 0.0), axis=1)
    row_gate = jnp.sum(jnp.where(placed, own_gate[None, :], 0.0), axis=1, keepdims=True)
    shared_weight = jax.nn.sigmoid(
        narrow_product(second_all, shared_gate_vector[:, None])
    )

    expert_rows = narrow_product(spread, second_all).astype(half)
    expert_middle = [
        chosen(narrow_product(expert_rows, expert_first[kind]), row_selector) for kind in range(2)
    ]
    expert_pre = [
        narrow_product(expert_rows, expert_gate_up_weight[0, kind])
        + narrow_product(expert_middle[kind], expert_second[kind])
        for kind in range(2)
    ]
    expert_hidden = (jax.nn.silu(expert_pre[0]) * expert_pre[1]).astype(half)
    expert_down_middle = chosen(narrow_product(expert_hidden, expert_down_first), row_selector)
    expert_result = (
        narrow_product(expert_hidden, expert_down_weight[0])
        + narrow_product(expert_down_middle, expert_down_second)
    ).astype(half)

    shared_middle = [
        chosen(narrow_product(second_all, shared_first[kind]), selector) for kind in range(2)
    ]
    shared_pre = [
        narrow_product(second_all, shared_gate_up_weight[kind])
        + narrow_product(shared_middle[kind], shared_second[kind])
        for kind in range(2)
    ]
    shared_hidden = (jax.nn.silu(shared_pre[0]) * shared_pre[1]).astype(half)
    down_middle = chosen(narrow_product(shared_hidden, down_first), selector)
    shared_part = narrow_product(shared_hidden, shared_down_weight) + narrow_product(
        down_middle, down_second
    )
    upstream_wide = upstream_all.astype(jnp.float32)
    shared_dot = jnp.sum(upstream_wide * shared_part, axis=1)

    upstream_rows = narrow_product(spread, upstream_all)
    row_dot = jnp.sum(upstream_rows * expert_result.astype(jnp.float32), axis=1, keepdims=True)
    gate_dot = jnp.sum(jnp.where(placed, row_dot, 0.0), axis=0)
    expert_upstream = (row_gate * upstream_rows).astype(half)
    expert_down_inner = chosen(rows_product(expert_upstream, expert_down_second), row_selector)
    expert_grad_hidden = rows_product(expert_upstream, expert_down_weight[0]) + rows_product(
        expert_down_inner, expert_down_first
    )
    expert_grad_pre = gated_back(expert_pre[0], expert_pre[1], expert_grad_hidden)
    expert_inner = [
        chosen(rows_product(expert_grad_pre[kind], expert_second[kind]), row_selector)
        for kind in range(2)
    ]
    copy_grad = sum(
        rows_product(expert_grad_pre[kind], expert_gate_up_weight[0, kind])
        + rows_product(expert_inner[kind], expert_first[kind])
        for kind in range(2)
    ).astype(half)

    value_grads = (shared_weight * upstream_wide).astype(half)
    down_inner = chosen(rows_product(value_grads, down_second), selector)
    shared_grad_hidden = rows_product(value_grads, shared_down_weight) + rows_product(
        down_inner, down_first
    )
    shared_grad_pre = gated_back(shared_pre[0], shared_pre[1], shared_grad_hidden)
    shared_inner = [
        chosen(rows_product(shared_grad_pre[kind], shared_second[kind]), selector)
        for kind in range(2)
    ]
    second_part = token_product(spread, copy_grad) + sum(
        rows_product(shared_grad_pre[kind], shared_gate_up_weight[kind])
        + rows_product(shared_inner[kind], shared_first[kind])
        for kind in range(2)
    )
    dots = jnp.concatenate(
        [
            jnp.where(expert_range[:, None] == owner_index, gate_dot[None, :], 0.0),
            shared_dot[None, :],
            jnp.zeros((7, group_rows), jnp.float32),
        ],
        axis=0,
    )
    own_dots = jnp.transpose(lax.psum_scatter(dots, "expert", scatter_dimension=1, tiled=True))
    second_sum = scatter_rows(second_part).astype(jnp.float32)
    layer_part = (
        token_product(spread, (row_gate * expert_result.astype(jnp.float32)).astype(half))
        + shared_weight * shared_part
    )

    own_weights = own_rows(gate_weights)
    gate_grads = own_dots[:, :experts]
    centered = own_weights * (
        gate_grads - jnp.sum(own_weights * gate_grads, axis=1, keepdims=True)
    )
    logit_grads = centered.astype(half)
    own_selector = None if selector is None else own_rows(selector)
    router_inner = chosen(rows_product(logit_grads, router_second), own_selector)
    own_shared_weight = own_rows(shared_weight)
    weight_grads = own_dots[:, experts : experts + 1] * own_shared_weight * (1.0 - own_shared_weight)
    second_grad = (
        second_sum
        + rows_product(logit_grads, router_projection)
        + rows_product(router_inner, router_first)
        + weight_grads * shared_gate_vector.astype(jnp.float32)[None, :]
    )
    residual_grad = cotangent.astype(jnp.float32) + rms_backward(
        residual_stream, factor_second, experts_norm_gain, second_grad
    )
    output_upstream = slot_rows(
        lax.all_gather(residual_grad.astype(half), "expert", axis=0, tiled=True)
    )

    output_inner = rows_product(output_upstream, output_second).astype(half)
    attended_grad = (
        (rows_product(output_upstream, output_weight) + rows_product(output_inner, output_first))
        .astype(half)
        .reshape(shaped)
    )
    row_delta = jnp.transpose(jnp.sum(attended_grad.astype(jnp.float32) * attended, axis=2))
    prob_grads = jnp.einsum(
        "qhd,khd->hqk", attended_grad, value_low, preferred_element_type=jnp.float32
    )
    score_grad = (probabilities * (prob_grads - row_delta[:, :, None])).astype(half)
    query_grad = (
        jnp.einsum("hqk,khd->qhd", score_grad, key_low, preferred_element_type=jnp.float32)
        * score_scale
    )
    key_grad = (
        jnp.einsum("hqk,qhd->khd", score_grad, query_low, preferred_element_type=jnp.float32)
        * score_scale
    )
    value_grad = jnp.einsum(
        "hqk,qhd->khd", probabilities_low, attended_grad, preferred_element_type=jnp.float32
    )
    pre_grads = [
        rotate(query_grad, cosine_table, sine_table, -1.0).astype(half).reshape(seq_length, width),
        rotate(key_grad, cosine_table, sine_table, -1.0).astype(half).reshape(seq_length, width),
        value_grad.astype(half).reshape(seq_length, width),
    ]
    qkv_inner = [rows_product(pre_grads[kind], qkv_second[kind]).astype(half) for kind in range(3)]
    first_part = sum(
        rows_product(pre_grads[kind], qkv_weights[kind])
        + rows_product(qkv_inner[kind], attention_first[kind])
        for kind in range(3)
    )
    first_grad = scatter_rows(group_wide(first_part)).astype(jnp.float32)
    unused, factor_first = rms_forward(input_rows, attention_norm_gain)
    tokens_grad = residual_grad + rms_backward(
        input_rows, factor_first, attention_norm_gain, first_grad
    )
    layer_out = (residual_stream + scatter_rows(layer_part).astype(jnp.float32)).astype(half)

    own_router_middle = own_rows(router_middle)
    early, early_own = reduce_adapters(
        [
            slot_wide(token_product(output_middle, output_upstream)),
            token_product(shared_inner[0], second_all),
            token_product(shared_inner[1], second_all),
            token_product(down_middle, value_grads),
            token_product(router_inner, second_own),
            token_product(own_router_middle, logit_grads),
        ],
        [
            slot_wide(token_product(output_inner, attended_low)),
            token_product(shared_middle[0], shared_grad_pre[0]),
            token_product(shared_middle[1], shared_grad_pre[1]),
            token_product(down_inner, shared_hidden),
        ],
        [head_column] + [owner_index * shared_wide] * 3,
        [model_width_size] + [owners * shared_wide] * 3,
        adapter_slot_index,
        adapter_groups,
        owner_index,
        owners,
    )
    late, late_own = reduce_adapters(
        [slot_wide(token_product(qkv_inner[kind], first_narrow)) for kind in range(3)],
        [slot_wide(token_product(attention_middle[kind], pre_grads[kind])) for kind in range(3)],
        [head_column] * 3,
        [model_width_size] * 3,
        adapter_slot_index,
        adapter_groups,
        owner_index,
        owners,
    )
    attn_grad_a = jnp.stack([jnp.transpose(value) for value in late + [early_own[0]]])
    attn_grad_b = jnp.stack(late_own + [early[0]])

    wide_grads = jnp.concatenate(
        [
            token_product(expert_inner[0], expert_rows),
            token_product(expert_inner[1], expert_rows),
            token_product(expert_middle[0], expert_grad_pre[0]),
            token_product(expert_middle[1], expert_grad_pre[1]),
            token_product(expert_down_inner, expert_hidden),
            token_product(expert_down_middle, expert_upstream),
        ],
        axis=1,
    ).astype(half)
    expert_grads = lax.all_gather(wide_grads, "dp", axis=0, tiled=True)
    rank_range = jnp.arange(ADAPTER_COUNT * ADAPTER_RANK, dtype=jnp.int32)
    source_rank = jnp.arange(expert_grads.shape[0], dtype=jnp.int32)
    source_place = jnp.repeat(adapter_groups, ADAPTER_RANK) * ADAPTER_RANK + (
        source_rank % ADAPTER_RANK
    )
    placement = (source_place[:, None] == rank_range[None, :]).astype(half)
    feed = expert_down_weight.shape[1]
    bounds = [0, model_width_size, 2 * model_width_size]
    bounds += [bounds[-1] + feed, bounds[-1] + 2 * feed, bounds[-1] + 3 * feed]
    expert_pieces = [
        expert_grads[:, start:stop] for start, stop in zip(bounds, bounds[1:] + [None])
    ]
    in_grad_a = jnp.stack([token_product(value, placement) for value in expert_pieces[:2]])
    in_grad_b = jnp.stack([token_product(placement, value) for value in expert_pieces[2:4]])
    down_grad_a = token_product(expert_pieces[4], placement)
    down_grad_b = token_product(placement, expert_pieces[5])
    return (
        layer_out,
        tokens_grad,
        attn_grad_a,
        attn_grad_b,
        jnp.transpose(early[4]),
        early[5],
        jnp.stack([jnp.transpose(early[1]), jnp.transpose(early[2])]),
        jnp.stack(early_own[1:3]),
        jnp.transpose(early_own[3]),
        early[3],
        in_grad_a[None],
        in_grad_b[None],
        down_grad_a[None],
        down_grad_b[None],
    )


def solution(mesh):
    return jax.shard_map(
        on_device,
        mesh=mesh,
        in_specs=(
            P(("dp", "expert"), None),
            P(("dp", "expert"), None),
            P(),
            P(),
            P(None, "expert"),
            P("expert", None),
            P(),
            P(None, None, "expert"),
            P("expert", None),
            P(),
            P("expert", None, None, None),
            P("expert", None, None),
            P(("dp", "expert"), None),
            P("dp"),
            P("dp"),
            P(),
            P(),
            P(),
            P(),
            P(),
            P(),
            P(),
            P(),
            P("expert", None, None, None),
            P("expert", None, None, None),
            P("expert", None, None),
            P("expert", None, None),
        ),
        out_specs=(
            P(("dp", "expert"), None),
            P(("dp", "expert"), None),
            P(None, None, ("dp", "expert")),
            P(None, ("dp", "expert"), None),
            P(None, ("dp", "expert")),
            P(("dp", "expert"), None),
            P(None, None, ("dp", "expert")),
            P(None, ("dp", "expert"), None),
            P(None, ("dp", "expert")),
            P(("dp", "expert"), None),
            P("expert", None, None, None),
            P("expert", None, None, None),
            P("expert", None, None),
            P("expert", None, None),
        ),
        check_vma=False,
    )
```

time: 1930 us -> 783 us (0.41)
  waiting for transfers between devices: 1260 us -> 311 us
  local copies, waits for them, and re-layouts: 167 us -> 36.7 us
  other arithmetic: 91 us -> 50.3 us
    all_gather x6 -> x5, waiting for transfers between devices: 568 us -> 88.8 us  [the longest x1 40.7 us: on_device(): lax.all_gather(residual_grad.astype(half), 'expert', axis=0, tiled=True)]
    unnamed x10 -> x12, waiting for transfers between devices: 336 us -> 1.37 us
    all_to_all x5 -> x2, waiting for transfers between devices: 306 us -> 2.22 us  [reduce_adapters(): lax.all_to_all(owned_all, 'expert', split_axis=0, concat_axis=1, tiled=True)]
    reduce_scatter x1 -> x7, waiting for transfers between devices: 21.7 us -> 137 us  [the longest x4 137 us: scatter_rows(): lax.psum_scatter(values.astype(half), 'expert', scatter_dimension=0, tile...]
    ppermute x0 -> x7, waiting for transfers between devices: none -> 81.5 us  [the longest x3 64.4 us: head_weights(): lax.ppermute(columns[:, step * width:(step + 1) * width], 'expert', [(sou...]
    dot_general x71 -> x67, matrix products: 262 us -> 183 us  [the longest x32 125 us: rows_product(): lax.dot_general(left_side, right_side, (((1,), (1,)), ((), ())), preferre...]
    dot_general x4 -> x36, matrix products: 22.4 us -> 83 us  [narrow_product(): return jnp.dot(left_side, right_side, preferred_element_type=jnp.float32)]
    dynamic_slice x16 -> x0, local copies, waits for them, and re-layouts: 52.4 us -> none  [the longest x6 31.6 us: block_rows(): lax.dynamic_slice_in_dim(source_table, start_row, key_step, 0)]
  transfers between devices with their start and end apart: 14 -> 21, of which waited for: 12 -> 13; matrix products, arithmetic and copies ran while one was open for 22% -> 26% of each run, Pallas kernels for 0% -> 0%
where the time goes in v1:
time: 783 us; the launch traced here: 768 us
  waiting for transfers between devices  311 us (40%)
  matrix products  278 us (36%)
  other arithmetic  50.3 us (6%)
  starting transfers between devices  38.4 us (5%)
  local copies, waits for them, and re-layouts  36.7 us (5%)
  blocking collectives  35.9 us (5%)
  between operations  17.8 us (2%)
    reduce_scatter x4, waiting for transfers between devices, scatter_rows(): lax.psum_scatter(values.astype(half), 'expert', scatter_dimension=0, tile...  137 us
    dot_general x32, matrix products, rows_product(): lax.dot_general(left_side, right_side, (((1,), (1,)), ((), ())), preferre...  125 us
    dot_general x36, matrix products, narrow_product(): return jnp.dot(left_side, right_side, preferred_element_type=jnp.float32)  83 us
    ppermute x3, waiting for transfers between devices, head_weights(): lax.ppermute(columns[:, step * width:(step + 1) * width], 'expert', [(sou...  64.4 us
    dot_general x30, matrix products, token_product(): lax.dot_general(left_side, right_side, (((0,), (0,)), ((), ())), preferre...  46.8 us
    all_gather x1, waiting for transfers between devices, on_device(): lax.all_gather(residual_grad.astype(half), 'expert', axis=0, tiled=True)  40.7 us
    all_gather x1, waiting for transfers between devices, on_device(): second_all = lax.all_gather(second_own, 'expert', axis=0, tiled=True)  32.3 us
    unnamed x267, local copies, waits for them, and re-layouts  21.6 us
  transfers between devices with their start and end apart: 21, of which 13 were waited for; matrix products, arithmetic and copies ran while one was open for 26% of the time, Pallas kernels for 0%

profile of v1, /device:TPU:11, one launch (start us, length us, event | category | flops | bytes accessed | tf_op | source)
XLA Modules:
  0.0 767.7 jit_solution(2849973054389609829)
XLA Ops:
  13.7 9.5 %collective-permute-start.2 = (bf16[2048,256]{1,0:T(8,128)(2,1)}, bf16[2048,256]{1,0:T(8,128)(2,1)}, u32[]{:S(2)}, u32[]{:S(2)}) collective-permute-start(bf16[2048,256]{1,0:T(8,128)(2,1)} %get-tuple-element.34), channel_id=1, source_target_pairs={{0,2},{1,5},{2,0},{3,3},{4,6},{5,1},{6,4},{7,7},{8,10},{9,13},{10,... | collective-permute-start | bytes 3145736 | tf_op jit(solution)/shard_map/ppermute | solution.py:82
  31.6 42.8 %collective-permute-done = bf16[2048,256]{1,0:T(8,128)(2,1)} collective-permute-done((bf16[2048,256]{1,0:T(8,128)(2,1)}, bf16[2048,256]{1,0:T(8,128)(2,1)}, u32[]{:S(2)}, u32[]{:S(2)}) %collective-permute-start) | collective-permute-done | bytes 1048608 | tf_op jit(solution)/shard_map/ppermute | solution.py:82
  74.4 21.6 %collective-permute-done.1 = bf16[2048,256]{1,0:T(8,128)(2,1)} collective-permute-done((bf16[2048,256]{1,0:T(8,128)(2,1)}, bf16[2048,256]{1,0:T(8,128)(2,1)}, u32[]{:S(2)}, u32[]{:S(2)}) %collective-permute-start.1) | collective-permute-done | bytes 1048608 | tf_op jit(solution)/shard_map/ppermute | solution.py:82
  134.1 11.2 %fusion.216 = (f32[2,1024]{1,0:T(2,128)S(1)}, f32[2,1024,1024]{1,2,0:T(8,128)}) fusion(f32[1024,1024]{0,1:T(8,128)} %get-tuple-element.73, pred[1024,1024]{0,1:T(8,128)(4,1)} %get-tuple-element.72, bf16[1024,2,64]{2,0,1:T(8,128)(2,1)} %get-tuple-element.44, bf16[1024,2,64]{2,0,1:T(8,128)(2,1)} %get-tuple-element.45, ...), kind=kOutput, calls=%fused_computation.420 | convolution fusion | flops 549454848 | bytes 14688256 | tf_op jit(solution)/shard_map/sub | solution.py:372
  158.6 50.3 %reduce-scatter.8.cloned.1.call-done = bf16[128,2048]{1,0:T(8,128)(2,1)} async-done(((bf16[1024,2048]{1,0:T(8,128)(2,1)}), bf16[128,2048]{1,0:T(8,128)(2,1)}) %reduce-scatter.8.cloned.1.call-update) | async-done | bytes 524304 | tf_op jit(solution)/shard_map/reduce_scatter | solution.py:282
  214.1 12.2 %all_gather.34 = s32[1024,4]{0,1:T(4,128)S(1)} all-gather(s32[128,4]{0,1:T(4,128)S(1)} %copy-done.110), channel_id=1, replica_groups=mesh['dp'=4,'expert'=8] {'expert'}, dimensions={0}, use_global_device_ids=true | all-gather | bytes 18432 | tf_op jit(solution)/shard_map/all_gather | solution.py:288
  227.0 32.3 %all-gather.12.cloned.1.call-done = bf16[1024,2048]{1,0:T(8,128)(2,1)} async-done(((bf16[128,2048]{1,0:T(8,128)(2,1)}), bf16[1024,2048]{1,0:T(8,128)(2,1)}) %all-gather.12.cloned.1.call-update) | async-done | bytes 4194320 | tf_op jit(solution)/shard_map/all_gather | solution.py:387
  290.7 15.8 %all-gather.14.cloned.1.call-done = bf16[1024,2048]{1,0:T(8,128)(2,1)} async-done(((bf16[128,2048]{1,0:T(8,128)(2,1)}), bf16[1024,2048]{1,0:T(8,128)(2,1)}) %all-gather.14.cloned.1.call-update) | async-done | bytes 4194320 | tf_op jit(solution)/shard_map/all_gather | solution.py:290
  306.5 5.9 fusion.24
  315.4 6.4 fusion.7
  332.2 5.9 fusion.15
  371.7 5.9 fusion.33
  392.1 13.0 %fusion.46 = f32[1024,2048]{1,0:T(8,128)} fusion(s32[1024]{0:T(1024)S(1)} %add_bitcast_fusion, pred[1024]{0:T(1024)(128)(4,1)S(1)} %compare_reduce_fusion, f32[576,2048]{1,0:T(8,128)} %fusion.11, f32[576,2048]{1,0:T(8,128)} %fusion.15, f32[576,2048]{1,0:T(8,128)} %fusion.92, bf16[576,16]{0,1:T(8,128)(2,1)S(1)} %convolution_convert_fusion.23, ...), kind=kOutput, calls=%fused_computation.88 | convolution fusion | flops 2459566080 | bytes 23094280 | tf_op jit(solution)/shard_map/dot_general | solution.py:66
  405.1 14.0 %add_convert_fusion.1 = bf16[1024,2048]{1,0:T(8,128)(2,1)} fusion(f32[1024,2048]{1,0:T(8,128)} %fusion.46, f32[1024,2048]{1,0:T(8,128)} %fusion.29, f32[1024,2048]{1,0:T(8,128)} %fusion.33, f32[1024,2048]{1,0:T(8,128)} %fusion.93, bf16[1024,16]{0,1:T(8,128)(2,1)S(1)} %convolution_convert_fusion.8, bf16[2,2048,128]{2,1,0:T(8,128)(2,1)S(1)} %copy-done.38, ...), kind=kOutput, calls=%fused_computation.12 | convolution fusion | flops 77594624 | bytes 38305800 | tf_op jit(solution)/shard_map/dot_general | solution.py:60
  423.9 43.7 %reduce-scatter.12.cloned.1.call-done = bf16[128,2048]{1,0:T(8,128)(2,1)} async-done(((bf16[1024,2048]{1,0:T(8,128)(2,1)}), bf16[128,2048]{1,0:T(8,128)(2,1)}) %reduce-scatter.12.cloned.1.call-update) | async-done | bytes 524304 | tf_op jit(solution)/shard_map/reduce_scatter | solution.py:282
  479.7 40.7 %all-gather.16.cloned.1.call-done = bf16[1024,2048]{1,0:T(8,128)(2,1)} async-done(((bf16[128,2048]{1,0:T(8,128)(2,1)}), bf16[1024,2048]{1,0:T(8,128)(2,1)}) %all-gather.16.cloned.1.call-update) | async-done | bytes 4194320 | tf_op jit(solution)/shard_map/all_gather | solution.py:503
  588.6 16.9 %add_convert_fusion = bf16[1024,2048]{1,0:T(8,128)(2,1)} fusion(f32[1024,2048]{1,0:T(8,128)} %fusion.96, f32[1024,2048]{1,0:T(8,128)} %fusion.75, f32[1024,2048]{1,0:T(8,128)} %fusion.97, f32[1024,2048]{1,0:T(8,128)} %fusion.78, f32[1024,2048]{1,0:T(8,128)} %fusion.91, bf16[1024,256]{0,1:T(8,128)(2,1)S(1)} %bitcast.374, ...), kind=kOutput, calls=%fused_computation.10 | convolution fusion | flops 1086324736 | bytes 47710212 | tf_op jit(solution)/shard_map/dot_general | solution.py:60
  619.1 7.6 add_convert_fusion.2
  636.8 6.9 all-to-all-start
  652.9 7.3 all-gather.2
  674.0 10.9 %all-gather.3 = f32[4,2,30208]{2,1,0:T(2,128)S(1)} all-gather(f32[1,2,30208]{2,1,0:T(2,128)S(1)} %maximum_bitcast_fusion.2), channel_id=3, replica_groups=mesh['dp'=4,'expert'=8] {'dp'}, dimensions={0}, use_global_device_ids=true | all-gather | bytes 1208320 | tf_op jit(solution)/shard_map/all_gather | solution.py:158
  686.8 7.4 collective-permute-start.5
  697.6 7.2 collective-permute-done.5
  713.6 43.0 %reduce-scatter.10.cloned.1.call-done = bf16[128,2048]{1,0:T(8,128)(2,1)} async-done(((bf16[1024,2048]{1,0:T(8,128)(2,1)}), bf16[128,2048]{1,0:T(8,128)(2,1)}) %reduce-scatter.10.cloned.1.call-update) | async-done | bytes 524304 | tf_op jit(solution)/shard_map/reduce_scatter | solution.py:282
  (504 shorter events, 311.3 us)
Async XLA Ops:
  7.2 345.0 %copy-start = (bf16[2,128,5632]{2,1,0:T(8,128)(2,1)S(1)}, bf16[2,128,5632]{2,1,0:T(8,128)(2,1)}, u32[]{:S(2)}) copy-start(bf16[2,128,5632]{2,1,0:T(8,128)(2,1)} %param.47) | copy-start | bytes 8650756
  7.2 92.7 %all-gather.10.cloned.1.call-start = ((), (), s32[]{:S(2)}) async-start(), calls=%async_computation.9 | async-start | bytes 4718592 | tf_op jit(solution)/shard_map/all_gather | solution.py:284
  7.9 201.0 %reduce-scatter.8.cloned.1.call-start = ((), (), s32[]{:S(2)}) async-start(), calls=%async_computation.10 | async-start | bytes 4718592 | tf_op jit(solution)/shard_map/reduce_scatter | solution.py:282
  11.7 62.8 %collective-permute-start = (bf16[2048,256]{1,0:T(8,128)(2,1)}, bf16[2048,256]{1,0:T(8,128)(2,1)}, u32[]{:S(2)}, u32[]{:S(2)}) collective-permute-start(bf16[2048,256]{1,0:T(8,128)(2,1)} %get-tuple-element.33), channel_id=1, source_target_pairs={{0,0},{1,3},{2,6},{3,1},{4,4},{5,7},{6,2},{7,5},{8,8},{9,11},{10,1... | collective-permute-start | bytes 3145736 | tf_op jit(solution)/shard_map/ppermute | solution.py:82
  13.7 60.7 %collective-permute-start.2 = (bf16[2048,256]{1,0:T(8,128)(2,1)}, bf16[2048,256]{1,0:T(8,128)(2,1)}, u32[]{:S(2)}, u32[]{:S(2)}) collective-permute-start(bf16[2048,256]{1,0:T(8,128)(2,1)} %get-tuple-element.34), channel_id=1, source_target_pairs={{0,2},{1,5},{2,0},{3,3},{4,6},{5,1},{6,4},{7,7},{8,10},{9,13},{10,... | collective-permute-start | bytes 3145736 | tf_op jit(solution)/shard_map/ppermute | solution.py:82
  23.3 72.8 %collective-permute-start.1 = (bf16[2048,256]{1,0:T(8,128)(2,1)}, bf16[2048,256]{1,0:T(8,128)(2,1)}, u32[]{:S(2)}, u32[]{:S(2)}) collective-permute-start(bf16[2048,256]{1,0:T(8,128)(2,1)} %get-tuple-element.35), channel_id=1, source_target_pairs={{0,1},{1,4},{2,7},{3,2},{4,5},{5,0},{6,3},{7,6},{8,9},{9,12},{10,1... | collective-permute-start | bytes 3145736 | tf_op jit(solution)/shard_map/ppermute | solution.py:82
  28.7 103.6 %copy-start.34 = (f32[1024,64]{1,0:T(8,128)}, f32[1024,64]{1,0:T(8,128)S(1)}, u32[]{:S(2)}) copy-start(f32[1024,64]{1,0:T(8,128)S(1)} %get-tuple-element.76) | copy-start | bytes 786436
  158.6 100.7 %all-gather.12.cloned.1.call-start = ((), (), s32[]{:S(2)}) async-start(), calls=%async_computation.11 | async-start | bytes 4718592 | tf_op jit(solution)/shard_map/all_gather | solution.py:387
  213.4 93.1 %all-gather.14.cloned.1.call-start = ((), (), s32[]{:S(2)}) async-start(), calls=%async_computation.13 | async-start | bytes 4718592 | tf_op jit(solution)/shard_map/all_gather | solution.py:290
  214.0 206.4 %reduce-scatter.14.cloned.1.call-start = ((), (), s32[]{:S(2)}) async-start(), calls=%async_computation.15 | async-start | bytes 73728 | tf_op jit(solution)/shard_map/reduce_scatter | solution.py:476
  226.3 165.9 %copy-start.99 = (pred[1024]{0:T(1024)(128)(4,1)}, pred[1024]{0:T(1024)(128)(4,1)S(1)}, u32[]{:S(2)}) copy-start(pred[1024]{0:T(1024)(128)(4,1)S(1)} %compare_reduce_fusion) | copy-start | bytes 3076
  387.2 80.5 %reduce-scatter.12.cloned.1.call-start = ((), (), s32[]{:S(2)}) async-start(), calls=%async_computation.14 | async-start | bytes 4718592 | tf_op jit(solution)/shard_map/reduce_scatter | solution.py:282
  419.2 101.2 %all-gather.16.cloned.1.call-start = ((), (), s32[]{:S(2)}) async-start(), calls=%async_computation.16 | async-start | bytes 4718592 | tf_op jit(solution)/shard_map/all_gather | solution.py:503
  474.8 151.9 %all-gather.18.cloned.1.call-start = ((), (), s32[]{:S(2)}) async-start(), calls=%async_computation.20 | async-start | bytes 1658880 | tf_op jit(solution)/shard_map/all_gather | solution.py:593
  479.3 165.6 %reduce-scatter.18.cloned.1.call-start = ((), (), s32[]{:S(2)}) async-start(), calls=%async_computation.18 | async-start | bytes 442368 | tf_op jit(solution)/shard_map/reduce_scatter | solution.py:154
  576.9 96.1 %reduce-scatter.20.cloned.1.call-start = ((), (), s32[]{:S(2)}) async-start(), calls=%async_computation.19 | async-start | bytes 811008 | tf_op jit(solution)/shard_map/reduce_scatter | solution.py:154
  588.5 123.8 %reduce-scatter.16.cloned.1.call-start = ((), (), s32[]{:S(2)}) async-start(), calls=%async_computation.17 | async-start | bytes 4718592 | tf_op jit(solution)/shard_map/reduce_scatter | solution.py:282
  605.6 151.1 %reduce-scatter.10.cloned.1.call-start = ((), (), s32[]{:S(2)}) async-start(), calls=%async_computation.12 | async-start | bytes 4718592 | tf_op jit(solution)/shard_map/reduce_scatter | solution.py:282
  636.8 11.1 %all-to-all-start = ((f32[8,2,768]{2,1,0:T(2,128)}), f32[8,2,768]{2,1,0:T(2,128)S(1)}, u32[]{:S(2)}, u32[]{:S(2)}) async-start(f32[8,2,768]{2,1,0:T(2,128)} %all_to_all.28), calls=%async_computation.6 | async-start | bytes 98304 | tf_op jit(solution)/shard_map/all_to_all | solution.py:156
  647.9 18.0 %all-to-all-start.1 = ((f32[8,2,2368]{2,1,0:T(2,128)}), f32[8,2,2368]{2,1,0:T(2,128)S(1)}, u32[]{:S(2)}, u32[]{:S(2)}) async-start(f32[8,2,2368]{2,1,0:T(2,128)} %all_to_all.32), calls=%async_computation.8 | async-start | bytes 311296 | tf_op jit(solution)/shard_map/all_to_all | solution.py:156
  660.9 6.7 collective-permute-start.4
  661.1 11.6 %collective-permute-start.3 = (f32[2,12288]{1,0:T(2,128)S(1)}, f32[2,12288]{1,0:T(2,128)S(1)}, u32[]{:S(2)}, u32[]{:S(2)}) collective-permute-start(f32[2,12288]{1,0:T(2,128)S(1)} %get-tuple-element.68), channel_id=1, source_target_pairs={{0,0},{1,4},{2,1},{3,5},{4,2},{5,6},{6,3},{7,7},{8,8},{9,12},{10,9... | collective-permute-start | bytes 294920 | tf_op jit(solution)/shard_map/ppermute | solution.py:168
  686.3 11.3 %collective-permute-start.6 = (f32[2,30208]{1,0:T(2,128)S(1)}, f32[2,30208]{1,0:T(2,128)S(1)}, u32[]{:S(2)}, u32[]{:S(2)}) collective-permute-start(f32[2,30208]{1,0:T(2,128)S(1)} %get-tuple-element.57), channel_id=1, source_target_pairs={{0,4},{1,0},{2,5},{3,1},{4,6},{5,2},{6,7},{7,3},{8,12},{9,8},{10,1... | collective-permute-start | bytes 725000 | tf_op jit(solution)/shard_map/ppermute | solution.py:168
  686.8 18.1 %collective-permute-start.5 = (f32[2,30208]{1,0:T(2,128)S(1)}, f32[2,30208]{1,0:T(2,128)S(1)}, u32[]{:S(2)}, u32[]{:S(2)}) collective-permute-start(f32[2,30208]{1,0:T(2,128)S(1)} %get-tuple-element.58), channel_id=1, source_target_pairs={{0,0},{1,4},{2,1},{3,5},{4,2},{5,6},{6,3},{7,7},{8,8},{9,12},{10,9... | collective-permute-start | bytes 725000 | tf_op jit(solution)/shard_map/ppermute | solution.py:168
  (125 other events, 1420.3 us)
Sparse Core Ops, SparseCore 0:
  9.6 78.1 all-gather.9
  158.7 50.2 reduce-scatter.7
  213.5 45.7 all-gather.11
  260.8 45.6 all-gather.13
  387.3 23.6 reduce-scatter.13
  419.3 48.3 reduce-scatter.11
  474.9 45.4 all-gather.15
  522.8 28.2 all-gather.17
  577.0 24.1 reduce-scatter.17
  603.3 29.9 reduce-scatter.19
  635.6 71.6 reduce-scatter.15
  709.4 47.2 reduce-scatter.9

commit v2 on v1

--- a/solution.py
+++ b/solution.py
@@ -77,21 +77,40 @@
 
 def head_weights(columns, owner_index, owners, slot_count, head_start, width):
     model_width_size, held = columns.shape
-    if slot_count == 1 and held == 3 * width and owners % 3:
-        moved = [
-            lax.ppermute(
-                columns[:, step * width : (step + 1) * width],
-                "expert",
-                [(source, (3 * source + step) % owners) for source in range(owners)],
-            )
-            for step in range(3)
-        ]
-        stacked = jnp.stack(moved)
-        return jnp.stack(
+    groups = lax.axis_size("dp")
+    group_index = lax.axis_index("dp")
+    if slot_count == 1 and held == 3 * width and owners % 3 and groups & (groups - 1) == 0:
+        share = model_width_size // groups
+        mine = lax.dynamic_slice_in_dim(columns, group_index * share, share, 0)
+        moved = jnp.stack(
             [
-                lax.dynamic_index_in_dim(stacked, (owner_index + owners * kind) % 3, 0, False)
+                lax.ppermute(
+                    mine[:, step * width : (step + 1) * width],
+                    "expert",
+                    [(source, (3 * source + step) % owners) for source in range(owners)],
+                )
+                for step in range(3)
+            ]
+        )
+        kinds = jnp.stack(
+            [
+                lax.dynamic_index_in_dim(moved, (owner_index + owners * kind) % 3, 0, False)
                 for kind in range(3)
             ]
+        )
+        shares = jnp.stack(
+            [kinds]
+            + [
+                lax.ppermute(kinds, "dp", [(source, source ^ step) for source in range(groups)])
+                for step in range(1, groups)
+            ]
+        )
+        return jnp.concatenate(
+            [
+                lax.dynamic_index_in_dim(shares, group_index ^ place, 0, False)
+                for place in range(groups)
+            ],
+            axis=1,
         )
     full = lax.all_gather(columns, "expert", axis=1, tiled=True)
     return jnp.stack(
@@ -114,7 +133,7 @@
 
 
 def reduce_adapters(
-    partial, owned, owned_starts, owned_totals, adapter_index, adapter_groups, owner_index, owners
+    partial, owned, owned_starts, owned_totals, adapter_index, owner_index, owners
 ):
     groups = lax.axis_size("dp")
     group_index = lax.axis_index("dp")
@@ -148,19 +167,30 @@
     local = ADAPTER_COUNT // groups
     own_rows = ADAPTER_RANK // owners
     held = sum(partial_sizes)
-    padded = -(-held // (8 * 128)) * 8 * 128
-    tall = jnp.pad(partial_all, ((0, 0), (0, padded - held)))
-    tall = tall.reshape(8 * ADAPTER_RANK, padded // 8)
-    scattered = lax.psum_scatter(tall, "expert", scatter_dimension=0, tiled=True)
-    scattered = scattered.reshape(own_rows, padded)
-    moved = lax.all_to_all(owned_all, "expert", split_axis=0, concat_axis=1, tiled=True)
-    joined = jnp.concatenate([scattered, moved], axis=1)
-    gathered = lax.all_gather(joined, "dp", axis=0)
+    joined = jnp.concatenate([partial_all, owned_all], axis=1).astype(jnp.bfloat16)
+    moved = lax.all_to_all(
+        joined.reshape(owners, own_rows, joined.shape[1]),
+        "expert",
+        split_axis=0,
+        concat_axis=0,
+        tiled=True,
+    )
+    scattered = jnp.sum(moved[:, :, :held].astype(jnp.float32), axis=0).astype(jnp.bfloat16)
+    placed = [
+        jnp.transpose(value, (1, 0, 2)).reshape(own_rows, owners * size)
+        for value, size in zip(cut(moved[:, :, held:], owned_sizes), owned_sizes)
+    ]
+    label = jnp.broadcast_to(adapter_index[:, None], (own_rows, 128)).astype(jnp.bfloat16)
+    gathered = lax.all_gather(
+        jnp.concatenate([scattered] + placed + [label], axis=1), "dp", axis=0
+    ).astype(jnp.float32)
+    labels = gathered[:, :, -1:]
+    gathered = gathered[:, :, :-128]
     sums = []
     for which in range(local):
-        mine = (adapter_groups == group_index * local + which).astype(jnp.float32)
-        sums.append(jnp.sum(jnp.where(mine[:, None, None] > 0, gathered, 0.0), axis=0))
-    sums = jnp.stack(sums)
+        wanted = labels == (group_index * local + which).astype(jnp.float32)
+        sums.append(jnp.sum(jnp.where(wanted, gathered, 0.0), axis=0))
+    sums = jnp.stack(sums).astype(jnp.bfloat16)
     arrived = []
     for step in range(local):
         piece = lax.dynamic_index_in_dim(sums, (step + owner_index) % local, 0, False)
@@ -183,13 +213,8 @@
         ],
         axis=0,
     )
-    pieces = cut(rows[:, :held], partial_sizes)
-    wide = rows[:, padded:].reshape(local * own_rows, owners, sum(owned_sizes))
-    owned_pieces = [
-        value.reshape(local * own_rows, owners * size)
-        for value, size in zip(cut(wide, owned_sizes), owned_sizes)
-    ]
-    return pieces, owned_pieces
+    pieces = cut(rows.astype(jnp.float32), partial_sizes + [owners * size for size in owned_sizes])
+    return pieces[: len(partial)], pieces[len(partial) :]
 
 
 def on_device(
@@ -286,7 +311,7 @@
         attention_query_key_value, owner_index, owners, slot_count, head_start, width
     )
     routes_all = lax.all_gather(routes, "expert", axis=0, tiled=True)
-    adapter_groups = lax.all_gather(adapter_slot_index, "dp", axis=0, tiled=True)
+    tokens_all, routes_all = lax.optimization_barrier((tokens_all, routes_all))
     upstream_all = lax.all_gather(cotangent, "expert", axis=0, tiled=True)
     if attention_output_weight.shape[0] == width:
         output_weight = attention_output_weight
@@ -428,6 +453,11 @@
     shared_part = narrow_product(shared_hidden, shared_down_weight) + narrow_product(
         down_middle, down_second
     )
+    layer_part = (
+        token_product(spread, (row_gate * expert_result.astype(jnp.float32)).astype(half))
+        + shared_weight * shared_part
+    )
+    layer_sum = scatter_rows(layer_part)
     upstream_wide = upstream_all.astype(jnp.float32)
     shared_dot = jnp.sum(upstream_wide * shared_part, axis=1)
 
@@ -460,6 +490,7 @@
         chosen(rows_product(shared_grad_pre[kind], shared_second[kind]), selector)
         for kind in range(2)
     ]
+    copy_grad, layer_sum = lax.optimization_barrier((copy_grad, layer_sum))
     second_part = token_product(spread, copy_grad) + sum(
         rows_product(shared_grad_pre[kind], shared_gate_up_weight[kind])
         + rows_product(shared_inner[kind], shared_first[kind])
@@ -475,11 +506,6 @@
     )
     own_dots = jnp.transpose(lax.psum_scatter(dots, "expert", scatter_dimension=1, tiled=True))
     second_sum = scatter_rows(second_part).astype(jnp.float32)
-    layer_part = (
-        token_product(spread, (row_gate * expert_result.astype(jnp.float32)).astype(half))
-        + shared_weight * shared_part
-    )
-
     own_weights = own_rows(gate_weights)
     gate_grads = own_dots[:, :experts]
     centered = own_weights * (
@@ -541,43 +567,36 @@
     tokens_grad = residual_grad + rms_backward(
         input_rows, factor_first, attention_norm_gain, first_grad
     )
-    layer_out = (residual_stream + scatter_rows(layer_part).astype(jnp.float32)).astype(half)
+    layer_out = (residual_stream + layer_sum.astype(jnp.float32)).astype(half)
 
     own_router_middle = own_rows(router_middle)
-    early, early_own = reduce_adapters(
-        [
+    router_grad_b = token_product(own_router_middle, logit_grads)
+    spare = -experts % 128
+    summed, owned = reduce_adapters(
+        [slot_wide(token_product(qkv_inner[kind], first_narrow)) for kind in range(3)]
+        + [
             slot_wide(token_product(output_middle, output_upstream)),
             token_product(shared_inner[0], second_all),
             token_product(shared_inner[1], second_all),
             token_product(down_middle, value_grads),
             token_product(router_inner, second_own),
-            token_product(own_router_middle, logit_grads),
+            jnp.pad(router_grad_b, ((0, 0), (0, spare))),
         ],
-        [
+        [slot_wide(token_product(attention_middle[kind], pre_grads[kind])) for kind in range(3)]
+        + [
             slot_wide(token_product(output_inner, attended_low)),
             token_product(shared_middle[0], shared_grad_pre[0]),
             token_product(shared_middle[1], shared_grad_pre[1]),
             token_product(down_inner, shared_hidden),
         ],
-        [head_column] + [owner_index * shared_wide] * 3,
-        [model_width_size] + [owners * shared_wide] * 3,
+        [head_column] * 4 + [owner_index * shared_wide] * 3,
+        [model_width_size] * 4 + [owners * shared_wide] * 3,
         adapter_slot_index,
-        adapter_groups,
         owner_index,
         owners,
     )
-    late, late_own = reduce_adapters(
-        [slot_wide(token_product(qkv_inner[kind], first_narrow)) for kind in range(3)],
-        [slot_wide(token_product(attention_middle[kind], pre_grads[kind])) for kind in range(3)],
-        [head_column] * 3,
-        [model_width_size] * 3,
-        adapter_slot_index,
-        adapter_groups,
-        owner_index,
-        owners,
-    )
-    attn_grad_a = jnp.stack([jnp.transpose(value) for value in late + [early_own[0]]])
-    attn_grad_b = jnp.stack(late_own + [early[0]])
+    attn_grad_a = jnp.stack([jnp.transpose(value) for value in summed[:3] + owned[3:4]])
+    attn_grad_b = jnp.stack(owned[:3] + summed[3:4])
 
     wide_grads = jnp.concatenate(
         [
@@ -587,21 +606,23 @@
             token_product(expert_middle[1], expert_grad_pre[1]),
             token_product(expert_down_inner, expert_hidden),
             token_product(expert_down_middle, expert_upstream),
+            jnp.broadcast_to(
+                jnp.repeat(adapter_slot_index, ADAPTER_RANK).astype(jnp.float32)[:, None],
+                (slot_count * ADAPTER_RANK, 128),
+            ),
         ],
         axis=1,
     ).astype(half)
     expert_grads = lax.all_gather(wide_grads, "dp", axis=0, tiled=True)
     rank_range = jnp.arange(ADAPTER_COUNT * ADAPTER_RANK, dtype=jnp.int32)
     source_rank = jnp.arange(expert_grads.shape[0], dtype=jnp.int32)
-    source_place = jnp.repeat(adapter_groups, ADAPTER_RANK) * ADAPTER_RANK + (
-        source_rank % ADAPTER_RANK
-    )
+    source_place = expert_grads[:, -1].astype(jnp.int32) * ADAPTER_RANK + source_rank % ADAPTER_RANK
     placement = (source_place[:, None] == rank_range[None, :]).astype(half)
     feed = expert_down_weight.shape[1]
     bounds = [0, model_width_size, 2 * model_width_size]
     bounds += [bounds[-1] + feed, bounds[-1] + 2 * feed, bounds[-1] + 3 * feed]
     expert_pieces = [
-        expert_grads[:, start:stop] for start, stop in zip(bounds, bounds[1:] + [None])
+        expert_grads[:, start:stop] for start, stop in zip(bounds, bounds[1:] + [expert_grads.shape[1] - 128])
     ]
     in_grad_a = jnp.stack([token_product(value, placement) for value in expert_pieces[:2]])
     in_grad_b = jnp.stack([token_product(placement, value) for value in expert_pieces[2:4]])
@@ -612,12 +633,12 @@
         tokens_grad,
         attn_grad_a,
         attn_grad_b,
-        jnp.transpose(early[4]),
-        early[5],
-        jnp.stack([jnp.transpose(early[1]), jnp.transpose(early[2])]),
-        jnp.stack(early_own[1:3]),
-        jnp.transpose(early_own[3]),
-        early[3],
+        jnp.transpose(summed[7]),
+        summed[8][:, :experts],
+        jnp.stack([jnp.transpose(summed[4]), jnp.transpose(summed[5])]),
+        jnp.stack(owned[4:6]),
+        jnp.transpose(owned[6]),
+        summed[6],
         in_grad_a[None],
         in_grad_b[None],
         down_grad_a[None],

time: 783 us -> 709 us (0.905); the launches traced: 768 us -> 704 us
  waiting for transfers between devices: 311 us -> 249 us
  starting transfers between devices: 38.4 us -> 21 us
  matrix products: 278 us -> 287 us
    ppermute x3 -> x6, waiting for transfers between devices: 64.4 us -> 10.8 us  [the longest x3 10.8 us: head_weights(): lax.ppermute(mine[:, step * width:(step + 1) * width], 'expert', [(source...]
    reduce_scatter x4, waiting for transfers between devices: 137 us -> 114 us  [scatter_rows(): lax.psum_scatter(values.astype(half), 'expert', scatter_dimension=0, tile...]
    all_gather x1, blocking collectives: 12.2 us -> 32.3 us  [on_device(): routes_all = lax.all_gather(routes, 'expert', axis=0, tiled=True)]
    all_gather x1, waiting for transfers between devices: 32.3 us -> 44.6 us  [on_device(): second_all = lax.all_gather(second_own, 'expert', axis=0, tiled=True)]
    all_gather x1, waiting for transfers between devices: 15.8 us -> 27.6 us  [on_device(): upstream_all = lax.all_gather(cotangent, 'expert', axis=0, tiled=True)]
    dot_general x32 -> x33, matrix products: 125 us -> 134 us  [rows_product(): lax.dot_general(left_side, right_side, (((1,), (1,)), ((), ())), preferre...]
    all_gather x2 -> x1, blocking collectives: 18.2 us -> 9.74 us  [reduce_adapters(): lax.all_gather(jnp.concatenate([scattered] + placed + [label], axis=1), '...]
    concatenate x1 -> x16, local copies, waits for them, and re-layouts: 0.11 us -> 8.16 us  [the longest x12 7.13 us: reduce_adapters(): jnp.concatenate([partial_all, owned_all], axis=1).astype(jnp.bfloat16)]
  transfers between devices with their start and end apart: 21 -> 19, of which waited for: 13 -> 10; matrix products, arithmetic and copies ran while one was open for 26% -> 27% of each run, Pallas kernels for 0% -> 0%
where the time goes in v2:
time: 709 us; the launch traced here: 704 us
  matrix products  287 us (40%)
  waiting for transfers between devices  249 us (35%)
  other arithmetic  57.7 us (8%)
  blocking collectives  42 us (6%)
  local copies, waits for them, and re-layouts  30.1 us (4%)
  starting transfers between devices  21 us (3%)
  between operations  17.5 us (2%)
    dot_general x33, matrix products, rows_product(): lax.dot_general(left_side, right_side, (((1,), (1,)), ((), ())), preferre...  134 us
    reduce_scatter x4, waiting for transfers between devices, scatter_rows(): lax.psum_scatter(values.astype(half), 'expert', scatter_dimension=0, tile...  114 us
    dot_general x36, matrix products, narrow_product(): return jnp.dot(left_side, right_side, preferred_element_type=jnp.float32)  80.4 us
    dot_general x30, matrix products, token_product(): lax.dot_general(left_side, right_side, (((0,), (0,)), ((), ())), preferre...  49.8 us
    all_gather x1, waiting for transfers between devices, on_device(): second_all = lax.all_gather(second_own, 'expert', axis=0, tiled=True)  44.6 us
    all_gather x1, waiting for transfers between devices, on_device(): lax.all_gather(residual_grad.astype(half), 'expert', axis=0, tiled=True)  34.6 us
    all_gather x1, blocking collectives, on_device(): routes_all = lax.all_gather(routes, 'expert', axis=0, tiled=True)  32.3 us
    all_gather x1, waiting for transfers between devices, on_device(): upstream_all = lax.all_gather(cotangent, 'expert', axis=0, tiled=True)  27.6 us
  transfers between devices with their start and end apart: 19, of which 10 were waited for; matrix products, arithmetic and copies ran while one was open for 27% of the time, Pallas kernels for 0%

profile of v2, /device:TPU:11, one launch (start us, length us, event | category | flops | bytes accessed | tf_op | source)
XLA Modules:
  0.0 704.0 jit_solution(16555448382478104826)
XLA Ops:
  17.7 10.3 %collective-permute-done.1 = bf16[512,256]{1,0:T(8,128)(2,1)} collective-permute-done((bf16[512,256]{1,0:T(8,128)(2,1)S(1)}, bf16[512,256]{1,0:T(8,128)(2,1)}, u32[]{:S(2)}, u32[]{:S(2)}) %collective-permute-start.1) | collective-permute-done | bytes 262176 | tf_op jit(solution)/shard_map/ppermute | solution.py:87
  33.8 32.3 %all_gather.25 = s32[1024,4]{0,1:T(4,128)S(1)} all-gather(s32[128,4]{0,1:T(4,128)S(1)} %copy-done.94), channel_id=1, replica_groups=mesh['dp'=4,'expert'=8] {'expert'}, dimensions={0}, use_global_device_ids=true | all-gather | bytes 18432 | tf_op jit(solution)/shard_map/all_gather | solution.py:313
  112.2 11.4 %fusion.185 = (f32[2,1024]{1,0:T(2,128)S(1)}, f32[2,1024,1024]{1,2,0:T(8,128)}) fusion(f32[1024,1024]{0,1:T(8,128)} %get-tuple-element.94, pred[1024,1024]{0,1:T(8,128)(4,1)} %get-tuple-element.93, bf16[1024,2,64]{2,0,1:T(8,128)(2,1)} %get-tuple-element.56, bf16[1024,2,64]{2,0,1:T(8,128)(2,1)} %get-tuple-element.57, ...), kind=kOutput, calls=%fused_computation.413 | convolution fusion | flops 549454848 | bytes 14688256 | tf_op jit(solution)/shard_map/sub | solution.py:397
  136.9 53.0 %reduce-scatter.6.cloned.1.call-done = bf16[128,2048]{1,0:T(8,128)(2,1)} async-done(((bf16[1024,2048]{1,0:T(8,128)(2,1)}), bf16[128,2048]{1,0:T(8,128)(2,1)}) %reduce-scatter.6.cloned.1.call-update) | async-done | bytes 524304 | tf_op jit(solution)/shard_map/reduce_scatter | solution.py:307
  195.1 44.6 %all-gather.10.cloned.1.call-done = bf16[1024,2048]{1,0:T(8,128)(2,1)} async-done(((bf16[128,2048]{1,0:T(8,128)(2,1)}), bf16[1024,2048]{1,0:T(8,128)(2,1)}) %all-gather.10.cloned.1.call-update) | async-done | bytes 4194320 | tf_op jit(solution)/shard_map/all_gather | solution.py:412
  248.3 5.6 fusion.9
  259.3 27.6 %all-gather.12.cloned.1.call-done = bf16[1024,2048]{1,0:T(8,128)(2,1)} async-done(((bf16[128,2048]{1,0:T(8,128)(2,1)}), bf16[1024,2048]{1,0:T(8,128)(2,1)}) %all-gather.12.cloned.1.call-update) | async-done | bytes 4194320 | tf_op jit(solution)/shard_map/all_gather | solution.py:315
  340.6 5.6 add_convert_fusion.2
  355.1 6.4 fusion.17
  374.3 5.8 fusion.29
  380.1 5.7 fusion.33
  385.8 5.5 fusion.11
  397.3 7.7 %add_convert_fusion.5 = bf16[576,2048]{1,0:T(8,128)(2,1)} fusion(f32[576,2048]{1,0:T(8,128)} %fusion.11, f32[576,2048]{1,0:T(8,128)} %fusion.7, f32[576,2048]{1,0:T(8,128)} %fusion.83, bf16[576,16]{0,1:T(8,128)(2,1)S(1)} %convolution_convert_fusion.35, bf16[1,2,2048,128]{3,2,1,0:T(8,128)(2,1)S(1)} %copy-done.41, s32[]{:T(128)S(6)} %add.407, s32[]{:T(128)S(6)} %select_n.181), kind=kOutput, calls=%fused_computation.39 | convolution fusion | flops 42467328 | bytes 17059848 | tf_op jit(solution)/shard_map/dot_general | solution.py:60
  405.0 7.3 %fusion.46 = f32[1024,2048]{1,0:T(8,128)} fusion(bf16[576,2048]{1,0:T(8,128)(2,1)} %add_convert_fusion.5, s32[1024]{0:T(1024)S(1)} %add_bitcast_fusion, pred[1024]{0:T(1024)(128)(4,1)S(1)} %compare_reduce_fusion), kind=kOutput, calls=%fused_computation.89 | convolution fusion | flops 2417098752 | bytes 10753024 | tf_op jit(solution)/shard_map/dot_general | solution.py:66
  412.4 14.0 %add_convert_fusion.1 = bf16[1024,2048]{1,0:T(8,128)(2,1)} fusion(f32[1024,2048]{1,0:T(8,128)} %fusion.46, f32[1024,2048]{1,0:T(8,128)} %fusion.29, f32[1024,2048]{1,0:T(8,128)} %fusion.33, f32[1024,2048]{1,0:T(8,128)} %fusion.84, bf16[1024,16]{0,1:T(8,128)(2,1)S(1)} %convolution_convert_fusion.16, bf16[2,2048,128]{2,1,0:T(8,128)(2,1)S(1)} %copy-done.38, ...), kind=kOutput, calls=%fused_computation.12 | convolution fusion | flops 77594624 | bytes 38305800 | tf_op jit(solution)/shard_map/dot_general | solution.py:60
  437.3 39.6 %reduce-scatter.10.cloned.1.call-done = bf16[128,2048]{1,0:T(8,128)(2,1)} async-done(((bf16[1024,2048]{1,0:T(8,128)(2,1)}), bf16[128,2048]{1,0:T(8,128)(2,1)}) %reduce-scatter.10.cloned.1.call-update) | async-done | bytes 524304 | tf_op jit(solution)/shard_map/reduce_scatter | solution.py:307
  501.1 6.6 all-gather.16.cloned.1.call-done
  521.0 34.6 %all-gather.14.cloned.1.call-done = bf16[1024,2048]{1,0:T(8,128)(2,1)} async-done(((bf16[128,2048]{1,0:T(8,128)(2,1)}), bf16[1024,2048]{1,0:T(8,128)(2,1)}) %all-gather.14.cloned.1.call-update) | async-done | bytes 4194320 | tf_op jit(solution)/shard_map/all_gather | solution.py:529
  574.5 5.9 fusion.78
  581.5 6.0 fusion.76
  618.3 16.8 %add_convert_fusion = bf16[1024,2048]{1,0:T(8,128)(2,1)} fusion(f32[1024,2048]{1,0:T(8,128)} %fusion.87, f32[1024,2048]{1,0:T(8,128)} %fusion.78, f32[1024,2048]{1,0:T(8,128)} %fusion.88, f32[1024,2048]{1,0:T(8,128)} %fusion.76, f32[1024,2048]{1,0:T(8,128)} %fusion.82, bf16[1024,256]{0,1:T(8,128)(2,1)S(1)} %bitcast.408, ...), kind=kOutput, calls=%fused_computation.10 | convolution fusion | flops 1086324736 | bytes 47710208 | tf_op jit(solution)/shard_map/dot_general | solution.py:60
  636.4 9.7 %all-gather.1 = bf16[4,2,41728]{2,1,0:T(2,128)(2,1)S(1)} all-gather(bf16[1,2,41728]{2,1,0:T(2,128)(2,1)S(1)} %bitcast.424), channel_id=2, replica_groups=mesh['dp'=4,'expert'=8] {'dp'}, dimensions={0}, use_global_device_ids=true | all-gather | bytes 834560 | tf_op jit(solution)/shard_map/all_gather | solution.py:184
  655.2 9.6 %collective-permute-done.6 = bf16[2,41600]{1,0:T(2,128)(2,1)S(1)} collective-permute-done((bf16[2,41600]{1,0:T(2,128)(2,1)S(1)}, bf16[2,41600]{1,0:T(2,128)(2,1)S(1)}, u32[]{:S(2)}, u32[]{:S(2)}) %collective-permute-start.6) | collective-permute-done | bytes 166432 | tf_op jit(solution)/shard_map/ppermute | solution.py:198
  670.6 21.3 %reduce-scatter.14.cloned.1.call-done = bf16[128,2048]{1,0:T(8,128)(2,1)} async-done(((bf16[1024,2048]{1,0:T(8,128)(2,1)}), bf16[128,2048]{1,0:T(8,128)(2,1)}) %reduce-scatter.14.cloned.1.call-update) | async-done | bytes 524304 | tf_op jit(solution)/shard_map/reduce_scatter | solution.py:307
  (477 shorter events, 293.6 us)
Async XLA Ops:
  7.2 296.2 %copy-start = (bf16[2,128,5632]{2,1,0:T(8,128)(2,1)S(1)}, bf16[2,128,5632]{2,1,0:T(8,128)(2,1)}, u32[]{:S(2)}) copy-start(bf16[2,128,5632]{2,1,0:T(8,128)(2,1)} %param.47) | copy-start | bytes 8650756
  7.2 69.3 %all-gather.8.cloned.1.call-start = ((), (), s32[]{:S(2)}) async-start(), calls=%async_computation.6 | async-start | bytes 4718592 | tf_op jit(solution)/shard_map/all_gather | solution.py:309
  7.9 182.0 %reduce-scatter.6.cloned.1.call-start = ((), (), s32[]{:S(2)}) async-start(), calls=%async_computation.7 | async-start | bytes 4718592 | tf_op jit(solution)/shard_map/reduce_scatter | solution.py:307
  9.9 7.7 %collective-permute-start = (bf16[512,256]{1,0:T(8,128)(2,1)}, bf16[512,256]{1,0:T(8,128)(2,1)}, u32[]{:S(2)}, u32[]{:S(2)}) collective-permute-start(bf16[512,256]{1,0:T(8,128)(2,1)} %get-tuple-element.45), channel_id=1, source_target_pairs={{0,0},{1,3},{2,6},{3,1},{4,4},{5,7},{6,2},{7,5},{8,8},{9,11},{10,1... | collective-permute-start | bytes 786440 | tf_op jit(solution)/shard_map/ppermute | solution.py:87
  12.0 15.9 %collective-permute-start.1 = (bf16[512,256]{1,0:T(8,128)(2,1)S(1)}, bf16[512,256]{1,0:T(8,128)(2,1)}, u32[]{:S(2)}, u32[]{:S(2)}) collective-permute-start(bf16[512,256]{1,0:T(8,128)(2,1)S(1)} %get-tuple-element.46), channel_id=1, source_target_pairs={{0,1},{1,4},{2,7},{3,2},{4,5},{5,0},{6,3},{7,6},{8,9},{9,12},{10,1... | collective-permute-start | bytes 786440 | tf_op jit(solution)/shard_map/ppermute | solution.py:87
  15.2 12.8 %collective-permute-start.2 = (bf16[512,256]{1,0:T(8,128)(2,1)S(1)}, bf16[512,256]{1,0:T(8,128)(2,1)}, u32[]{:S(2)}, u32[]{:S(2)}) collective-permute-start(bf16[512,256]{1,0:T(8,128)(2,1)S(1)} %get-tuple-element.47), channel_id=1, source_target_pairs={{0,2},{1,5},{2,0},{3,3},{4,6},{5,1},{6,4},{7,7},{8,10},{9,13},{10,... | collective-permute-start | bytes 786440 | tf_op jit(solution)/shard_map/ppermute | solution.py:87
  30.5 41.6 %collective-permute-start.4 = (bf16[3,512,256]{2,1,0:T(8,128)(2,1)}, bf16[3,512,256]{2,1,0:T(8,128)(2,1)}, u32[]{:S(2)}, u32[]{:S(2)}) collective-permute-start(bf16[3,512,256]{2,1,0:T(8,128)(2,1)} %get-tuple-element.63), channel_id=1, source_target_pairs={{0,16},{8,24},{16,0},{24,8},{1,17},{9,25},{17,1},{25,9},{2,18},{10... | collective-permute-start | bytes 2359304 | tf_op jit(solution)/shard_map/ppermute | solution.py:104
  31.8 40.3 %collective-permute-start.3 = (bf16[3,512,256]{2,1,0:T(8,128)(2,1)}, bf16[3,512,256]{2,1,0:T(8,128)(2,1)}, u32[]{:S(2)}, u32[]{:S(2)}) collective-permute-start(bf16[3,512,256]{2,1,0:T(8,128)(2,1)} %get-tuple-element.63), channel_id=1, source_target_pairs={{0,8},{8,0},{16,24},{24,16},{1,9},{9,1},{17,25},{25,17},{2,10},{10... | collective-permute-start | bytes 2359304 | tf_op jit(solution)/shard_map/ppermute | solution.py:104
  32.0 40.1 %collective-permute-start.5 = (bf16[3,512,256]{2,1,0:T(8,128)(2,1)}, bf16[3,512,256]{2,1,0:T(8,128)(2,1)}, u32[]{:S(2)}, u32[]{:S(2)}) collective-permute-start(bf16[3,512,256]{2,1,0:T(8,128)(2,1)} %get-tuple-element.63), channel_id=1, source_target_pairs={{0,24},{8,16},{16,8},{24,0},{1,25},{9,17},{17,9},{25,1},{2,26},{10... | collective-permute-start | bytes 2359304 | tf_op jit(solution)/shard_map/ppermute | solution.py:104
  136.8 53.1 %copy-start.10 = (bf16[128,2048]{1,0:T(8,128)(2,1)S(1)}, bf16[128,2048]{1,0:T(8,128)(2,1)}, u32[]{:S(2)}) copy-start(bf16[128,2048]{1,0:T(8,128)(2,1)} %param.27) | copy-start | bytes 1572868
  136.8 54.9 %copy-start.85 = (f32[2048]{0:T(1024)S(1)}, f32[2048]{0:T(1024)}, u32[]{:S(2)}) copy-start(f32[2048]{0:T(1024)} %param.30) | copy-start | bytes 24580
  136.8 57.6 %copy-start.87 = (bf16[2048]{0:T(1024)(128)(2,1)S(1)}, bf16[2048]{0:T(1024)(128)(2,1)}, u32[]{:S(2)}) copy-start(bf16[2048]{0:T(1024)(128)(2,1)} %param.36) | copy-start | bytes 12292
  136.9 102.8 %all-gather.10.cloned.1.call-start = ((), (), s32[]{:S(2)}) async-start(), calls=%async_computation.8 | async-start | bytes 4718592 | tf_op jit(solution)/shard_map/all_gather | solution.py:412
  191.8 51.5 %copy-start.91 = (f32[128]{0:T(128)}, f32[128]{0:T(128)S(1)}, u32[]{:S(2)}) copy-start(f32[128]{0:T(128)S(1)} %get-tuple-element.101) | copy-start | bytes 1540
  193.8 93.0 %all-gather.12.cloned.1.call-start = ((), (), s32[]{:S(2)}) async-start(), calls=%async_computation.9 | async-start | bytes 4718592 | tf_op jit(solution)/shard_map/all_gather | solution.py:315
  194.4 210.6 %reduce-scatter.8.cloned.1.call-start = ((), (), s32[]{:S(2)}) async-start(), calls=%async_computation.10 | async-start | bytes 4718592 | tf_op jit(solution)/shard_map/reduce_scatter | solution.py:307
  346.2 88.6 %reduce-scatter.12.cloned.1.call-start = ((), (), s32[]{:S(2)}) async-start(), calls=%async_computation.12 | async-start | bytes 73728 | tf_op jit(solution)/shard_map/reduce_scatter | solution.py:507
  396.8 80.0 %reduce-scatter.10.cloned.1.call-start = ((), (), s32[]{:S(2)}) async-start(), calls=%async_computation.11 | async-start | bytes 4718592 | tf_op jit(solution)/shard_map/reduce_scatter | solution.py:307
  426.4 81.3 %all-gather.16.cloned.1.call-start = ((), (), s32[]{:S(2)}) async-start(), calls=%async_computation.15 | async-start | bytes 1679360 | tf_op jit(solution)/shard_map/all_gather | solution.py:616
  434.8 120.8 %all-gather.14.cloned.1.call-start = ((), (), s32[]{:S(2)}) async-start(), calls=%async_computation.13 | async-start | bytes 4718592 | tf_op jit(solution)/shard_map/all_gather | solution.py:529
  613.2 22.0 %all-to-all-start = ((bf16[8,2,19648]{2,1,0:T(2,128)(2,1)}), bf16[8,2,19648]{2,1,0:T(2,128)(2,1)S(1)}, u32[]{:S(2)}, u32[]{:S(2)}) async-start(bf16[8,2,19648]{2,1,0:T(2,128)(2,1)} %concatenate.79), calls=%async_computation.5 | async-start | bytes 1261568 | tf_op jit(solution)/shard_map/all_to_all | solution.py:171
  618.3 73.6 %reduce-scatter.14.cloned.1.call-start = ((), (), s32[]{:S(2)}) async-start(), calls=%async_computation.14 | async-start | bytes 4718592 | tf_op jit(solution)/shard_map/reduce_scatter | solution.py:307
  649.2 15.6 %collective-permute-start.6 = (bf16[2,41600]{1,0:T(2,128)(2,1)S(1)}, bf16[2,41600]{1,0:T(2,128)(2,1)S(1)}, u32[]{:S(2)}, u32[]{:S(2)}) collective-permute-start(bf16[2,41600]{1,0:T(2,128)(2,1)S(1)} %get-tuple-element.91), channel_id=1, source_target_pairs={{0,0},{1,4},{2,1},{3,5},{4,2},{5,6},{6,3},{7,7},{8,8},{9,12},{10,9... | collective-permute-start | bytes 499208 | tf_op jit(solution)/shard_map/ppermute | solution.py:198
  652.3 12.5 %collective-permute-start.7 = (bf16[2,41600]{1,0:T(2,128)(2,1)S(1)}, bf16[2,41600]{1,0:T(2,128)(2,1)S(1)}, u32[]{:S(2)}, u32[]{:S(2)}) collective-permute-start(bf16[2,41600]{1,0:T(2,128)(2,1)S(1)} %get-tuple-element.92), channel_id=1, source_target_pairs={{0,4},{1,0},{2,5},{3,1},{4,6},{5,2},{6,7},{7,3},{8,12},{9,8},{10,1... | collective-permute-start | bytes 499208 | tf_op jit(solution)/shard_map/ppermute | solution.py:198
  (107 other events, 1020.0 us)
Sparse Core Ops, SparseCore 0:
  9.6 52.4 all-gather.7
  137.0 52.8 reduce-scatter.5
  193.9 45.7 all-gather.9
  241.2 45.6 all-gather.11
  346.4 48.3 reduce-scatter.7
  397.4 23.6 reduce-scatter.11
  426.5 50.2 reduce-scatter.9
  479.3 28.4 all-gather.15
  509.3 46.2 all-gather.13
  635.3 56.5 reduce-scatter.13

commit v3 on v2

--- a/solution.py
+++ b/solution.py
@@ -68,11 +68,44 @@
     )
 
 
+def joint_products(left_side, right_sides):
+    product = narrow_product(left_side, jnp.concatenate(right_sides, axis=1))
+    pieces, at = [], 0
+    for value in right_sides:
+        pieces.append(product[:, at : at + value.shape[1]])
+        at += value.shape[1]
+    return pieces
+
+
+def block_diagonal(blocks):
+    rows = []
+    for place, value in enumerate(blocks):
+        row = [
+            value if other == place else jnp.zeros((value.shape[0], side.shape[1]), value.dtype)
+            for other, side in enumerate(blocks)
+        ]
+        rows.append(jnp.concatenate(row, axis=1))
+    return jnp.concatenate(rows, axis=0)
+
+
+def diagonal_blocks(product, count):
+    rows, columns = product.shape[0] // count, product.shape[1] // count
+    return [
+        product[place * rows : (place + 1) * rows, place * columns : (place + 1) * columns]
+        for place in range(count)
+    ]
+
+
+def row_blocks(product, count):
+    rows = product.shape[0] // count
+    return [product[place * rows : (place + 1) * rows] for place in range(count)]
+
+
 def gated_back(gate_value, up_value, grad_hidden):
     sigmoid_gate = jax.nn.sigmoid(gate_value)
     grad_gate = grad_hidden * up_value * sigmoid_gate * (1.0 + gate_value * (1.0 - sigmoid_gate))
     grad_up = grad_hidden * gate_value * sigmoid_gate
-    return (grad_gate.astype(jnp.bfloat16), grad_up.astype(jnp.bfloat16))
+    return jnp.concatenate([grad_gate, grad_up], axis=1).astype(jnp.bfloat16)
 
 
 def head_weights(columns, owner_index, owners, slot_count, head_start, width):
@@ -105,20 +138,19 @@
                 for step in range(1, groups)
             ]
         )
-        return jnp.concatenate(
+        ordered = jnp.concatenate(
             [
                 lax.dynamic_index_in_dim(shares, group_index ^ place, 0, False)
                 for place in range(groups)
             ],
             axis=1,
         )
+        return [ordered[kind] for kind in range(3)]
     full = lax.all_gather(columns, "expert", axis=1, tiled=True)
-    return jnp.stack(
-        [
-            lax.dynamic_slice_in_dim(full, kind * model_width_size + head_start * HEAD_DIM, width, 1)
-            for kind in range(3)
-        ]
-    )
+    return [
+        lax.dynamic_slice_in_dim(full, kind * model_width_size + head_start * HEAD_DIM, width, 1)
+        for kind in range(3)
+    ]
 
 
 def spread_adapters(compact, adapter_index):
@@ -334,6 +366,9 @@
         narrow = values.astype(half)
         return narrow if picker is None else narrow * picker
 
+    def twice(picker):
+        return None if picker is None else jnp.concatenate([picker, picker], axis=1)
+
     attention_adapter = slot_value(adapter_slot_index) * ADAPTER_RANK
     attention_first = lax.dynamic_slice_in_dim(
         attention_adapter_first, attention_adapter, ADAPTER_RANK, 2
@@ -375,14 +410,12 @@
     positions = jnp.arange(seq_length, dtype=jnp.int32)
     cosine_table, sine_table = rope_tables(positions, HEAD_DIM)
     shaped = (seq_length, head_count, HEAD_DIM)
-    attention_middle = [
-        narrow_product(first_narrow, attention_first[kind]).astype(half) for kind in range(3)
-    ]
-    projected = [
-        narrow_product(first_narrow, qkv_weights[kind])
-        + narrow_product(attention_middle[kind], qkv_second[kind])
-        for kind in range(3)
-    ]
+    qkv_joined = jnp.concatenate(qkv_weights + [attention_first[kind] for kind in range(3)], axis=1)
+    qkv_up = block_diagonal([qkv_second[kind] for kind in range(3)])
+    projected = narrow_product(first_narrow, qkv_joined)
+    attention_middle = projected[:, 3 * width :].astype(half)
+    projected = projected[:, : 3 * width] + narrow_product(attention_middle, qkv_up)
+    projected = [projected[:, kind * width : (kind + 1) * width] for kind in range(3)]
     query_low = rotate(projected[0].reshape(shaped), cosine_table, sine_table, 1.0).astype(half)
     key_low = rotate(projected[1].reshape(shaped), cosine_table, sine_table, 1.0).astype(half)
     value_low = projected[2].reshape(shaped).astype(half)
@@ -401,6 +434,7 @@
         "hqk,khd->qhd", probabilities_low, value_low, preferred_element_type=jnp.float32
     )
     attended_low = attended.reshape(seq_length, width).astype(half)
+    attended_low, upstream_all = lax.optimization_barrier((attended_low, upstream_all))
     output_middle = narrow_product(attended_low, output_first).astype(half)
     attention_part = narrow_product(attended_low, output_weight) + narrow_product(
         output_middle, output_second
@@ -411,28 +445,29 @@
     second_own = normed_second.astype(half)
     second_all = lax.all_gather(second_own, "expert", axis=0, tiled=True)
 
-    router_middle = chosen(narrow_product(second_all, router_first), selector)
-    router_scores = narrow_product(second_all, router_projection) + narrow_product(
-        router_middle, router_second
-    )
+    router_raw, router_plain, gate_raw = joint_products(
+        second_all, [router_first, router_projection, shared_gate_vector[:, None]]
+    )
+    router_middle = chosen(router_raw, selector)
+    router_scores = router_plain + narrow_product(router_middle, router_second)
     reach = jnp.max(jnp.where(route_hits, router_scores, MASKED), axis=1, keepdims=True)
     gate_exponents = jnp.where(route_hits, jnp.exp(jnp.minimum(router_scores - reach, 0.0)), 0.0)
     gate_weights = gate_exponents / jnp.sum(gate_exponents, axis=1, keepdims=True)
     own_gate = jnp.sum(jnp.where(expert_range[None, :] == owner_index, gate_weights, 0.0), axis=1)
     row_gate = jnp.sum(jnp.where(placed, own_gate[None, :], 0.0), axis=1, keepdims=True)
-    shared_weight = jax.nn.sigmoid(
-        narrow_product(second_all, shared_gate_vector[:, None])
-    )
+    shared_weight = jax.nn.sigmoid(gate_raw)
 
     expert_rows = narrow_product(spread, second_all).astype(half)
-    expert_middle = [
-        chosen(narrow_product(expert_rows, expert_first[kind]), row_selector) for kind in range(2)
-    ]
-    expert_pre = [
-        narrow_product(expert_rows, expert_gate_up_weight[0, kind])
-        + narrow_product(expert_middle[kind], expert_second[kind])
-        for kind in range(2)
-    ]
+    feed = expert_down_weight.shape[1]
+    expert_joined = jnp.concatenate(
+        [expert_gate_up_weight[0, 0], expert_gate_up_weight[0, 1], expert_first[0], expert_first[1]],
+        axis=1,
+    )
+    expert_up = block_diagonal([expert_second[0], expert_second[1]])
+    expert_pre = narrow_product(expert_rows, expert_joined)
+    expert_middle = chosen(expert_pre[:, 2 * feed :], twice(row_selector))
+    expert_pre = expert_pre[:, : 2 * feed] + narrow_product(expert_middle, expert_up)
+    expert_pre = (expert_pre[:, :feed], expert_pre[:, feed:])
     expert_hidden = (jax.nn.silu(expert_pre[0]) * expert_pre[1]).astype(half)
     expert_down_middle = chosen(narrow_product(expert_hidden, expert_down_first), row_selector)
     expert_result = (
@@ -440,14 +475,14 @@
         + narrow_product(expert_down_middle, expert_down_second)
     ).astype(half)
 
-    shared_middle = [
-        chosen(narrow_product(second_all, shared_first[kind]), selector) for kind in range(2)
-    ]
-    shared_pre = [
-        narrow_product(second_all, shared_gate_up_weight[kind])
-        + narrow_product(shared_middle[kind], shared_second[kind])
-        for kind in range(2)
-    ]
+    shared_joined = jnp.concatenate(
+        [shared_gate_up_weight[0], shared_gate_up_weight[1], shared_first[0], shared_first[1]], axis=1
+    )
+    shared_up = block_diagonal([shared_second[0], shared_second[1]])
+    shared_pre = narrow_product(second_all, shared_joined)
+    shared_middle = chosen(shared_pre[:, 2 * shared_wide :], twice(selector))
+    shared_pre = shared_pre[:, : 2 * shared_wide] + narrow_product(shared_middle, shared_up)
+    shared_pre = (shared_pre[:, :shared_wide], shared_pre[:, shared_wide:])
     shared_hidden = (jax.nn.silu(shared_pre[0]) * shared_pre[1]).astype(half)
     down_middle = chosen(narrow_product(shared_hidden, down_first), selector)
     shared_part = narrow_product(shared_hidden, shared_down_weight) + narrow_product(
@@ -465,36 +500,28 @@
     row_dot = jnp.sum(upstream_rows * expert_result.astype(jnp.float32), axis=1, keepdims=True)
     gate_dot = jnp.sum(jnp.where(placed, row_dot, 0.0), axis=0)
     expert_upstream = (row_gate * upstream_rows).astype(half)
-    expert_down_inner = chosen(rows_product(expert_upstream, expert_down_second), row_selector)
-    expert_grad_hidden = rows_product(expert_upstream, expert_down_weight[0]) + rows_product(
+    expert_down_joined = jnp.concatenate([expert_down_weight[0], expert_down_second], axis=0)
+    expert_grad_hidden = rows_product(expert_upstream, expert_down_joined)
+    expert_down_inner = chosen(expert_grad_hidden[:, feed:], row_selector)
+    expert_grad_hidden = expert_grad_hidden[:, :feed] + rows_product(
         expert_down_inner, expert_down_first
     )
     expert_grad_pre = gated_back(expert_pre[0], expert_pre[1], expert_grad_hidden)
-    expert_inner = [
-        chosen(rows_product(expert_grad_pre[kind], expert_second[kind]), row_selector)
-        for kind in range(2)
-    ]
-    copy_grad = sum(
-        rows_product(expert_grad_pre[kind], expert_gate_up_weight[0, kind])
-        + rows_product(expert_inner[kind], expert_first[kind])
-        for kind in range(2)
+    expert_inner = chosen(rows_product(expert_grad_pre, expert_up), twice(row_selector))
+    copy_grad = rows_product(
+        jnp.concatenate([expert_grad_pre, expert_inner], axis=1), expert_joined
     ).astype(half)
 
     value_grads = (shared_weight * upstream_wide).astype(half)
-    down_inner = chosen(rows_product(value_grads, down_second), selector)
-    shared_grad_hidden = rows_product(value_grads, shared_down_weight) + rows_product(
-        down_inner, down_first
-    )
+    down_joined = jnp.concatenate([shared_down_weight, down_second], axis=0)
+    shared_grad_hidden = rows_product(value_grads, down_joined)
+    down_inner = chosen(shared_grad_hidden[:, shared_wide:], selector)
+    shared_grad_hidden = shared_grad_hidden[:, :shared_wide] + rows_product(down_inner, down_first)
     shared_grad_pre = gated_back(shared_pre[0], shared_pre[1], shared_grad_hidden)
-    shared_inner = [
-        chosen(rows_product(shared_grad_pre[kind], shared_second[kind]), selector)
-        for kind in range(2)
-    ]
+    shared_inner = chosen(rows_product(shared_grad_pre, shared_up), twice(selector))
     copy_grad, layer_sum = lax.optimization_barrier((copy_grad, layer_sum))
-    second_part = token_product(spread, copy_grad) + sum(
-        rows_product(shared_grad_pre[kind], shared_gate_up_weight[kind])
-        + rows_product(shared_inner[kind], shared_first[kind])
-        for kind in range(2)
+    second_part = token_product(spread, copy_grad) + rows_product(
+        jnp.concatenate([shared_grad_pre, shared_inner], axis=1), shared_joined
     )
     dots = jnp.concatenate(
         [
@@ -529,81 +556,10 @@
         lax.all_gather(residual_grad.astype(half), "expert", axis=0, tiled=True)
     )
 
-    output_inner = rows_product(output_upstream, output_second).astype(half)
-    attended_grad = (
-        (rows_product(output_upstream, output_weight) + rows_product(output_inner, output_first))
-        .astype(half)
-        .reshape(shaped)
-    )
-    row_delta = jnp.transpose(jnp.sum(attended_grad.astype(jnp.float32) * attended, axis=2))
-    prob_grads = jnp.einsum(
-        "qhd,khd->hqk", attended_grad, value_low, preferred_element_type=jnp.float32
-    )
-    score_grad = (probabilities * (prob_grads - row_delta[:, :, None])).astype(half)
-    query_grad = (
-        jnp.einsum("hqk,khd->qhd", score_grad, key_low, preferred_element_type=jnp.float32)
-        * score_scale
-    )
-    key_grad = (
-        jnp.einsum("hqk,qhd->khd", score_grad, query_low, preferred_element_type=jnp.float32)
-        * score_scale
-    )
-    value_grad = jnp.einsum(
-        "hqk,qhd->khd", probabilities_low, attended_grad, preferred_element_type=jnp.float32
-    )
-    pre_grads = [
-        rotate(query_grad, cosine_table, sine_table, -1.0).astype(half).reshape(seq_length, width),
-        rotate(key_grad, cosine_table, sine_table, -1.0).astype(half).reshape(seq_length, width),
-        value_grad.astype(half).reshape(seq_length, width),
-    ]
-    qkv_inner = [rows_product(pre_grads[kind], qkv_second[kind]).astype(half) for kind in range(3)]
-    first_part = sum(
-        rows_product(pre_grads[kind], qkv_weights[kind])
-        + rows_product(qkv_inner[kind], attention_first[kind])
-        for kind in range(3)
-    )
-    first_grad = scatter_rows(group_wide(first_part)).astype(jnp.float32)
-    unused, factor_first = rms_forward(input_rows, attention_norm_gain)
-    tokens_grad = residual_grad + rms_backward(
-        input_rows, factor_first, attention_norm_gain, first_grad
-    )
-    layer_out = (residual_stream + layer_sum.astype(jnp.float32)).astype(half)
-
-    own_router_middle = own_rows(router_middle)
-    router_grad_b = token_product(own_router_middle, logit_grads)
-    spare = -experts % 128
-    summed, owned = reduce_adapters(
-        [slot_wide(token_product(qkv_inner[kind], first_narrow)) for kind in range(3)]
-        + [
-            slot_wide(token_product(output_middle, output_upstream)),
-            token_product(shared_inner[0], second_all),
-            token_product(shared_inner[1], second_all),
-            token_product(down_middle, value_grads),
-            token_product(router_inner, second_own),
-            jnp.pad(router_grad_b, ((0, 0), (0, spare))),
-        ],
-        [slot_wide(token_product(attention_middle[kind], pre_grads[kind])) for kind in range(3)]
-        + [
-            slot_wide(token_product(output_inner, attended_low)),
-            token_product(shared_middle[0], shared_grad_pre[0]),
-            token_product(shared_middle[1], shared_grad_pre[1]),
-            token_product(down_inner, shared_hidden),
-        ],
-        [head_column] * 4 + [owner_index * shared_wide] * 3,
-        [model_width_size] * 4 + [owners * shared_wide] * 3,
-        adapter_slot_index,
-        owner_index,
-        owners,
-    )
-    attn_grad_a = jnp.stack([jnp.transpose(value) for value in summed[:3] + owned[3:4]])
-    attn_grad_b = jnp.stack(owned[:3] + summed[3:4])
-
     wide_grads = jnp.concatenate(
         [
-            token_product(expert_inner[0], expert_rows),
-            token_product(expert_inner[1], expert_rows),
-            token_product(expert_middle[0], expert_grad_pre[0]),
-            token_product(expert_middle[1], expert_grad_pre[1]),
+            *row_blocks(token_product(expert_inner, expert_rows), 2),
+            *diagonal_blocks(token_product(expert_middle, expert_grad_pre), 2),
             token_product(expert_down_inner, expert_hidden),
             token_product(expert_down_middle, expert_upstream),
             jnp.broadcast_to(
@@ -613,12 +569,80 @@
         ],
         axis=1,
     ).astype(half)
+    wide_grads, output_upstream = lax.optimization_barrier((wide_grads, output_upstream))
+
+    output_inner = rows_product(output_upstream, output_second).astype(half)
+    attended_grad = (
+        (rows_product(output_upstream, output_weight) + rows_product(output_inner, output_first))
+        .astype(half)
+        .reshape(shaped)
+    )
+    row_delta = jnp.transpose(jnp.sum(attended_grad.astype(jnp.float32) * attended, axis=2))
+    prob_grads = jnp.einsum(
+        "qhd,khd->hqk", attended_grad, value_low, preferred_element_type=jnp.float32
+    )
+    score_grad = (probabilities * (prob_grads - row_delta[:, :, None])).astype(half)
+    query_grad = (
+        jnp.einsum("hqk,khd->qhd", score_grad, key_low, preferred_element_type=jnp.float32)
+        * score_scale
+    )
+    key_grad = (
+        jnp.einsum("hqk,qhd->khd", score_grad, query_low, preferred_element_type=jnp.float32)
+        * score_scale
+    )
+    value_grad = jnp.einsum(
+        "hqk,qhd->khd", probabilities_low, attended_grad, preferred_element_type=jnp.float32
+    )
+    pre_grads = jnp.concatenate(
+        [
+            rotate(query_grad, cosine_table, sine_table, -1.0).reshape(seq_length, width),
+            rotate(key_grad, cosine_table, sine_table, -1.0).reshape(seq_length, width),
+            value_grad.reshape(seq_length, width),
+        ],
+        axis=1,
+    ).astype(half)
+    qkv_inner = rows_product(pre_grads, qkv_up).astype(half)
+    first_part = rows_product(jnp.concatenate([pre_grads, qkv_inner], axis=1), qkv_joined)
+    first_grad = scatter_rows(group_wide(first_part)).astype(jnp.float32)
+    unused, factor_first = rms_forward(input_rows, attention_norm_gain)
+    tokens_grad = residual_grad + rms_backward(
+        input_rows, factor_first, attention_norm_gain, first_grad
+    )
+    layer_out = (residual_stream + layer_sum.astype(jnp.float32)).astype(half)
+
+    own_router_middle = own_rows(router_middle)
+    router_grad_b = token_product(own_router_middle, logit_grads)
+    spare = -experts % 128
+    summed, owned = reduce_adapters(
+        [slot_wide(value) for value in row_blocks(token_product(qkv_inner, first_narrow), 3)]
+        + [slot_wide(token_product(output_middle, output_upstream))]
+        + row_blocks(token_product(shared_inner, second_all), 2)
+        + [
+            token_product(down_middle, value_grads),
+            token_product(router_inner, second_own),
+            jnp.pad(router_grad_b, ((0, 0), (0, spare))),
+        ],
+        [
+            slot_wide(value)
+            for value in diagonal_blocks(token_product(attention_middle, pre_grads), 3)
+        ]
+        + [slot_wide(token_product(output_inner, attended_low))]
+        + diagonal_blocks(token_product(shared_middle, shared_grad_pre), 2)
+        + [token_product(down_inner, shared_hidden)],
+        [head_column] * 4 + [owner_index * shared_wide] * 3,
+        [model_width_size] * 4 + [owners * shared_wide] * 3,
+        adapter_slot_index,
+        owner_index,
+        owners,
+    )
+    attn_grad_a = jnp.stack([jnp.transpose(value) for value in summed[:3] + owned[3:4]])
+    attn_grad_b = jnp.stack(owned[:3] + summed[3:4])
+
     expert_grads = lax.all_gather(wide_grads, "dp", axis=0, tiled=True)
     rank_range = jnp.arange(ADAPTER_COUNT * ADAPTER_RANK, dtype=jnp.int32)
     source_rank = jnp.arange(expert_grads.shape[0], dtype=jnp.int32)
     source_place = expert_grads[:, -1].astype(jnp.int32) * ADAPTER_RANK + source_rank % ADAPTER_RANK
     placement = (source_place[:, None] == rank_range[None, :]).astype(half)
-    feed = expert_down_weight.shape[1]
     bounds = [0, model_width_size, 2 * model_width_size]
     bounds += [bounds[-1] + feed, bounds[-1] + 2 * feed, bounds[-1] + 3 * feed]
     expert_pieces = [

time: 709 us -> 641 us (0.904)
  matrix products: 287 us -> 197 us
  local copies, waits for them, and re-layouts: 30.1 us -> 97.8 us
  waiting for transfers between devices: 249 us -> 215 us
  blocking collectives: 42 us -> 27.1 us
    dot_general x33 -> x16, matrix products: 134 us -> 63.6 us  [rows_product(): lax.dot_general(left_side, right_side, (((1,), (1,)), ((), ())), preferre...]
    all_gather x1, waiting for transfers between devices: 44.6 us -> 3.07 us  [on_device(): second_all = lax.all_gather(second_own, 'expert', axis=0, tiled=True)]
    reduce_scatter x4, waiting for transfers between devices: 114 us -> 152 us  [scatter_rows(): lax.psum_scatter(values.astype(half), 'expert', scatter_dimension=0, tile...]
    all_gather x1, waiting for transfers between devices: 27.6 us -> 0.01 us  [on_device(): upstream_all = lax.all_gather(cotangent, 'expert', axis=0, tiled=True)]
    squeeze x0 -> x11, local copies, waits for them, and re-layouts: none -> 26.7 us  [the longest x1 9.71 us: on_device(): expert_gate_up_weight[0, 1]]
    concatenate x1 -> x3, local copies, waits for them, and re-layouts: 0.59 us -> 25.6 us  [the longest x1 18.9 us: on_device(): jnp.concatenate([expert_gate_up_weight[0, 0], expert_gate_up_weight[0, 1]...]
    all_gather x1, waiting for transfers between devices: 34.6 us -> 15.2 us  [on_device(): lax.all_gather(residual_grad.astype(half), 'expert', axis=0, tiled=True)]
    dot_general x36 -> x19, matrix products: 80.4 us -> 61.8 us  [narrow_product(): return jnp.dot(left_side, right_side, preferred_element_type=jnp.float32)]
  transfers between devices with their start and end apart: 19 -> 19, of which waited for: 10 -> 11; matrix products, arithmetic and copies ran while one was open for 27% -> 35% of each run, Pallas kernels for 0% -> 0%
where the time goes in v3:
time: 641 us; the launch traced here: 631 us
  waiting for transfers between devices  215 us (34%)
  matrix products  197 us (31%)
  local copies, waits for them, and re-layouts  97.8 us (15%)
  other arithmetic  54.3 us (8%)
  blocking collectives  27.1 us (4%)
  starting transfers between devices  22.7 us (4%)
  between operations  17.6 us (3%)
    reduce_scatter x4, waiting for transfers between devices, scatter_rows(): lax.psum_scatter(values.astype(half), 'expert', scatter_dimension=0, tile...  152 us
    dot_general x16, matrix products, rows_product(): lax.dot_general(left_side, right_side, (((1,), (1,)), ((), ())), preferre...  63.6 us
    dot_general x19, matrix products, narrow_product(): return jnp.dot(left_side, right_side, preferred_element_type=jnp.float32)  61.8 us
    dot_general x22, matrix products, token_product(): lax.dot_general(left_side, right_side, (((0,), (0,)), ((), ())), preferre...  47.8 us
    unnamed x243, local copies, waits for them, and re-layouts  19.3 us
    concatenate x1, local copies, waits for them, and re-layouts, on_device(): jnp.concatenate([expert_gate_up_weight[0, 0], expert_gate_up_weight[0, 1]...  18.9 us
    all_gather x1, waiting for transfers between devices, on_device(): lax.all_gather(residual_grad.astype(half), 'expert', axis=0, tiled=True)  15.2 us
    all_gather x1, blocking collectives, on_device(): routes_all = lax.all_gather(routes, 'expert', axis=0, tiled=True)  13.8 us
  transfers between devices with their start and end apart: 19, of which 11 were waited for; matrix products, arithmetic and copies ran while one was open for 35% of the time, Pallas kernels for 0%

profile of v3, /device:TPU:11, one launch (start us, length us, event | category | flops | bytes accessed | tf_op | source)
XLA Modules:
  0.0 631.5 jit_solution(7234625929715453042)
XLA Ops:
  25.6 11.5 %collective-permute-done = bf16[512,256]{1,0:T(8,128)(2,1)S(1)} collective-permute-done((bf16[512,256]{1,0:T(8,128)(2,1)S(1)}, bf16[512,256]{1,0:T(8,128)(2,1)S(1)}, u32[]{:S(2)}, u32[]{:S(2)}) %collective-permute-start) | collective-permute-done | bytes 262176 | tf_op jit(solution)/shard_map/ppermute | solution.py:120
  40.8 13.8 %all_gather.25 = s32[1024,4]{0,1:T(4,128)S(1)} all-gather(s32[128,4]{0,1:T(4,128)} %param.39), channel_id=1, replica_groups=mesh['dp'=4,'expert'=8] {'expert'}, dimensions={0}, use_global_device_ids=true | all-gather | bytes 18432 | tf_op jit(solution)/shard_map/all_gather | solution.py:345
  63.4 10.6 %collective-permute-done.4 = bf16[3,512,256]{2,1,0:T(8,128)(2,1)} collective-permute-done((bf16[3,512,256]{2,1,0:T(8,128)(2,1)}, bf16[3,512,256]{2,1,0:T(8,128)(2,1)}, u32[]{:S(2)}, u32[]{:S(2)}) %collective-permute-start.4) | collective-permute-done | bytes 786464 | tf_op jit(solution)/shard_map/ppermute | solution.py:137
  78.2 6.7 %concatenate.142 = bf16[2048,816]{1,0:T(8,128)(2,1)} concatenate(bf16[2048,256]{1,0:T(8,128)(2,1)} %get-tuple-element.57, bf16[2048,256]{1,0:T(8,128)(2,1)} %get-tuple-element.56, bf16[2048,256]{1,0:T(8,128)(2,1)S(1)} %get-tuple-element.55, bf16[2048,16]{1,0:T(8,128)(2,1)} %get-tuple-element.76, bf16[2048,16]{1,0:T(8,128)(2,1)} %get-tuple-element.75, ...), dimensions={1} | concatenate | bytes 6684672 | tf_op jit(solution)/shard_map/concatenate | solution.py:413
  88.5 6.1 fusion.63
  110.6 10.8 %fusion.192 = (f32[2,1024]{1,0:T(2,128)S(1)}, f32[2,1024,1024]{1,2,0:T(8,128)}) fusion(f32[1024,1024]{0,1:T(8,128)} %get-tuple-element.135, pred[1024,1024]{0,1:T(8,128)(4,1)} %get-tuple-element.134, bf16[1024,2,64]{2,0,1:T(8,128)(2,1)} %get-tuple-element.83, bf16[1024,2,64]{2,0,1:T(8,128)(2,1)} %get-tuple-element.84, ...), kind=kOutput, calls=%fused_computation.413 | convolution fusion | flops 549454848 | bytes 14688256 | tf_op jit(solution)/shard_map/sub | solution.py:430
  137.5 46.8 %reduce-scatter.6.cloned.1.call-done = bf16[128,2048]{1,0:T(8,128)(2,1)} async-done(((bf16[1024,2048]{1,0:T(8,128)(2,1)}), bf16[128,2048]{1,0:T(8,128)(2,1)}) %reduce-scatter.6.cloned.1.call-update) | async-done | bytes 524304 | tf_op jit(solution)/shard_map/reduce_scatter | solution.py:339
  192.2 9.7 %slice_bitcast_fusion = (bf16[2048,1408]{1,0:T(8,128)(2,1)}, bf16[2048,1408]{1,0:T(8,128)(2,1)}) fusion(bf16[1,2,2048,1408]{3,2,1,0:T(8,128)(2,1)} %param.37), kind=kLoop, calls=%fused_computation.26 | loop fusion | bytes 23068672 | tf_op jit(solution)/shard_map/squeeze | solution.py:463
  201.9 18.9 %concatenate.151 = bf16[2048,2848]{1,0:T(8,128)(2,1)} concatenate(bf16[2048,1408]{1,0:T(8,128)(2,1)} %get-tuple-element.41, bf16[2048,1408]{1,0:T(8,128)(2,1)} %get-tuple-element.40, bf16[2048,16]{1,0:T(8,128)(2,1)S(1)} %get-tuple-element.90, bf16[2048,16]{1,0:T(8,128)(2,1)S(1)} %get-tuple-element.89), dimensions={1} | concatenate | bytes 23330816 | tf_op jit(solution)/shard_map/concatenate | solution.py:462
  224.2 6.2 slice_bitcast_fusion.3
  237.8 11.5 %fusion.80 = f32[1024,1440]{0,1:T(8,128)} fusion(bf16[1024,2048]{1,0:T(8,128)(2,1)S(1)} %copy-done.7, bf16[2048,16]{0,1:T(8,128)(2,1)S(1)} %copy.161, bf16[2048,16]{0,1:T(8,128)(2,1)S(1)} %copy.160, bf16[2048,704]{0,1:T(8,128)(2,1)} %get-tuple-element.48, bf16[2048,704]{0,1:T(8,128)(2,1)} %get-tuple-element.47), kind=kOutput, calls=%fused_computation.175 | convolution fusion | flops 6063390720 | bytes 15990784 | tf_op jit(solution)/shard_map/dot_general | solution.py:22
  271.5 7.5 %fusion.196 = f32[576,2848]{1,0:T(8,128)S(1)} fusion(bf16[576,2048]{1,0:T(8,128)(2,1)S(1)} %convolution_convert_fusion.2, bf16[2048,2848]{1,0:T(8,128)(2,1)S(1)} %bitcast.263), kind=kOutput, calls=%fused_computation.417 | convolution fusion | flops 6719275008 | bytes 20586496 | tf_op jit(solution)/shard_map/dot_general | solution.py:22
  305.4 8.0 %fusion.7 = f32[576,1424]{1,0:T(8,128)S(1)} fusion(bf16[16,2048]{1,0:T(8,128)(2,1)S(1)} %dynamic-slice_bitcast_fusion.13, bf16[1408,2048]{1,0:T(8,128)(2,1)} %bitcast.305, f32[576,2048]{1,0:T(8,128)} %get-tuple-element.148, f32[576]{0:T(1024)S(1)} %get-tuple-element.37), kind=kOutput, calls=%fused_computation.21 | convolution fusion | flops 3373662208 | bytes 13834496 | tf_op jit(solution)/shard_map/dot_general | solution.py:60
  318.0 12.7 %fusion.23 = bf16[576,2048]{1,0:T(8,128)(2,1)} fusion(bf16[2048,2848]{1,0:T(8,128)(2,1)} %concatenate.151, bf16[576,32]{1,0:T(8,128)(2,1)S(1)} %fusion.73, bf16[576,1408]{1,0:T(8,128)(2,1)} %copy-done.99, bf16[576,1408]{1,0:T(8,128)(2,1)} %copy-done.98), kind=kOutput, calls=%fused_computation.56 | convolution fusion | flops 6730297344 | bytes 17305600 | tf_op jit(solution)/shard_map/dot_general | solution.py:60
  332.8 21.0 %reduce-scatter.8.cloned.1.call-done = bf16[128,2048]{1,0:T(8,128)(2,1)} async-done(((bf16[1024,2048]{1,0:T(8,128)(2,1)}), bf16[128,2048]{1,0:T(8,128)(2,1)}) %reduce-scatter.8.cloned.1.call-update) | async-done | bytes 524304 | tf_op jit(solution)/shard_map/reduce_scatter | solution.py:339
  353.8 7.5 %fusion.40 = f32[1024,2048]{1,0:T(8,128)} fusion(bf16[576,2048]{1,0:T(8,128)(2,1)} %fusion.23, s32[1024]{0:T(1024)S(1)} %add_bitcast_fusion, pred[1024]{0:T(1024)(128)(4,1)S(1)} %compare_reduce_fusion), kind=kOutput, calls=%fused_computation.90 | convolution fusion | flops 2417098752 | bytes 10753024 | tf_op jit(solution)/shard_map/dot_general | solution.py:66
  361.3 11.5 %add_convert_fusion = bf16[1024,2048]{1,0:T(8,128)(2,1)} fusion(f32[1024,2048]{1,0:T(8,128)} %fusion.40, bf16[1024,32]{0,1:T(8,128)(2,1)S(1)} %fusion.74, bf16[1024,704]{0,1:T(8,128)(2,1)} %get-tuple-element.45, bf16[1024,704]{0,1:T(8,128)(2,1)} %get-tuple-element.44, bf16[2048,16]{0,1:T(8,128)(2,1)S(1)} %copy.161, bf16[2048,16]{0,1:T(8,128)(2,1)S(1)} %copy.160, ...), kind=kOutput, calls=%fused_computation.11 | convolution fusion | flops 6076432384 | bytes 21430272 | tf_op jit(solution)/shard_map/dot_general | solution.py:60
  373.6 6.6 %reduce-scatter.12.cloned.1.call-done = f32[16,128]{1,0:T(8,128)} async-done(((f32[16,1024]{1,0:T(8,128)}), f32[16,128]{1,0:T(8,128)}) %reduce-scatter.12.cloned.1.call-update) | async-done | bytes 8208 | tf_op jit(solution)/shard_map/reduce_scatter | solution.py:534
  382.4 53.4 %reduce-scatter.10.cloned.1.call-done = bf16[128,2048]{1,0:T(8,128)(2,1)} async-done(((bf16[1024,2048]{1,0:T(8,128)(2,1)}), bf16[128,2048]{1,0:T(8,128)(2,1)}) %reduce-scatter.10.cloned.1.call-update) | async-done | bytes 524304 | tf_op jit(solution)/shard_map/reduce_scatter | solution.py:339
  470.4 15.2 %all-gather.14.cloned.1.call-done = bf16[1024,2048]{1,0:T(8,128)(2,1)} async-done(((bf16[128,2048]{1,0:T(8,128)(2,1)}), bf16[1024,2048]{1,0:T(8,128)(2,1)}) %all-gather.14.cloned.1.call-update) | async-done | bytes 4194320 | tf_op jit(solution)/shard_map/all_gather | solution.py:556
  524.8 13.3 %all-to-all-done = bf16[8,2,19648]{2,1,0:T(2,128)(2,1)S(1)} async-done(((bf16[8,2,19648]{2,1,0:T(2,128)(2,1)}), bf16[8,2,19648]{2,1,0:T(2,128)(2,1)S(1)}, u32[]{:S(2)}, u32[]{:S(2)}) %all-to-all-start) | async-done | bytes 628768 | tf_op jit(solution)/shard_map/all_to_all | solution.py:203
  540.9 13.4 %all-gather.1 = bf16[4,2,41728]{2,1,0:T(2,128)(2,1)S(1)} all-gather(bf16[1,2,41728]{2,1,0:T(2,128)(2,1)S(1)} %bitcast.286), channel_id=2, replica_groups=mesh['dp'=4,'expert'=8] {'dp'}, dimensions={0}, use_global_device_ids=true | all-gather | bytes 834560 | tf_op jit(solution)/shard_map/all_gather | solution.py:216
  563.4 6.3 convolution_convert_fusion
  588.7 31.1 %reduce-scatter.14.cloned.1.call-done = bf16[128,2048]{1,0:T(8,128)(2,1)} async-done(((bf16[1024,2048]{1,0:T(8,128)(2,1)}), bf16[128,2048]{1,0:T(8,128)(2,1)}) %reduce-scatter.14.cloned.1.call-update) | async-done | bytes 524304 | tf_op jit(solution)/shard_map/reduce_scatter | solution.py:339
  (458 shorter events, 253.9 us)
Async XLA Ops:
  7.2 251.3 %copy-start = (bf16[5632,128]{1,0:T(8,128)(2,1)S(1)}, bf16[5632,128]{1,0:T(8,128)(2,1)}, u32[]{:S(2)}) copy-start(bf16[5632,128]{1,0:T(8,128)(2,1)} %param.48) | copy-start | bytes 4325380
  7.2 77.8 %all-gather.8.cloned.1.call-start = ((), (), s32[]{:S(2)}) async-start(), calls=%async_computation.6 | async-start | bytes 4718592 | tf_op jit(solution)/shard_map/all_gather | solution.py:341
  7.9 122.3 %all-gather.10.cloned.1.call-start = ((), (), s32[]{:S(2)}) async-start(), calls=%async_computation.7 | async-start | bytes 4718592 | tf_op jit(solution)/shard_map/all_gather | solution.py:347
  9.2 14.5 %collective-permute-start.2 = (bf16[512,256]{1,0:T(8,128)(2,1)S(1)}, bf16[512,256]{1,0:T(8,128)(2,1)S(1)}, u32[]{:S(2)}, u32[]{:S(2)}) collective-permute-start(bf16[512,256]{1,0:T(8,128)(2,1)S(1)} %get-tuple-element.64), channel_id=1, source_target_pairs={{0,2},{1,5},{2,0},{3,3},{4,6},{5,1},{6,4},{7,7},{8,10},{9,13},{10,... | collective-permute-start | bytes 786440 | tf_op jit(solution)/shard_map/ppermute | solution.py:120
  9.8 15.7 %collective-permute-start.1 = (bf16[512,256]{1,0:T(8,128)(2,1)S(1)}, bf16[512,256]{1,0:T(8,128)(2,1)S(1)}, u32[]{:S(2)}, u32[]{:S(2)}) collective-permute-start(bf16[512,256]{1,0:T(8,128)(2,1)S(1)} %get-tuple-element.63), channel_id=1, source_target_pairs={{0,1},{1,4},{2,7},{3,2},{4,5},{5,0},{6,3},{7,6},{8,9},{9,12},{10,1... | collective-permute-start | bytes 786440 | tf_op jit(solution)/shard_map/ppermute | solution.py:120
  12.3 24.8 %collective-permute-start = (bf16[512,256]{1,0:T(8,128)(2,1)S(1)}, bf16[512,256]{1,0:T(8,128)(2,1)S(1)}, u32[]{:S(2)}, u32[]{:S(2)}) collective-permute-start(bf16[512,256]{1,0:T(8,128)(2,1)S(1)} %get-tuple-element.62), channel_id=1, source_target_pairs={{0,0},{1,3},{2,6},{3,1},{4,4},{5,7},{6,2},{7,5},{8,8},{9,11},{10,1... | collective-permute-start | bytes 786440 | tf_op jit(solution)/shard_map/ppermute | solution.py:120
  17.7 166.7 %reduce-scatter.6.cloned.1.call-start = ((), (), s32[]{:S(2)}) async-start(), calls=%async_computation.8 | async-start | bytes 4718592 | tf_op jit(solution)/shard_map/reduce_scatter | solution.py:339
  38.2 25.3 %collective-permute-start.5 = (bf16[3,512,256]{2,1,0:T(8,128)(2,1)}, bf16[3,512,256]{2,1,0:T(8,128)(2,1)}, u32[]{:S(2)}, u32[]{:S(2)}) collective-permute-start(bf16[3,512,256]{2,1,0:T(8,128)(2,1)} %get-tuple-element.92), channel_id=1, source_target_pairs={{0,24},{8,16},{16,8},{24,0},{1,25},{9,17},{17,9},{25,1},{2,26},{10... | collective-permute-start | bytes 2359304 | tf_op jit(solution)/shard_map/ppermute | solution.py:137
  39.4 34.6 %collective-permute-start.4 = (bf16[3,512,256]{2,1,0:T(8,128)(2,1)}, bf16[3,512,256]{2,1,0:T(8,128)(2,1)}, u32[]{:S(2)}, u32[]{:S(2)}) collective-permute-start(bf16[3,512,256]{2,1,0:T(8,128)(2,1)} %get-tuple-element.92), channel_id=1, source_target_pairs={{0,16},{8,24},{16,0},{24,8},{1,17},{9,25},{17,1},{25,9},{2,18},{10... | collective-permute-start | bytes 2359304 | tf_op jit(solution)/shard_map/ppermute | solution.py:137
  39.9 34.1 %collective-permute-start.3 = (bf16[3,512,256]{2,1,0:T(8,128)(2,1)}, bf16[3,512,256]{2,1,0:T(8,128)(2,1)}, u32[]{:S(2)}, u32[]{:S(2)}) collective-permute-start(bf16[3,512,256]{2,1,0:T(8,128)(2,1)} %get-tuple-element.92), channel_id=1, source_target_pairs={{0,8},{8,0},{16,24},{24,16},{1,9},{9,1},{17,25},{25,17},{2,10},{10... | collective-permute-start | bytes 2359304 | tf_op jit(solution)/shard_map/ppermute | solution.py:137
  137.4 96.7 %all-gather.12.cloned.1.call-start = ((), (), s32[]{:S(2)}) async-start(), calls=%async_computation.9 | async-start | bytes 4718592 | tf_op jit(solution)/shard_map/all_gather | solution.py:446
  188.2 165.6 %reduce-scatter.8.cloned.1.call-start = ((), (), s32[]{:S(2)}) async-start(), calls=%async_computation.10 | async-start | bytes 4718592 | tf_op jit(solution)/shard_map/reduce_scatter | solution.py:339
  305.3 74.8 %reduce-scatter.12.cloned.1.call-start = ((), (), s32[]{:S(2)}) async-start(), calls=%async_computation.12 | async-start | bytes 73728 | tf_op jit(solution)/shard_map/reduce_scatter | solution.py:534
  330.7 105.1 %reduce-scatter.10.cloned.1.call-start = ((), (), s32[]{:S(2)}) async-start(), calls=%async_computation.11 | async-start | bytes 4718592 | tf_op jit(solution)/shard_map/reduce_scatter | solution.py:339
  372.9 64.4 %copy-start.22 = (bf16[2048,16]{1,0:T(8,128)(2,1)S(1)}, bf16[2048,16]{1,0:T(8,128)(2,1)}, u32[]{:S(2)}) copy-start(bf16[2048,16]{1,0:T(8,128)(2,1)} %copy-done.21) | copy-start | bytes 196612
  372.9 65.5 %copy-start.20 = (bf16[128,2048]{1,0:T(8,128)(2,1)S(1)}, bf16[128,2048]{1,0:T(8,128)(2,1)}, u32[]{:S(2)}) copy-start(bf16[128,2048]{1,0:T(8,128)(2,1)} %param.28) | copy-start | bytes 1572868
  372.9 65.5 %copy-start.87 = (f32[128]{0:T(128)S(1)}, f32[128]{0:T(128)}, u32[]{:S(2)}) copy-start(f32[128]{0:T(128)} %copy-done.86) | copy-start | bytes 1540
  372.9 65.5 %copy-start.92 = (f32[128]{0:T(128)S(1)}, f32[128]{0:T(128)}, u32[]{:S(2)}) copy-start(f32[128]{0:T(128)} %get-tuple-element.141) | copy-start | bytes 1540
  372.9 112.7 %all-gather.14.cloned.1.call-start = ((), (), s32[]{:S(2)}) async-start(), calls=%async_computation.13 | async-start | bytes 4718592 | tf_op jit(solution)/shard_map/all_gather | solution.py:556
  519.0 19.1 %all-to-all-start = ((bf16[8,2,19648]{2,1,0:T(2,128)(2,1)}), bf16[8,2,19648]{2,1,0:T(2,128)(2,1)S(1)}, u32[]{:S(2)}, u32[]{:S(2)}) async-start(bf16[8,2,19648]{2,1,0:T(2,128)(2,1)} %concatenate.186), calls=%async_computation.5 | async-start | bytes 1261568 | tf_op jit(solution)/shard_map/all_to_all | solution.py:203
  524.0 51.4 %all-gather.16.cloned.1.call-start = ((), (), s32[]{:S(2)}) async-start(), calls=%async_computation.15 | async-start | bytes 1679360 | tf_op jit(solution)/shard_map/all_gather | solution.py:641
  524.8 95.0 %reduce-scatter.14.cloned.1.call-start = ((), (), s32[]{:S(2)}) async-start(), calls=%async_computation.14 | async-start | bytes 4718592 | tf_op jit(solution)/shard_map/reduce_scatter | solution.py:339
  557.4 12.3 %collective-permute-start.7 = (bf16[2,41600]{1,0:T(2,128)(2,1)S(1)}, bf16[2,41600]{1,0:T(2,128)(2,1)S(1)}, u32[]{:S(2)}, u32[]{:S(2)}) collective-permute-start(bf16[2,41600]{1,0:T(2,128)(2,1)S(1)} %get-tuple-element.123), channel_id=1, source_target_pairs={{0,4},{1,0},{2,5},{3,1},{4,6},{5,2},{6,7},{7,3},{8,12},{9,8},{10,1... | collective-permute-start | bytes 499208 | tf_op jit(solution)/shard_map/ppermute | solution.py:230
  560.1 9.6 %collective-permute-start.6 = (bf16[2,41600]{1,0:T(2,128)(2,1)S(1)}, bf16[2,41600]{1,0:T(2,128)(2,1)S(1)}, u32[]{:S(2)}, u32[]{:S(2)}) collective-permute-start(bf16[2,41600]{1,0:T(2,128)(2,1)S(1)} %get-tuple-element.122), channel_id=1, source_target_pairs={{0,0},{1,4},{2,1},{3,5},{4,2},{5,6},{6,3},{7,7},{8,8},{9,12},{10,9... | collective-permute-start | bytes 499208 | tf_op jit(solution)/shard_map/ppermute | solution.py:230
  (107 other events, 1183.7 us)
Sparse Core Ops, SparseCore 0:
  9.6 52.2 all-gather.7
  63.5 45.9 all-gather.9
  137.6 46.7 reduce-scatter.5
  188.3 45.7 all-gather.11
  305.4 48.3 reduce-scatter.7
  356.4 23.6 reduce-scatter.11
  382.4 53.4 reduce-scatter.9
  439.8 45.7 all-gather.13
  527.3 31.9 all-gather.15
  569.8 49.8 reduce-scatter.13

commit v4 on v3

--- a/solution.py
+++ b/solution.py
@@ -1,8 +1,11 @@
+import functools
 import math
 
 import jax
 import jax.numpy as jnp
 from jax import lax
+from jax.experimental import pallas as pl
+from jax.experimental.pallas import tpu as pltpu
 from jax.sharding import PartitionSpec as P
 
 HEADS = 16
@@ -41,19 +44,123 @@
     return (jnp.cos(angles), jnp.sin(angles))
 
 
-def rotate(values, cosine_table, sine_table, direction):
-    half_width = values.shape[-1] // 2
-    first_half = values[..., :half_width]
-    second_half = values[..., half_width:]
-    cosine_part = cosine_table[:, None, :]
-    sine_part = sine_table[:, None, :] * direction
-    return jnp.concatenate(
-        [
-            first_half * cosine_part - second_half * sine_part,
-            second_half * cosine_part + first_half * sine_part,
+def turn(values, cosine_table, sine_table):
+    return values * cosine_table + pltpu.roll(values, HEAD_DIM // 2, 1) * sine_table
+
+
+def head_product(left_side, right_side, left_dim, right_dim):
+    return lax.dot_general(
+        left_side,
+        right_side,
+        (((left_dim,), (right_dim,)), ((), ())),
+        preferred_element_type=jnp.float32,
+    )
+
+
+def block_probabilities(query_rows, key_rows, live, score_scale):
+    scores = head_product(query_rows, key_rows, 1, 1) * score_scale
+    scores = jnp.where(live, scores, MASKED)
+    exponents = jnp.exp(scores - jnp.max(scores, axis=1, keepdims=True))
+    return exponents / jnp.sum(exponents, axis=1, keepdims=True)
+
+
+def attention_forward(
+    score_scale, length_ref, q_ref, k_ref, v_ref, cos_ref, sin_ref, out_ref, ql_ref, kl_ref, vl_ref
+):
+    rows = q_ref.shape[0]
+    cosine_table, sine_table = cos_ref[...], sin_ref[...]
+    ql_ref[...] = turn(q_ref[...], cosine_table, sine_table).astype(jnp.bfloat16)
+    kl_ref[...] = turn(k_ref[...], cosine_table, sine_table).astype(jnp.bfloat16)
+    vl_ref[...] = v_ref[...].astype(jnp.bfloat16)
+    for start in range(0, rows, BLOCK):
+        stop = start + BLOCK
+        live = lax.broadcasted_iota(jnp.int32, (BLOCK, stop), 1) < length_ref[0]
+        probabilities = block_probabilities(
+            ql_ref[start:stop, :], kl_ref[:stop, :], live, score_scale
+        )
+        out_ref[start:stop, :] = head_product(
+            probabilities.astype(jnp.bfloat16), vl_ref[:stop, :], 1, 0
+        ).astype(jnp.bfloat16)
+
+
+def attention_backward(
+    score_scale,
+    length_ref,
+    q_ref,
+    k_ref,
+    v_ref,
+    grad_ref,
+    cos_ref,
+    sin_ref,
+    dq_ref,
+    dk_ref,
+    dv_ref,
+    key_sum,
+    value_sum,
+):
+    rows = q_ref.shape[0]
+    cosine_table, sine_table = cos_ref[...], sin_ref[...]
+    key_sum[...] = jnp.zeros_like(key_sum)
+    value_sum[...] = jnp.zeros_like(value_sum)
+    for start in range(0, rows, BLOCK):
+        stop = start + BLOCK
+        live = lax.broadcasted_iota(jnp.int32, (BLOCK, stop), 1) < length_ref[0]
+        query_rows, grad_rows = q_ref[start:stop, :], grad_ref[start:stop, :]
+        probabilities = block_probabilities(query_rows, k_ref[:stop, :], live, score_scale)
+        narrow = probabilities.astype(jnp.bfloat16)
+        prob_grads = head_product(grad_rows, v_ref[:stop, :], 1, 1)
+        delta = jnp.sum(narrow.astype(jnp.float32) * prob_grads, axis=1, keepdims=True)
+        score_grads = (probabilities * (prob_grads - delta)).astype(jnp.bfloat16)
+        query_grads = head_product(score_grads, k_ref[:stop, :], 1, 0) * score_scale
+        dq_ref[start:stop, :] = turn(
+            query_grads, cosine_table[start:stop, :], -sine_table[start:stop, :]
+        ).astype(jnp.bfloat16)
+        key_sum[:stop, :] += head_product(score_grads, query_rows, 0, 0)
+        value_sum[:stop, :] += head_product(narrow, grad_rows, 0, 0)
+    dk_ref[...] = turn(key_sum[...] * score_scale, cosine_table, -sine_table).astype(jnp.bfloat16)
+    dv_ref[...] = value_sum[...].astype(jnp.bfloat16)
+
+
+def head_attention(query, key, value, length, cosine_table, sine_table, score_scale):
+    rows, width = query.shape
+    head = pl.BlockSpec((rows, HEAD_DIM), lambda place: (0, place))
+    table = pl.BlockSpec((rows, HEAD_DIM), lambda place: (0, 0))
+    shape = jax.ShapeDtypeStruct((rows, width), jnp.bfloat16)
+    return pl.pallas_call(
+        functools.partial(attention_forward, score_scale),
+        grid=(width // HEAD_DIM,),
+        in_specs=[pl.BlockSpec(memory_space=pltpu.SMEM), head, head, head, table, table],
+        out_specs=[head] * 4,
+        out_shape=[shape] * 4,
+        compiler_params=pltpu.CompilerParams(vmem_limit_bytes=48 * 1024 * 1024),
+        cost_estimate=pl.CostEstimate(
+            flops=3 * rows * rows * width, bytes_accessed=24 * rows * width, transcendentals=rows * rows
+        ),
+        name="head_attention",
+    )(length, query, key, value, cosine_table, sine_table)
+
+
+def head_attention_back(query, key, value, grad, length, cosine_table, sine_table, score_scale):
+    rows, width = query.shape
+    head = pl.BlockSpec((rows, HEAD_DIM), lambda place: (0, place))
+    table = pl.BlockSpec((rows, HEAD_DIM), lambda place: (0, 0))
+    shape = jax.ShapeDtypeStruct((rows, width), jnp.bfloat16)
+    return pl.pallas_call(
+        functools.partial(attention_backward, score_scale),
+        grid=(width // HEAD_DIM,),
+        in_specs=[pl.BlockSpec(memory_space=pltpu.SMEM)] + [head] * 4 + [table, table],
+        out_specs=[head] * 3,
+        out_shape=[shape] * 3,
+        scratch_shapes=[
+            pltpu.VMEM((rows, HEAD_DIM), jnp.float32),
+            pltpu.VMEM((rows, HEAD_DIM), jnp.float32),
         ],
-        axis=-1,
-    )
+        compiler_params=pltpu.CompilerParams(vmem_limit_bytes=48 * 1024 * 1024),
+        cost_estimate=pl.CostEstimate(
+            flops=7 * rows * rows * width, bytes_accessed=16 * rows * width, transcendentals=rows * rows
+        ),
+        name="head_attention_back",
+    )(length, query, key, value, grad, cosine_table, sine_table)
 
 
 def rows_product(left_side, right_side):
@@ -165,7 +272,7 @@
 
 
 def reduce_adapters(
-    partial, owned, owned_starts, owned_totals, adapter_index, owner_index, owners
+    partial, owned, owned_starts, owned_totals, adapter_index, owner_index, owners, ahead
 ):
     groups = lax.axis_size("dp")
     group_index = lax.axis_index("dp")
@@ -194,12 +301,13 @@
         dense = spread_adapters(jnp.concatenate([partial_all] + wide, axis=1), adapter_index)
         summed = lax.psum_scatter(dense, ("dp", "expert"), scatter_dimension=0, tiled=True)
         pieces = cut(summed, partial_sizes + owned_totals)
-        return pieces[: len(partial)], pieces[len(partial) :]
+        return pieces[: len(partial)], pieces[len(partial) :], ahead
 
     local = ADAPTER_COUNT // groups
     own_rows = ADAPTER_RANK // owners
     held = sum(partial_sizes)
     joined = jnp.concatenate([partial_all, owned_all], axis=1).astype(jnp.bfloat16)
+    joined, ahead = lax.optimization_barrier((joined, ahead))
     moved = lax.all_to_all(
         joined.reshape(owners, own_rows, joined.shape[1]),
         "expert",
@@ -246,7 +354,7 @@
         axis=0,
     )
     pieces = cut(rows.astype(jnp.float32), partial_sizes + [owners * size for size in owned_sizes])
-    return pieces[: len(partial)], pieces[len(partial) :]
+    return pieces[: len(partial)], pieces[len(partial) :], ahead
 
 
 def on_device(
@@ -409,31 +517,18 @@
     first_narrow = normed_first.astype(half)
     positions = jnp.arange(seq_length, dtype=jnp.int32)
     cosine_table, sine_table = rope_tables(positions, HEAD_DIM)
-    shaped = (seq_length, head_count, HEAD_DIM)
+    cosine_table = jnp.concatenate([cosine_table, cosine_table], axis=1)
+    sine_table = jnp.concatenate([-sine_table, sine_table], axis=1)
+    length = slot_value(lengths).reshape(1)
     qkv_joined = jnp.concatenate(qkv_weights + [attention_first[kind] for kind in range(3)], axis=1)
     qkv_up = block_diagonal([qkv_second[kind] for kind in range(3)])
     projected = narrow_product(first_narrow, qkv_joined)
     attention_middle = projected[:, 3 * width :].astype(half)
     projected = projected[:, : 3 * width] + narrow_product(attention_middle, qkv_up)
     projected = [projected[:, kind * width : (kind + 1) * width] for kind in range(3)]
-    query_low = rotate(projected[0].reshape(shaped), cosine_table, sine_table, 1.0).astype(half)
-    key_low = rotate(projected[1].reshape(shaped), cosine_table, sine_table, 1.0).astype(half)
-    value_low = projected[2].reshape(shaped).astype(half)
-    allowed = ((positions // BLOCK)[None, :] <= (positions // BLOCK)[:, None]) & (
-        positions < slot_value(lengths)
-    )[None, :]
-    scores = (
-        jnp.einsum("qhd,khd->hqk", query_low, key_low, preferred_element_type=jnp.float32)
-        * score_scale
-    )
-    scores = jnp.where(allowed[None], scores, MASKED)
-    exponents = jnp.exp(scores - jnp.max(scores, axis=2, keepdims=True)) * allowed[None]
-    probabilities = exponents / jnp.sum(exponents, axis=2, keepdims=True)
-    probabilities_low = probabilities.astype(half)
-    attended = jnp.einsum(
-        "hqk,khd->qhd", probabilities_low, value_low, preferred_element_type=jnp.float32
-    )
-    attended_low = attended.reshape(seq_length, width).astype(half)
+    attended_low, query_low, key_low, value_low = head_attention(
+        *projected, length, cosine_table, sine_table, score_scale
+    )
     attended_low, upstream_all = lax.optimization_barrier((attended_low, upstream_all))
     output_middle = narrow_product(attended_low, output_first).astype(half)
     attention_part = narrow_product(attended_low, output_weight) + narrow_product(
@@ -519,7 +614,6 @@
     shared_grad_hidden = shared_grad_hidden[:, :shared_wide] + rows_product(down_inner, down_first)
     shared_grad_pre = gated_back(shared_pre[0], shared_pre[1], shared_grad_hidden)
     shared_inner = chosen(rows_product(shared_grad_pre, shared_up), twice(selector))
-    copy_grad, layer_sum = lax.optimization_barrier((copy_grad, layer_sum))
     second_part = token_product(spread, copy_grad) + rows_product(
         jnp.concatenate([shared_grad_pre, shared_inner], axis=1), shared_joined
     )
@@ -531,7 +625,11 @@
         ],
         axis=0,
     )
-    own_dots = jnp.transpose(lax.psum_scatter(dots, "expert", scatter_dimension=1, tiled=True))
+    dots = jnp.transpose(dots.reshape(dots.shape[0], owners, count_rows), (1, 0, 2))
+    own_dots = jnp.transpose(
+        jnp.sum(lax.all_to_all(dots, "expert", split_axis=0, concat_axis=0, tiled=True), axis=0)
+    )
+    second_part, layer_sum = lax.optimization_barrier((second_part.astype(half), layer_sum))
     second_sum = scatter_rows(second_part).astype(jnp.float32)
     own_weights = own_rows(gate_weights)
     gate_grads = own_dots[:, :experts]
@@ -570,50 +668,35 @@
         axis=1,
     ).astype(half)
     wide_grads, output_upstream = lax.optimization_barrier((wide_grads, output_upstream))
+    expert_grads = lax.all_gather(wide_grads, "dp", axis=0, tiled=True)
 
     output_inner = rows_product(output_upstream, output_second).astype(half)
     attended_grad = (
-        (rows_product(output_upstream, output_weight) + rows_product(output_inner, output_first))
-        .astype(half)
-        .reshape(shaped)
-    )
-    row_delta = jnp.transpose(jnp.sum(attended_grad.astype(jnp.float32) * attended, axis=2))
-    prob_grads = jnp.einsum(
-        "qhd,khd->hqk", attended_grad, value_low, preferred_element_type=jnp.float32
-    )
-    score_grad = (probabilities * (prob_grads - row_delta[:, :, None])).astype(half)
-    query_grad = (
-        jnp.einsum("hqk,khd->qhd", score_grad, key_low, preferred_element_type=jnp.float32)
-        * score_scale
-    )
-    key_grad = (
-        jnp.einsum("hqk,qhd->khd", score_grad, query_low, preferred_element_type=jnp.float32)
-        * score_scale
-    )
-    value_grad = jnp.einsum(
-        "hqk,qhd->khd", probabilities_low, attended_grad, preferred_element_type=jnp.float32
-    )
+        rows_product(output_upstream, output_weight) + rows_product(output_inner, output_first)
+    ).astype(half)
     pre_grads = jnp.concatenate(
-        [
-            rotate(query_grad, cosine_table, sine_table, -1.0).reshape(seq_length, width),
-            rotate(key_grad, cosine_table, sine_table, -1.0).reshape(seq_length, width),
-            value_grad.reshape(seq_length, width),
-        ],
+        head_attention_back(
+            query_low,
+            key_low,
+            value_low,
+            attended_grad,
+            length,
+            cosine_table,
+            sine_table,
+            score_scale,
+        ),
         axis=1,
-    ).astype(half)
+    )
+    pre_grads, expert_grads = lax.optimization_barrier((pre_grads, expert_grads))
     qkv_inner = rows_product(pre_grads, qkv_up).astype(half)
     first_part = rows_product(jnp.concatenate([pre_grads, qkv_inner], axis=1), qkv_joined)
-    first_grad = scatter_rows(group_wide(first_part)).astype(jnp.float32)
-    unused, factor_first = rms_forward(input_rows, attention_norm_gain)
-    tokens_grad = residual_grad + rms_backward(
-        input_rows, factor_first, attention_norm_gain, first_grad
-    )
+    first_part = group_wide(first_part).astype(half)
     layer_out = (residual_stream + layer_sum.astype(jnp.float32)).astype(half)
 
     own_router_middle = own_rows(router_middle)
     router_grad_b = token_product(own_router_middle, logit_grads)
     spare = -experts % 128
-    summed, owned = reduce_adapters(
+    summed, owned, first_part = reduce_adapters(
         [slot_wide(value) for value in row_blocks(token_product(qkv_inner, first_narrow), 3)]
         + [slot_wide(token_product(output_middle, output_upstream))]
         + row_blocks(token_product(shared_inner, second_all), 2)
@@ -634,11 +717,16 @@
         adapter_slot_index,
         owner_index,
         owners,
+        first_part,
+    )
+    first_grad = scatter_rows(first_part).astype(jnp.float32)
+    unused, factor_first = rms_forward(input_rows, attention_norm_gain)
+    tokens_grad = residual_grad + rms_backward(
+        input_rows, factor_first, attention_norm_gain, first_grad
     )
     attn_grad_a = jnp.stack([jnp.transpose(value) for value in summed[:3] + owned[3:4]])
     attn_grad_b = jnp.stack(owned[:3] + summed[3:4])
 
-    expert_grads = lax.all_gather(wide_grads, "dp", axis=0, tiled=True)
     rank_range = jnp.arange(ADAPTER_COUNT * ADAPTER_RANK, dtype=jnp.int32)
     source_rank = jnp.arange(expert_grads.shape[0], dtype=jnp.int32)
     source_place = expert_grads[:, -1].astype(jnp.int32) * ADAPTER_RANK + source_rank % ADAPTER_RANK

time: 641 us -> 581 us (0.906)
  waiting for transfers between devices: 215 us -> 172 us
  matrix products: 197 us -> 172 us
  other arithmetic: 54.3 us -> 37.7 us
  blocking collectives: 27.1 us -> 42.5 us
  Pallas kernels: 0 us -> 14.5 us
    reduce_scatter x4, waiting for transfers between devices: 152 us -> 103 us  [scatter_rows(): lax.psum_scatter(values.astype(half), 'expert', scatter_dimension=0, tile...]
    all_gather x1, blocking collectives: 13.8 us -> 34.3 us  [on_device(): routes_all = lax.all_gather(routes, 'expert', axis=0, tiled=True)]
    pallas_call x0 -> x2, Pallas kernels: none -> 14.5 us  [the longest x1 8.04 us: head_attention_back(): pl.pallas_call(functools.partial(attention_backward, score_scale), grid=(...]
    all_gather x1, waiting for transfers between devices: 0.01 us -> 13.2 us  [on_device(): expert_grads = lax.all_gather(wide_grads, 'dp', axis=0, tiled=True)]
    dot_general x5 -> x0, matrix products: 12.5 us -> none  [the longest x1 4.84 us: on_device(): jnp.einsum('qhd,khd->hqk', attended_grad, value_low, preferred_element_ty...]
    dot_general x16 -> x15, matrix products: 63.6 us -> 51.9 us  [rows_product(): lax.dot_general(left_side, right_side, (((1,), (1,)), ((), ())), preferre...]
    concatenate x16 -> x1, local copies, waits for them, and re-layouts: 11.5 us -> 0.24 us  [reduce_adapters(): jnp.concatenate([partial_all, owned_all], axis=1).astype(jnp.bfloat16)]
    sub x1 -> x0, matrix products: 10.8 us -> none  [on_device(): scores - jnp.max(scores, axis=2, keepdims=True)]
  transfers between devices with their start and end apart: 19 -> 19, of which waited for: 11 -> 12; matrix products, arithmetic and copies ran while one was open for 35% -> 33% of each run, Pallas kernels for 0% -> 3%
where the time goes in v4:
time: 581 us; the launch traced here: 574 us
  waiting for transfers between devices  172 us (30%)
  matrix products  172 us (30%)
  local copies, waits for them, and re-layouts  92 us (16%)
  blocking collectives  42.5 us (7%)
  other arithmetic  37.7 us (6%)
  starting transfers between devices  27.1 us (5%)
  between operations  17.1 us (3%)
  Pallas kernels  14.5 us (2%)
    reduce_scatter x4, waiting for transfers between devices, scatter_rows(): lax.psum_scatter(values.astype(half), 'expert', scatter_dimension=0, tile...  103 us
    dot_general x19, matrix products, narrow_product(): return jnp.dot(left_side, right_side, preferred_element_type=jnp.float32)  64.8 us
    dot_general x22, matrix products, token_product(): lax.dot_general(left_side, right_side, (((0,), (0,)), ((), ())), preferre...  55.2 us
    dot_general x15, matrix products, rows_product(): lax.dot_general(left_side, right_side, (((1,), (1,)), ((), ())), preferre...  51.9 us
    all_gather x1, blocking collectives, on_device(): routes_all = lax.all_gather(routes, 'expert', axis=0, tiled=True)  34.3 us
    all_gather x1, waiting for transfers between devices, on_device(): lax.all_gather(residual_grad.astype(half), 'expert', axis=0, tiled=True)  22.9 us
    unnamed x232, local copies, waits for them, and re-layouts  22.4 us
    concatenate x1, local copies, waits for them, and re-layouts, on_device(): jnp.concatenate([expert_gate_up_weight[0, 0], expert_gate_up_weight[0, 1]...  18.9 us
  transfers between devices with their start and end apart: 19, of which 12 were waited for; matrix products, arithmetic and copies ran while one was open for 33% of the time, Pallas kernels for 3%

profile of v4, /device:TPU:11, one launch (start us, length us, event | category | flops | bytes accessed | tf_op | source)
XLA Modules:
  0.0 574.4 jit_solution(1314770545453122771)
XLA Ops:
  17.3 10.0 %collective-permute-done.1 = bf16[512,256]{1,0:T(8,128)(2,1)S(1)} collective-permute-done((bf16[512,256]{1,0:T(8,128)(2,1)S(1)}, bf16[512,256]{1,0:T(8,128)(2,1)S(1)}, u32[]{:S(2)}, u32[]{:S(2)}) %collective-permute-start.1) | collective-permute-done | bytes 262176 | tf_op jit(solution)/shard_map/ppermute | solution.py:227
  30.3 34.3 %all_gather.25 = s32[1024,4]{0,1:T(4,128)S(1)} all-gather(s32[128,4]{0,1:T(4,128)S(1)} %copy-done.90), channel_id=1, replica_groups=mesh['dp'=4,'expert'=8] {'expert'}, dimensions={0}, use_global_device_ids=true | all-gather | bytes 18432 | tf_op jit(solution)/shard_map/all_gather | solution.py:453
  72.8 6.7 %concatenate.100 = bf16[2048,816]{1,0:T(8,128)(2,1)} concatenate(bf16[2048,256]{1,0:T(8,128)(2,1)} %get-tuple-element.76, bf16[2048,256]{1,0:T(8,128)(2,1)} %get-tuple-element.75, bf16[2048,256]{1,0:T(8,128)(2,1)S(1)} %get-tuple-element.74, bf16[2048,16]{1,0:T(8,128)(2,1)} %get-tuple-element.91, bf16[2048,16]{1,0:T(8,128)(2,1)} %get-tuple-element.90, ...), dimensions={1} | concatenate | bytes 6684672 | tf_op jit(solution)/shard_map/concatenate | solution.py:523
  83.1 6.1 %fusion.51 = f32[1024,816]{0,1:T(8,128)S(1)} fusion(bf16[2048,816]{1,0:T(8,128)(2,1)} %concatenate.100, bf16[1024,2048]{1,0:T(8,128)(2,1)S(1)} %copy-done.29, f32[2048]{0:T(1024)S(1)} %copy-done.66, f32[1024]{0:T(1024)S(1)} %add_rsqrt_fusion), kind=kOutput, calls=%fused_computation.108 | convolution fusion | flops 3430940672 | bytes 10891264 | tf_op jit(solution)/shard_map/dot_general | solution.py:25
  100.4 6.5 %head_attention.1 = (bf16[1024,256]{1,0:T(8,128)(2,1)S(1)}, bf16[1024,256]{1,0:T(8,128)(2,1)S(1)}, bf16[1024,256]{1,0:T(8,128)(2,1)S(1)}, bf16[1024,256]{1,0:T(8,128)(2,1)S(1)}) custom-call(s32[1]{0:T(128)S(6)} %copy.137.length_ref, f32[1024,256]{1,0:T(8,128)S(1)} %get-tuple-element.73.q_ref, f32[1024,256]{1,0:T(8,128)S(1)} %get-tuple-element.72.k_ref, ...), custom_call_target="tpu_custom_call" | custom-call | flops 805306368 | bytes 6291456 | tf_op jit(solution)/shard_map/head_attention/pallas_call | solution.py:129
  120.0 48.8 %reduce-scatter.5.cloned.1.call-done = bf16[128,2048]{1,0:T(8,128)(2,1)} async-done(((bf16[1024,2048]{1,0:T(8,128)(2,1)}), bf16[128,2048]{1,0:T(8,128)(2,1)}) %reduce-scatter.5.cloned.1.call-update) | async-done | bytes 524304 | tf_op jit(solution)/shard_map/reduce_scatter | solution.py:447
  185.4 9.5 %slice_bitcast_fusion = (bf16[2048,1408]{1,0:T(8,128)(2,1)}, bf16[2048,1408]{1,0:T(8,128)(2,1)}) fusion(bf16[1,2,2048,1408]{3,2,1,0:T(8,128)(2,1)} %param.37), kind=kLoop, calls=%fused_computation.21 | loop fusion | bytes 23068672 | tf_op jit(solution)/shard_map/squeeze | solution.py:558
  194.9 18.9 %concatenate.109 = bf16[2048,2848]{1,0:T(8,128)(2,1)} concatenate(bf16[2048,1408]{1,0:T(8,128)(2,1)} %get-tuple-element.63, bf16[2048,1408]{1,0:T(8,128)(2,1)} %get-tuple-element.62, bf16[2048,16]{1,0:T(8,128)(2,1)} %get-tuple-element.97, bf16[2048,16]{1,0:T(8,128)(2,1)} %get-tuple-element.96), dimensions={1} | concatenate | bytes 23330816 | tf_op jit(solution)/shard_map/concatenate | solution.py:557
  218.5 6.3 %slice_bitcast_fusion.3 = (bf16[2048,704]{0,1:T(8,128)(2,1)}, bf16[2048,704]{0,1:T(8,128)(2,1)}) fusion(bf16[2,2048,704]{1,2,0:T(8,128)(2,1)} %param.34), kind=kLoop, calls=%fused_computation.62 | loop fusion | bytes 11534336 | tf_op jit(solution)/shard_map/squeeze | solution.py:574
  230.4 11.5 %fusion.68 = f32[1024,1440]{0,1:T(8,128)} fusion(bf16[1024,2048]{1,0:T(8,128)(2,1)S(1)} %copy-done.11, bf16[2048,16]{0,1:T(8,128)(2,1)} %copy.110, bf16[2048,16]{0,1:T(8,128)(2,1)S(1)} %copy-done.63, bf16[2048,704]{0,1:T(8,128)(2,1)} %get-tuple-element.70, bf16[2048,704]{0,1:T(8,128)(2,1)} %get-tuple-element.69), kind=kOutput, calls=%fused_computation.144 | convolution fusion | flops 6063390720 | bytes 15990784 | tf_op jit(solution)/shard_map/dot_general | solution.py:25
  254.9 5.8 %fusion.175 = f32[1024,2048]{1,0:T(8,128)} fusion(bf16[1024,704]{0,1:T(8,128)(2,1)S(1)} %get-tuple-element.68, bf16[704,2048]{1,0:T(8,128)(2,1)S(1)} %copy-done.96), kind=kOutput, calls=%fused_computation.367 | convolution fusion | flops 2952790016 | bytes 12713984 | tf_op jit(solution)/shard_map/dot_general | solution.py:25
  263.7 7.5 %fusion.174 = f32[576,2848]{1,0:T(8,128)S(1)} fusion(bf16[576,2048]{1,0:T(8,128)(2,1)S(1)} %convolution_convert_fusion.2, bf16[2048,2848]{1,0:T(8,128)(2,1)S(1)} %bitcast.236), kind=kOutput, calls=%fused_computation.366 | convolution fusion | flops 6719275008 | bytes 20586496 | tf_op jit(solution)/shard_map/dot_general | solution.py:25
  291.3 5.6 add_convert_fusion
  300.5 7.3 %fusion.5 = f32[576,1424]{1,0:T(8,128)S(1)} fusion(bf16[16,2048]{1,0:T(8,128)(2,1)S(1)} %copy-done.44, bf16[1408,2048]{1,0:T(8,128)(2,1)} %bitcast.262, f32[576,2048]{1,0:T(8,128)S(1)} %copy-done.24, f32[576]{0:T(1024)S(1)} %get-tuple-element.59), kind=kOutput, calls=%fused_computation.16 | convolution fusion | flops 3373662208 | bytes 13834496 | tf_op jit(solution)/shard_map/dot_general | solution.py:167
  312.6 16.7 %fusion.35 = f32[1024,2048]{1,0:T(8,128)} fusion(s32[1024]{0:T(1024)S(1)} %add_bitcast_fusion, pred[1024]{0:T(1024)(128)(4,1)S(1)} %copy-done.82, bf16[2048,2848]{1,0:T(8,128)(2,1)} %concatenate.109, bf16[576,32]{1,0:T(8,128)(2,1)S(1)} %fusion.61, bf16[576,1408]{1,0:T(8,128)(2,1)} %copy-done.98, bf16[576,1408]{1,0:T(8,128)(2,1)} %copy-done.97), kind=kOutput, calls=%fused_computation.78 | convolution fusion | flops 9147396096 | bytes 23340032 | tf_op jit(solution)/shard_map/dot_general | solution.py:173
  329.4 12.6 %add_convert_fusion.1 = bf16[1024,2048]{1,0:T(8,128)(2,1)} fusion(f32[1024,2048]{1,0:T(8,128)} %fusion.35, bf16[1024,32]{0,1:T(8,128)(2,1)S(1)} %fusion.62, bf16[1024,704]{0,1:T(8,128)(2,1)} %get-tuple-element.67, bf16[1024,704]{0,1:T(8,128)(2,1)} %get-tuple-element.66, bf16[2048,16]{0,1:T(8,128)(2,1)S(1)} %copy-done.65, ...), kind=kOutput, calls=%fused_computation.10 | convolution fusion | flops 6076432384 | bytes 21430272 | tf_op jit(solution)/shard_map/dot_general | solution.py:167
  357.8 38.5 %reduce-scatter.9.cloned.1.call-done = bf16[128,2048]{1,0:T(8,128)(2,1)} async-done(((bf16[1024,2048]{1,0:T(8,128)(2,1)}), bf16[128,2048]{1,0:T(8,128)(2,1)}) %reduce-scatter.9.cloned.1.call-update) | async-done | bytes 524304 | tf_op jit(solution)/shard_map/reduce_scatter | solution.py:447
  424.5 22.9 %all-gather.14.cloned.1.call-done = bf16[1024,2048]{1,0:T(8,128)(2,1)} async-done(((bf16[128,2048]{1,0:T(8,128)(2,1)}), bf16[1024,2048]{1,0:T(8,128)(2,1)}) %all-gather.14.cloned.1.call-update) | async-done | bytes 4194320 | tf_op jit(solution)/shard_map/all_gather | solution.py:654
  454.3 8.0 %head_attention_back.1 = (bf16[1024,256]{1,0:T(8,128)(2,1)S(1)}, bf16[1024,256]{1,0:T(8,128)(2,1)S(1)}, bf16[1024,256]{1,0:T(8,128)(2,1)S(1)}) custom-call(s32[1]{0:T(128)S(6)} %copy.137.length_ref, bf16[1024,256]{1,0:T(8,128)(2,1)S(1)} %get-tuple-element.40.q_ref, bf16[1024,256]{1,0:T(8,128)(2,1)S(1)} %copy-done.5, bf16[1024,256]{1,0:T(8,128)(2,1)S(1)} %copy-done.7, ...), custom_call_target="tpu_custom_call" | custom-call | flops 1879048192 | bytes 4194304 | tf_op jit(solution)/shard_map/head_attention_back/pallas_call | solution.py:148
  464.5 13.2 %all-gather.16.cloned.1.call-done = bf16[64,10496]{1,0:T(8,128)(2,1)} async-done(((bf16[16,10496]{1,0:T(8,128)(2,1)}), bf16[64,10496]{1,0:T(8,128)(2,1)}) %all-gather.16.cloned.1.call-update) | async-done | bytes 1343504 | tf_op jit(solution)/shard_map/all_gather | solution.py:671
  485.5 6.2 %convolution_convert_fusion = bf16[1024,2048]{1,0:T(8,128)(2,1)} fusion(bf16[2048,816]{1,0:T(8,128)(2,1)S(1)} %copy-done.31, bf16[1024,48]{1,0:T(8,128)(2,1)S(1)} %convolution_convert_fusion.12, bf16[1024,768]{1,0:T(8,128)(2,1)S(1)} %copy-done.21), kind=kOutput, calls=%fused_computation.28 | convolution fusion | flops 3427991552 | bytes 9207808 | tf_op jit(solution)/shard_map/dot_general | solution.py:167
  507.6 10.0 %all-to-all-done.1 = bf16[8,2,19648]{2,1,0:T(2,128)(2,1)S(1)} async-done(((bf16[8,2,19648]{2,1,0:T(2,128)(2,1)}), bf16[8,2,19648]{2,1,0:T(2,128)(2,1)S(1)}, u32[]{:S(2)}, u32[]{:S(2)}) %all-to-all-start.1) | async-done | bytes 628768 | tf_op jit(solution)/shard_map/all_to_all | solution.py:311
  518.8 8.3 %all-gather.1 = bf16[4,2,41728]{2,1,0:T(2,128)(2,1)S(1)} all-gather(bf16[1,2,41728]{2,1,0:T(2,128)(2,1)S(1)} %bitcast.244), channel_id=2, replica_groups=mesh['dp'=4,'expert'=8] {'dp'}, dimensions={0}, use_global_device_ids=true | all-gather | bytes 834560 | tf_op jit(solution)/shard_map/all_gather | solution.py:324
  551.3 11.7 %reduce-scatter.11.cloned.1.call-done = bf16[128,2048]{1,0:T(8,128)(2,1)} async-done(((bf16[1024,2048]{1,0:T(8,128)(2,1)}), bf16[128,2048]{1,0:T(8,128)(2,1)}) %reduce-scatter.11.cloned.1.call-update) | async-done | bytes 524304 | tf_op jit(solution)/shard_map/reduce_scatter | solution.py:447
  (419 shorter events, 224.4 us)
Async XLA Ops:
  7.2 243.9 %copy-start = (bf16[5632,128]{1,0:T(8,128)(2,1)S(1)}, bf16[5632,128]{1,0:T(8,128)(2,1)}, u32[]{:S(2)}) copy-start(bf16[5632,128]{1,0:T(8,128)(2,1)} %param.48) | copy-start | bytes 4325380
  7.2 72.3 %all-gather.8.cloned.1.call-start = ((), (), s32[]{:S(2)}) async-start(), calls=%async_computation.6 | async-start | bytes 4718592 | tf_op jit(solution)/shard_map/all_gather | solution.py:449
  7.9 104.1 %all-gather.10.cloned.1.call-start = ((), (), s32[]{:S(2)}) async-start(), calls=%async_computation.7 | async-start | bytes 4718592 | tf_op jit(solution)/shard_map/all_gather | solution.py:455
  8.7 160.0 %reduce-scatter.5.cloned.1.call-start = ((), (), s32[]{:S(2)}) async-start(), calls=%async_computation.8 | async-start | bytes 4718592 | tf_op jit(solution)/shard_map/reduce_scatter | solution.py:447
  9.9 7.4 %collective-permute-start = (bf16[512,256]{1,0:T(8,128)(2,1)S(1)}, bf16[512,256]{1,0:T(8,128)(2,1)S(1)}, u32[]{:S(2)}, u32[]{:S(2)}) collective-permute-start(bf16[512,256]{1,0:T(8,128)(2,1)S(1)} %get-tuple-element.81), channel_id=1, source_target_pairs={{0,0},{1,3},{2,6},{3,1},{4,4},{5,7},{6,2},{7,5},{8,8},{9,11},{10,1... | collective-permute-start | bytes 786440 | tf_op jit(solution)/shard_map/ppermute | solution.py:227
  12.0 15.3 %collective-permute-start.1 = (bf16[512,256]{1,0:T(8,128)(2,1)S(1)}, bf16[512,256]{1,0:T(8,128)(2,1)S(1)}, u32[]{:S(2)}, u32[]{:S(2)}) collective-permute-start(bf16[512,256]{1,0:T(8,128)(2,1)S(1)} %get-tuple-element.82), channel_id=1, source_target_pairs={{0,1},{1,4},{2,7},{3,2},{4,5},{5,0},{6,3},{7,6},{8,9},{9,12},{10,1... | collective-permute-start | bytes 786440 | tf_op jit(solution)/shard_map/ppermute | solution.py:227
  15.2 12.1 %collective-permute-start.2 = (bf16[512,256]{1,0:T(8,128)(2,1)S(1)}, bf16[512,256]{1,0:T(8,128)(2,1)S(1)}, u32[]{:S(2)}, u32[]{:S(2)}) collective-permute-start(bf16[512,256]{1,0:T(8,128)(2,1)S(1)} %get-tuple-element.83), channel_id=1, source_target_pairs={{0,2},{1,5},{2,0},{3,3},{4,6},{5,1},{6,4},{7,7},{8,10},{9,13},{10,... | collective-permute-start | bytes 786440 | tf_op jit(solution)/shard_map/ppermute | solution.py:227
  27.6 42.2 %collective-permute-start.4 = (bf16[3,512,256]{2,1,0:T(8,128)(2,1)S(1)}, bf16[3,512,256]{2,1,0:T(8,128)(2,1)S(1)}, u32[]{:S(2)}, u32[]{:S(2)}) collective-permute-start(bf16[3,512,256]{2,1,0:T(8,128)(2,1)S(1)} %get-tuple-element.99), channel_id=1, source_target_pairs={{0,16},{8,24},{16,0},{24,8},{1,17},{9,25},{17,1},{25,9},{2,18},{10... | collective-permute-start | bytes 2359304 | tf_op jit(solution)/shard_map/ppermute | solution.py:244
  29.0 40.8 %collective-permute-start.3 = (bf16[3,512,256]{2,1,0:T(8,128)(2,1)S(1)}, bf16[3,512,256]{2,1,0:T(8,128)(2,1)S(1)}, u32[]{:S(2)}, u32[]{:S(2)}) collective-permute-start(bf16[3,512,256]{2,1,0:T(8,128)(2,1)S(1)} %get-tuple-element.99), channel_id=1, source_target_pairs={{0,8},{8,0},{16,24},{24,16},{1,9},{9,1},{17,25},{25,17},{2,10},{10... | collective-permute-start | bytes 2359304 | tf_op jit(solution)/shard_map/ppermute | solution.py:244
  29.2 40.6 %collective-permute-start.5 = (bf16[3,512,256]{2,1,0:T(8,128)(2,1)S(1)}, bf16[3,512,256]{2,1,0:T(8,128)(2,1)S(1)}, u32[]{:S(2)}, u32[]{:S(2)}) collective-permute-start(bf16[3,512,256]{2,1,0:T(8,128)(2,1)S(1)} %get-tuple-element.99), channel_id=1, source_target_pairs={{0,24},{8,16},{16,8},{24,0},{1,25},{9,17},{17,9},{25,1},{2,26},{10... | collective-permute-start | bytes 2359304 | tf_op jit(solution)/shard_map/ppermute | solution.py:244
  119.9 106.8 %all-gather.12.cloned.1.call-start = ((), (), s32[]{:S(2)}) async-start(), calls=%async_computation.9 | async-start | bytes 4718592 | tf_op jit(solution)/shard_map/all_gather | solution.py:541
  173.2 172.4 %reduce-scatter.7.cloned.1.call-start = ((), (), s32[]{:S(2)}) async-start(), calls=%async_computation.10 | async-start | bytes 4718592 | tf_op jit(solution)/shard_map/reduce_scatter | solution.py:447
  230.4 57.5 %copy-start.36 = (f32[1024,25]{0,1:T(8,128)}, f32[1024,25]{0,1:T(8,128)S(1)}, u32[]{:S(2)}) copy-start(f32[1024,25]{0,1:T(8,128)S(1)} %fusion.99) | copy-start | bytes 307204
  297.0 99.3 %reduce-scatter.9.cloned.1.call-start = ((), (), s32[]{:S(2)}) async-start(), calls=%async_computation.11 | async-start | bytes 4718592 | tf_op jit(solution)/shard_map/reduce_scatter | solution.py:447
  341.9 55.7 %copy-start.10 = (bf16[128,2048]{1,0:T(8,128)(2,1)S(1)}, bf16[128,2048]{1,0:T(8,128)(2,1)}, u32[]{:S(2)}) copy-start(bf16[128,2048]{1,0:T(8,128)(2,1)} %param.27) | copy-start | bytes 1572868
  342.0 55.7 %copy-start.18 = (bf16[128,2048]{1,0:T(8,128)(2,1)S(1)}, bf16[128,2048]{1,0:T(8,128)(2,1)}, u32[]{:S(2)}) copy-start(bf16[128,2048]{1,0:T(8,128)(2,1)} %reduce-scatter.5.cloned.1.call-done) | copy-start | bytes 1572868
  342.0 55.7 %copy-start.77 = (f32[2048]{0:T(1024)S(1)}, f32[2048]{0:T(1024)}, u32[]{:S(2)}) copy-start(f32[2048]{0:T(1024)} %param.30) | copy-start | bytes 24580
  346.5 9.6 %all-to-all-start = ((f32[8,16,128]{2,1,0:T(8,128)}), f32[8,16,128]{2,1,0:T(8,128)S(1)}, u32[]{:S(2)}, u32[]{:S(2)}) async-start(f32[8,16,128]{2,1,0:T(8,128)} %maximum_bitcast_fusion.2), calls=%async_computation.3 | async-start | bytes 131072 | tf_op jit(solution)/shard_map/all_to_all | solution.py:630
  351.8 95.7 %all-gather.14.cloned.1.call-start = ((), (), s32[]{:S(2)}) async-start(), calls=%async_computation.12 | async-start | bytes 4718592 | tf_op jit(solution)/shard_map/all_gather | solution.py:654
  402.1 75.7 %all-gather.16.cloned.1.call-start = ((), (), s32[]{:S(2)}) async-start(), calls=%async_computation.13 | async-start | bytes 1679360 | tf_op jit(solution)/shard_map/all_gather | solution.py:671
  493.0 24.5 %all-to-all-start.1 = ((bf16[8,2,19648]{2,1,0:T(2,128)(2,1)}), bf16[8,2,19648]{2,1,0:T(2,128)(2,1)S(1)}, u32[]{:S(2)}, u32[]{:S(2)}) async-start(bf16[8,2,19648]{2,1,0:T(2,128)(2,1)} %reshape.214), calls=%async_computation.5 | async-start | bytes 1261568 | tf_op jit(solution)/shard_map/all_to_all | solution.py:311
  498.6 64.3 %reduce-scatter.11.cloned.1.call-start = ((), (), s32[]{:S(2)}) async-start(), calls=%async_computation.14 | async-start | bytes 4718592 | tf_op jit(solution)/shard_map/reduce_scatter | solution.py:447
  530.2 15.4 %collective-permute-start.6 = (bf16[2,41600]{1,0:T(2,128)(2,1)S(1)}, bf16[2,41600]{1,0:T(2,128)(2,1)S(1)}, u32[]{:S(2)}, u32[]{:S(2)}) collective-permute-start(bf16[2,41600]{1,0:T(2,128)(2,1)S(1)} %get-tuple-element.129), channel_id=1, source_target_pairs={{0,0},{1,4},{2,1},{3,5},{4,2},{5,6},{6,3},{7,7},{8,8},{9,12},{10,9... | collective-permute-start | bytes 499208 | tf_op jit(solution)/shard_map/ppermute | solution.py:338
  532.1 13.4 %collective-permute-start.7 = (bf16[2,41600]{1,0:T(2,128)(2,1)S(1)}, bf16[2,41600]{1,0:T(2,128)(2,1)S(1)}, u32[]{:S(2)}, u32[]{:S(2)}) collective-permute-start(bf16[2,41600]{1,0:T(2,128)(2,1)S(1)} %get-tuple-element.130), channel_id=1, source_target_pairs={{0,4},{1,0},{2,5},{3,1},{4,6},{5,2},{6,7},{7,3},{8,12},{9,8},{10,1... | collective-permute-start | bytes 499208 | tf_op jit(solution)/shard_map/ppermute | solution.py:338
  (103 other events, 1225.3 us)
Sparse Core Ops, SparseCore 0:
  9.6 51.9 all-gather.7
  63.2 48.7 all-gather.9
  120.0 48.6 reduce-scatter.4
  173.3 45.7 all-gather.11
  297.1 48.4 reduce-scatter.6
  347.7 48.5 reduce-scatter.8
  402.2 45.2 all-gather.13
  449.3 28.4 all-gather.15
  501.7 61.2 reduce-scatter.10

commit v5 on v4

--- a/solution.py
+++ b/solution.py
@@ -451,7 +451,6 @@
         attention_query_key_value, owner_index, owners, slot_count, head_start, width
     )
     routes_all = lax.all_gather(routes, "expert", axis=0, tiled=True)
-    tokens_all, routes_all = lax.optimization_barrier((tokens_all, routes_all))
     upstream_all = lax.all_gather(cotangent, "expert", axis=0, tiled=True)
     if attention_output_weight.shape[0] == width:
         output_weight = attention_output_weight
@@ -503,6 +502,28 @@
     expert_down_first = picked_maps(expert_down_adapter_first[0], 1)
     expert_down_second = picked_maps(expert_down_adapter_second[0], 0)
 
+    expert_joined = jnp.concatenate(
+        [expert_gate_up_weight[0, 0], expert_gate_up_weight[0, 1], expert_first[0], expert_first[1]],
+        axis=1,
+    )
+    shared_joined = jnp.concatenate(
+        [shared_gate_up_weight[0], shared_gate_up_weight[1], shared_first[0], shared_first[1]], axis=1
+    )
+    expert_down_joined = jnp.concatenate([expert_down_weight[0], expert_down_second], axis=0)
+    down_joined = jnp.concatenate([shared_down_weight, down_second], axis=0)
+    tokens_all, routes_all, expert_joined, shared_joined, expert_down_joined, down_joined = (
+        lax.optimization_barrier(
+            (
+                tokens_all,
+                routes_all,
+                expert_joined,
+                shared_joined,
+                expert_down_joined,
+                down_joined,
+            )
+        )
+    )
+
     expert_range = jnp.arange(experts, dtype=jnp.int32)
     route_hits = jnp.any(routes_all[:, :, None] == expert_range[None, None, :], axis=1)
     own_hits = jnp.any(routes_all == owner_index, axis=1)
@@ -520,6 +541,7 @@
     cosine_table = jnp.concatenate([cosine_table, cosine_table], axis=1)
     sine_table = jnp.concatenate([-sine_table, sine_table], axis=1)
     length = slot_value(lengths).reshape(1)
+    first_narrow, qkv_weights = lax.optimization_barrier((first_narrow, qkv_weights))
     qkv_joined = jnp.concatenate(qkv_weights + [attention_first[kind] for kind in range(3)], axis=1)
     qkv_up = block_diagonal([qkv_second[kind] for kind in range(3)])
     projected = narrow_product(first_narrow, qkv_joined)
@@ -554,10 +576,6 @@
 
     expert_rows = narrow_product(spread, second_all).astype(half)
     feed = expert_down_weight.shape[1]
-    expert_joined = jnp.concatenate(
-        [expert_gate_up_weight[0, 0], expert_gate_up_weight[0, 1], expert_first[0], expert_first[1]],
-        axis=1,
-    )
     expert_up = block_diagonal([expert_second[0], expert_second[1]])
     expert_pre = narrow_product(expert_rows, expert_joined)
     expert_middle = chosen(expert_pre[:, 2 * feed :], twice(row_selector))
@@ -570,9 +588,6 @@
         + narrow_product(expert_down_middle, expert_down_second)
     ).astype(half)
 
-    shared_joined = jnp.concatenate(
-        [shared_gate_up_weight[0], shared_gate_up_weight[1], shared_first[0], shared_first[1]], axis=1
-    )
     shared_up = block_diagonal([shared_second[0], shared_second[1]])
     shared_pre = narrow_product(second_all, shared_joined)
     shared_middle = chosen(shared_pre[:, 2 * shared_wide :], twice(selector))
@@ -595,7 +610,6 @@
     row_dot = jnp.sum(upstream_rows * expert_result.astype(jnp.float32), axis=1, keepdims=True)
     gate_dot = jnp.sum(jnp.where(placed, row_dot, 0.0), axis=0)
     expert_upstream = (row_gate * upstream_rows).astype(half)
-    expert_down_joined = jnp.concatenate([expert_down_weight[0], expert_down_second], axis=0)
     expert_grad_hidden = rows_product(expert_upstream, expert_down_joined)
     expert_down_inner = chosen(expert_grad_hidden[:, feed:], row_selector)
     expert_grad_hidden = expert_grad_hidden[:, :feed] + rows_product(
@@ -603,19 +617,22 @@
     )
     expert_grad_pre = gated_back(expert_pre[0], expert_pre[1], expert_grad_hidden)
     expert_inner = chosen(rows_product(expert_grad_pre, expert_up), twice(row_selector))
-    copy_grad = rows_product(
-        jnp.concatenate([expert_grad_pre, expert_inner], axis=1), expert_joined
-    ).astype(half)
+    expert_grad_joined = lax.optimization_barrier(
+        jnp.concatenate([expert_grad_pre, expert_inner], axis=1)
+    )
+    copy_grad = rows_product(expert_grad_joined, expert_joined).astype(half)
 
     value_grads = (shared_weight * upstream_wide).astype(half)
-    down_joined = jnp.concatenate([shared_down_weight, down_second], axis=0)
     shared_grad_hidden = rows_product(value_grads, down_joined)
     down_inner = chosen(shared_grad_hidden[:, shared_wide:], selector)
     shared_grad_hidden = shared_grad_hidden[:, :shared_wide] + rows_product(down_inner, down_first)
     shared_grad_pre = gated_back(shared_pre[0], shared_pre[1], shared_grad_hidden)
     shared_inner = chosen(rows_product(shared_grad_pre, shared_up), twice(selector))
+    shared_grad_joined = lax.optimization_barrier(
+        jnp.concatenate([shared_grad_pre, shared_inner], axis=1)
+    )
     second_part = token_product(spread, copy_grad) + rows_product(
-        jnp.concatenate([shared_grad_pre, shared_inner], axis=1), shared_joined
+        shared_grad_joined, shared_joined
     )
     dots = jnp.concatenate(
         [
@@ -667,8 +684,18 @@
         ],
         axis=1,
     ).astype(half)
-    wide_grads, output_upstream = lax.optimization_barrier((wide_grads, output_upstream))
-    expert_grads = lax.all_gather(wide_grads, "dp", axis=0, tiled=True)
+    groups = lax.axis_size("dp")
+    if groups & (groups - 1):
+        expert_grads = lax.all_gather(wide_grads, "dp", axis=0, tiled=True)
+    else:
+        expert_grads = jnp.concatenate(
+            [wide_grads]
+            + [
+                lax.ppermute(wide_grads, "dp", [(source, source ^ step) for source in range(groups)])
+                for step in range(1, groups)
+            ],
+            axis=0,
+        )
 
     output_inner = rows_product(output_upstream, output_second).astype(half)
     attended_grad = (

time: 581 us -> 591 us (1.017)
  other arithmetic: 37.7 us -> 67.4 us
  blocking collectives: 42.5 us -> 22.5 us
  matrix products: 172 us -> 161 us
  local copies, waits for them, and re-layouts: 92 us -> 102 us
    all_gather x1, waiting for transfers between devices: 0.01 us -> 29.6 us  [on_device(): second_all = lax.all_gather(second_own, 'expert', axis=0, tiled=True)]
    all_gather x1, blocking collectives: 34.3 us -> 13 us  [on_device(): routes_all = lax.all_gather(routes, 'expert', axis=0, tiled=True)]
    dot_general x22, matrix products: 55.2 us -> 37.3 us  [token_product(): lax.dot_general(left_side, right_side, (((0,), (0,)), ((), ())), preferre...]
    concatenate x0 -> x6, other arithmetic: none -> 17.4 us  [the longest x1 5.87 us: on_device(): jnp.concatenate([shared_gate_up_weight[0], shared_gate_up_weight[1], shar...]
    all_gather x1 -> x0, waiting for transfers between devices: 13.2 us -> none  [on_device(): expert_grads = lax.all_gather(wide_grads, 'dp', axis=0, tiled=True)]
    all_gather x1, waiting for transfers between devices: 22.9 us -> 11.9 us  [on_device(): lax.all_gather(residual_grad.astype(half), 'expert', axis=0, tiled=True)]
    ppermute x3, waiting for transfers between devices: 10 us -> 0.01 us  [head_weights(): lax.ppermute(mine[:, step * width:(step + 1) * width], 'expert', [(source...]
    reduce_scatter x4, waiting for transfers between devices: 103 us -> 93.5 us  [scatter_rows(): lax.psum_scatter(values.astype(half), 'expert', scatter_dimension=0, tile...]
  transfers between devices with their start and end apart: 19 -> 21, of which waited for: 12 -> 9; matrix products, arithmetic and copies ran while one was open for 33% -> 36% of each run, Pallas kernels for 3% -> 1%
where the time goes in v5:
time: 591 us; the launch traced here: 584 us
  waiting for transfers between devices  167 us (28%)
  matrix products  161 us (27%)
  local copies, waits for them, and re-layouts  102 us (17%)
  other arithmetic  67.4 us (11%)
  starting transfers between devices  32.1 us (5%)
  blocking collectives  22.5 us (4%)
  between operations  17.4 us (3%)
  Pallas kernels  14.3 us (2%)
    reduce_scatter x4, waiting for transfers between devices, scatter_rows(): lax.psum_scatter(values.astype(half), 'expert', scatter_dimension=0, tile...  93.5 us
    dot_general x19, matrix products, narrow_product(): return jnp.dot(left_side, right_side, preferred_element_type=jnp.float32)  63.1 us
    dot_general x16, matrix products, rows_product(): lax.dot_general(left_side, right_side, (((1,), (1,)), ((), ())), preferre...  61 us
    dot_general x22, matrix products, token_product(): lax.dot_general(left_side, right_side, (((0,), (0,)), ((), ())), preferre...  37.3 us
    all_gather x1, waiting for transfers between devices, on_device(): second_all = lax.all_gather(second_own, 'expert', axis=0, tiled=True)  29.6 us
    unnamed x252, local copies, waits for them, and re-layouts  27.1 us
    concatenate x1, local copies, waits for them, and re-layouts, on_device(): jnp.concatenate([expert_gate_up_weight[0, 0], expert_gate_up_weight[0, 1]...  19 us
    all_to_all x1, waiting for transfers between devices, reduce_adapters(): lax.all_to_all(joined.reshape(owners, own_rows, joined.shape[1]), 'expert...  13.6 us
  transfers between devices with their start and end apart: 21, of which 9 were waited for; matrix products, arithmetic and copies ran while one was open for 36% of the time, Pallas kernels for 1%

profile of v5, /device:TPU:11, one launch (start us, length us, event | category | flops | bytes accessed | tf_op | source)
XLA Modules:
  0.0 583.9 jit_solution(7866184210237435946)
XLA Ops:
  21.9 6.4 %slice_bitcast_fusion.3 = (bf16[2048,704]{0,1:T(8,128)(2,1)}, bf16[2048,704]{0,1:T(8,128)(2,1)}) fusion(bf16[2,2048,704]{1,2,0:T(8,128)(2,1)} %param.34), kind=kLoop, calls=%fused_computation.47 | loop fusion | bytes 11534336 | tf_op jit(solution)/shard_map/squeeze | solution.py:510
  40.0 9.6 %slice_bitcast_fusion = (bf16[2048,1408]{1,0:T(8,128)(2,1)}, bf16[2048,1408]{1,0:T(8,128)(2,1)}) fusion(bf16[1,2,2048,1408]{3,2,1,0:T(8,128)(2,1)} %param.37), kind=kLoop, calls=%fused_computation.18 | loop fusion | bytes 23068672 | tf_op jit(solution)/shard_map/squeeze | solution.py:506
  65.1 19.0 %concatenate.102 = bf16[2048,2848]{1,0:T(8,128)(2,1)} concatenate(bf16[2048,1408]{1,0:T(8,128)(2,1)} %get-tuple-element.75, bf16[2048,1408]{1,0:T(8,128)(2,1)} %get-tuple-element.74, bf16[2048,16]{1,0:T(8,128)(2,1)} %get-tuple-element.109, bf16[2048,16]{1,0:T(8,128)(2,1)} %get-tuple-element.108), dimensions={1} | concatenate | bytes 23330816 | tf_op jit(solution)/shard_map/concatenate | solution.py:505
  84.1 13.0 %all_gather.22 = s32[1024,4]{0,1:T(4,128)S(1)} all-gather(s32[128,4]{0,1:T(4,128)} %param.39), channel_id=1, replica_groups=mesh['dp'=4,'expert'=8] {'expert'}, dimensions={0}, use_global_device_ids=true | all-gather | bytes 18432 | tf_op jit(solution)/shard_map/all_gather | solution.py:453
  97.1 5.9 %pad_maximum_fusion = bf16[2048,1440]{0,1:T(8,128)(2,1)} fusion(bf16[2048,16]{0,1:T(8,128)(2,1)} %copy.107, bf16[2048,16]{0,1:T(8,128)(2,1)} %copy.106, bf16[2048,704]{0,1:T(8,128)(2,1)} %get-tuple-element.82, bf16[2048,704]{0,1:T(8,128)(2,1)} %get-tuple-element.81), kind=kLoop, calls=%fused_computation.13 | loop fusion | flops 23592960 | bytes 11796480 | tf_op jit(solution)/shard_map/concatenate | solution.py:509
  113.9 6.7 %concatenate.107 = bf16[2048,816]{1,0:T(8,128)(2,1)} concatenate(bf16[2048,256]{1,0:T(8,128)(2,1)} %get-tuple-element.41, bf16[2048,256]{1,0:T(8,128)(2,1)} %get-tuple-element.42, bf16[2048,256]{1,0:T(8,128)(2,1)} %get-tuple-element.43, bf16[2048,16]{1,0:T(8,128)(2,1)} %get-tuple-element.103, bf16[2048,16]{1,0:T(8,128)(2,1)S(1)} %get-tuple-element.102, ...), dimensions={1} | concatenate | bytes 6684672 | tf_op jit(solution)/shard_map/concatenate | solution.py:545
  120.6 6.6 %fusion.141 = f32[1024,816]{0,1:T(8,128)S(1)} fusion(bf16[1024,2048]{1,0:T(8,128)(2,1)} %fusion.2, bf16[2048,816]{1,0:T(8,128)(2,1)} %concatenate.107), kind=kOutput, calls=%fused_computation.346 | convolution fusion | flops 3422552064 | bytes 10878976 | tf_op jit(solution)/shard_map/dot_general | solution.py:25
  138.6 6.1 %head_attention.1 = (bf16[1024,256]{1,0:T(8,128)(2,1)S(1)}, bf16[1024,256]{1,0:T(8,128)(2,1)S(1)}, bf16[1024,256]{1,0:T(8,128)(2,1)S(1)}, bf16[1024,256]{1,0:T(8,128)(2,1)S(1)}) custom-call(s32[1]{0:T(128)S(6)} %copy.137.length_ref, f32[1024,256]{1,0:T(8,128)S(1)} %get-tuple-element.85.q_ref, f32[1024,256]{1,0:T(8,128)S(1)} %get-tuple-element.84.k_ref, ...), custom_call_target="tpu_custom_call" | custom-call | flops 805306368 | bytes 6291456 | tf_op jit(solution)/shard_map/head_attention/pallas_call | solution.py:129
  154.5 48.2 %reduce-scatter.5.cloned.1.call-done = bf16[128,2048]{1,0:T(8,128)(2,1)} async-done(((bf16[1024,2048]{1,0:T(8,128)(2,1)}), bf16[128,2048]{1,0:T(8,128)(2,1)}) %reduce-scatter.5.cloned.1.call-update) | async-done | bytes 524304 | tf_op jit(solution)/shard_map/reduce_scatter | solution.py:447
  223.5 29.6 %all-gather.11.cloned.1.call-done = bf16[1024,2048]{1,0:T(8,128)(2,1)} async-done(((bf16[128,2048]{1,0:T(8,128)(2,1)}), bf16[1024,2048]{1,0:T(8,128)(2,1)}) %all-gather.11.cloned.1.call-update) | async-done | bytes 4194320 | tf_op jit(solution)/shard_map/all_gather | solution.py:563
  262.3 6.4 %fusion.144 = f32[1024,1440]{0,1:T(8,128)S(1)} fusion(bf16[1024,2048]{1,0:T(8,128)(2,1)S(1)} %copy-done.10, bf16[2048,1440]{0,1:T(8,128)(2,1)S(1)} %bitcast.249), kind=kOutput, calls=%fused_computation.349 | convolution fusion | flops 6039797760 | bytes 15990784 | tf_op jit(solution)/shard_map/dot_general | solution.py:25
  283.6 11.1 %fusion.143 = f32[576,2848]{1,0:T(8,128)} fusion(bf16[576,2048]{1,0:T(8,128)(2,1)} %convolution_convert_fusion.3, bf16[2048,2848]{1,0:T(8,128)(2,1)S(1)} %bitcast.245), kind=kOutput, calls=%fused_computation.348 | convolution fusion | flops 6719275008 | bytes 20586496 | tf_op jit(solution)/shard_map/dot_general | solution.py:25
  326.9 8.4 %fusion.130 = f32[576,1424]{1,0:T(8,128)S(1)} fusion(bf16[1424,2048]{1,0:T(8,128)(2,1)} %pad_maximum_fusion.1, f32[576,2048]{1,0:T(8,128)} %get-tuple-element.163, f32[576]{0:T(1024)S(1)} %get-tuple-element.71), kind=kOutput, calls=%fused_computation.336 | convolution fusion | flops 3361996800 | bytes 13834496 | tf_op jit(solution)/shard_map/dot_general | solution.py:167
  343.7 10.5 %convolution_convert_fusion.2 = bf16[576,2048]{1,0:T(8,128)(2,1)} fusion(bf16[576,2848]{1,0:T(8,128)(2,1)} %pad_maximum_fusion.2, bf16[2048,2848]{1,0:T(8,128)(2,1)S(1)} %bitcast.247), kind=kOutput, calls=%fused_computation.36 | convolution fusion | flops 6720454656 | bytes 17305600 | tf_op jit(solution)/shard_map/dot_general | solution.py:167
  359.7 11.7 %add_convert_fusion.1 = bf16[1024,2048]{1,0:T(8,128)(2,1)} fusion(f32[1024,2048]{1,0:T(8,128)S(1)} %fusion.13, bf16[1024,1440]{0,1:T(8,128)(2,1)S(1)} %copy-done.31, bf16[2048,1440]{0,1:T(8,128)(2,1)} %pad_maximum_fusion), kind=kOutput, calls=%fused_computation.10 | convolution fusion | flops 6043992064 | bytes 21430272 | tf_op jit(solution)/shard_map/dot_general | solution.py:167
  384.4 37.0 %reduce-scatter.9.cloned.1.call-done = bf16[128,2048]{1,0:T(8,128)(2,1)} async-done(((bf16[1024,2048]{1,0:T(8,128)(2,1)}), bf16[128,2048]{1,0:T(8,128)(2,1)}) %reduce-scatter.9.cloned.1.call-update) | async-done | bytes 524304 | tf_op jit(solution)/shard_map/reduce_scatter | solution.py:447
  452.2 6.0 %collective-permute-done.7 = bf16[16,10496]{1,0:T(8,128)(2,1)} collective-permute-done((bf16[16,10496]{1,0:T(8,128)(2,1)}, bf16[16,10496]{1,0:T(8,128)(2,1)}, u32[]{:S(2)}, u32[]{:S(2)}) %collective-permute-start.7) | collective-permute-done | bytes 335904 | tf_op jit(solution)/shard_map/ppermute | solution.py:694
  461.3 11.9 %all-gather.13.cloned.1.call-done = bf16[1024,2048]{1,0:T(8,128)(2,1)} async-done(((bf16[128,2048]{1,0:T(8,128)(2,1)}), bf16[1024,2048]{1,0:T(8,128)(2,1)}) %all-gather.13.cloned.1.call-update) | async-done | bytes 4194320 | tf_op jit(solution)/shard_map/all_gather | solution.py:671
  479.5 8.2 %head_attention_back.1 = (bf16[1024,256]{1,0:T(8,128)(2,1)S(1)}, bf16[1024,256]{1,0:T(8,128)(2,1)S(1)}, bf16[1024,256]{1,0:T(8,128)(2,1)S(1)}) custom-call(s32[1]{0:T(128)S(6)} %copy.137.length_ref, bf16[1024,256]{1,0:T(8,128)(2,1)S(1)} %get-tuple-element.54.q_ref, bf16[1024,256]{1,0:T(8,128)(2,1)S(1)} %copy-done.5, bf16[1024,256]{1,0:T(8,128)(2,1)S(1)} %copy-done.7, ...), custom_call_target="tpu_custom_call" | custom-call | flops 1879048192 | bytes 4194304 | tf_op jit(solution)/shard_map/head_attention_back/pallas_call | solution.py:148
  491.6 6.2 %convolution_convert_fusion = bf16[1024,2048]{1,0:T(8,128)(2,1)} fusion(bf16[2048,816]{1,0:T(8,128)(2,1)S(1)} %copy-done.29, bf16[1024,48]{1,0:T(8,128)(2,1)S(1)} %convolution_convert_fusion.13, bf16[1024,768]{1,0:T(8,128)(2,1)S(1)} %pad_maximum_fusion.13), kind=kOutput, calls=%fused_computation.25 | convolution fusion | flops 3427991552 | bytes 9207808 | tf_op jit(solution)/shard_map/dot_general | solution.py:167
  502.2 5.7 all-to-all-start.1
  512.9 13.6 %all-to-all-done.1 = bf16[8,2,19648]{2,1,0:T(2,128)(2,1)} async-done(((bf16[8,2,19648]{2,1,0:T(2,128)(2,1)}), bf16[8,2,19648]{2,1,0:T(2,128)(2,1)}, u32[]{:S(2)}, u32[]{:S(2)}) %all-to-all-start.1) | async-done | bytes 628768 | tf_op jit(solution)/shard_map/all_to_all | solution.py:311
  530.4 9.6 %all-gather.1 = bf16[4,2,41728]{2,1,0:T(2,128)(2,1)S(1)} all-gather(bf16[1,2,41728]{2,1,0:T(2,128)(2,1)S(1)} %bitcast.257), channel_id=2, replica_groups=mesh['dp'=4,'expert'=8] {'dp'}, dimensions={0}, use_global_device_ids=true | all-gather | bytes 834560 | tf_op jit(solution)/shard_map/all_gather | solution.py:324
  564.0 8.2 %reduce-scatter.11.cloned.1.call-done = bf16[128,2048]{1,0:T(8,128)(2,1)} async-done(((bf16[1024,2048]{1,0:T(8,128)(2,1)}), bf16[128,2048]{1,0:T(8,128)(2,1)}) %reduce-scatter.11.cloned.1.call-update) | async-done | bytes 524304 | tf_op jit(solution)/shard_map/reduce_scatter | solution.py:447
  (451 shorter events, 260.8 us)
Async XLA Ops:
  7.2 265.2 %copy-start = (bf16[5632,128]{1,0:T(8,128)(2,1)S(1)}, bf16[5632,128]{1,0:T(8,128)(2,1)}, u32[]{:S(2)}) copy-start(bf16[5632,128]{1,0:T(8,128)(2,1)} %param.48) | copy-start | bytes 4325380
  7.2 100.2 %all-gather.7.cloned.1.call-start = ((), (), s32[]{:S(2)}) async-start(), calls=%async_computation.6 | async-start | bytes 4718592 | tf_op jit(solution)/shard_map/all_gather | solution.py:449
  7.9 138.4 %all-gather.9.cloned.1.call-start = ((), (), s32[]{:S(2)}) async-start(), calls=%async_computation.7 | async-start | bytes 4718592 | tf_op jit(solution)/shard_map/all_gather | solution.py:454
  10.1 44.1 %collective-permute-start = (bf16[512,256]{1,0:T(8,128)(2,1)}, bf16[512,256]{1,0:T(8,128)(2,1)}, u32[]{:S(2)}, u32[]{:S(2)}) collective-permute-start(bf16[512,256]{1,0:T(8,128)(2,1)} %get-tuple-element.93), channel_id=1, source_target_pairs={{0,0},{1,3},{2,6},{3,1},{4,4},{5,7},{6,2},{7,5},{8,8},{9,11},{10,1... | collective-permute-start | bytes 786440 | tf_op jit(solution)/shard_map/ppermute | solution.py:227
  12.2 42.0 %collective-permute-start.1 = (bf16[512,256]{1,0:T(8,128)(2,1)}, bf16[512,256]{1,0:T(8,128)(2,1)}, u32[]{:S(2)}, u32[]{:S(2)}) collective-permute-start(bf16[512,256]{1,0:T(8,128)(2,1)} %get-tuple-element.94), channel_id=1, source_target_pairs={{0,1},{1,4},{2,7},{3,2},{4,5},{5,0},{6,3},{7,6},{8,9},{9,12},{10,1... | collective-permute-start | bytes 786440 | tf_op jit(solution)/shard_map/ppermute | solution.py:227
  15.3 38.8 %collective-permute-start.2 = (bf16[512,256]{1,0:T(8,128)(2,1)}, bf16[512,256]{1,0:T(8,128)(2,1)}, u32[]{:S(2)}, u32[]{:S(2)}) collective-permute-start(bf16[512,256]{1,0:T(8,128)(2,1)} %get-tuple-element.95), channel_id=1, source_target_pairs={{0,2},{1,5},{2,0},{3,3},{4,6},{5,1},{6,4},{7,7},{8,10},{9,13},{10,... | collective-permute-start | bytes 786440 | tf_op jit(solution)/shard_map/ppermute | solution.py:227
  18.9 183.8 %reduce-scatter.5.cloned.1.call-start = ((), (), s32[]{:S(2)}) async-start(), calls=%async_computation.8 | async-start | bytes 4718592 | tf_op jit(solution)/shard_map/reduce_scatter | solution.py:447
  56.7 46.2 %collective-permute-start.4 = (bf16[3,512,256]{2,1,0:T(8,128)(2,1)}, bf16[3,512,256]{2,1,0:T(8,128)(2,1)}, u32[]{:S(2)}, u32[]{:S(2)}) collective-permute-start(bf16[3,512,256]{2,1,0:T(8,128)(2,1)} %get-tuple-element.111), channel_id=1, source_target_pairs={{0,16},{8,24},{16,0},{24,8},{1,17},{9,25},{17,1},{25,9},{2,18},{10... | collective-permute-start | bytes 2359304 | tf_op jit(solution)/shard_map/ppermute | solution.py:244
  58.0 45.0 %collective-permute-start.3 = (bf16[3,512,256]{2,1,0:T(8,128)(2,1)}, bf16[3,512,256]{2,1,0:T(8,128)(2,1)}, u32[]{:S(2)}, u32[]{:S(2)}) collective-permute-start(bf16[3,512,256]{2,1,0:T(8,128)(2,1)} %get-tuple-element.111), channel_id=1, source_target_pairs={{0,8},{8,0},{16,24},{24,16},{1,9},{9,1},{17,25},{25,17},{2,10},{10... | collective-permute-start | bytes 2359304 | tf_op jit(solution)/shard_map/ppermute | solution.py:244
  58.2 44.7 %collective-permute-start.5 = (bf16[3,512,256]{2,1,0:T(8,128)(2,1)}, bf16[3,512,256]{2,1,0:T(8,128)(2,1)}, u32[]{:S(2)}, u32[]{:S(2)}) collective-permute-start(bf16[3,512,256]{2,1,0:T(8,128)(2,1)} %get-tuple-element.111), channel_id=1, source_target_pairs={{0,24},{8,16},{16,8},{24,0},{1,25},{9,17},{17,9},{25,1},{2,26},{10... | collective-permute-start | bytes 2359304 | tf_op jit(solution)/shard_map/ppermute | solution.py:244
  154.3 98.8 %all-gather.11.cloned.1.call-start = ((), (), s32[]{:S(2)}) async-start(), calls=%async_computation.9 | async-start | bytes 4718592 | tf_op jit(solution)/shard_map/all_gather | solution.py:563
  207.2 164.3 %reduce-scatter.7.cloned.1.call-start = ((), (), s32[]{:S(2)}) async-start(), calls=%async_computation.10 | async-start | bytes 4718592 | tf_op jit(solution)/shard_map/reduce_scatter | solution.py:447
  256.8 55.1 %copy-start.47 = (f32[1024,25]{0,1:T(8,128)}, f32[1024,25]{0,1:T(8,128)S(1)}, u32[]{:S(2)}) copy-start(f32[1024,25]{0,1:T(8,128)S(1)} %fusion.72) | copy-start | bytes 307204
  321.5 99.9 %reduce-scatter.9.cloned.1.call-start = ((), (), s32[]{:S(2)}) async-start(), calls=%async_computation.11 | async-start | bytes 4718592 | tf_op jit(solution)/shard_map/reduce_scatter | solution.py:447
  371.6 54.3 %copy-start.26 = (bf16[128,2048]{1,0:T(8,128)(2,1)S(1)}, bf16[128,2048]{1,0:T(8,128)(2,1)}, u32[]{:S(2)}) copy-start(bf16[128,2048]{1,0:T(8,128)(2,1)} %param.28) | copy-start | bytes 1572868
  372.9 9.8 %all-to-all-start = ((f32[8,16,128]{2,1,0:T(8,128)}), f32[8,16,128]{2,1,0:T(8,128)S(1)}, u32[]{:S(2)}, u32[]{:S(2)}) async-start(f32[8,16,128]{2,1,0:T(8,128)} %maximum_bitcast_fusion.2), calls=%async_computation.3 | async-start | bytes 131072 | tf_op jit(solution)/shard_map/all_to_all | solution.py:647
  377.5 95.7 %all-gather.13.cloned.1.call-start = ((), (), s32[]{:S(2)}) async-start(), calls=%async_computation.12 | async-start | bytes 4718592 | tf_op jit(solution)/shard_map/all_gather | solution.py:671
  440.5 11.7 %collective-permute-start.8 = (bf16[16,10496]{1,0:T(8,128)(2,1)}, bf16[16,10496]{1,0:T(8,128)(2,1)}, u32[]{:S(2)}, u32[]{:S(2)}) collective-permute-start(bf16[16,10496]{1,0:T(8,128)(2,1)} %constant_dynamic-update-slice_fusion), channel_id=1, source_target_pairs={{0,24},{8,16},{16,8},{24,0},{1,25},{9,17},{17,9},{25,1},{2,26},{10... | collective-permute-start | bytes 1007624 | tf_op jit(solution)/shard_map/ppermute | solution.py:694
  441.7 16.6 %collective-permute-start.7 = (bf16[16,10496]{1,0:T(8,128)(2,1)}, bf16[16,10496]{1,0:T(8,128)(2,1)}, u32[]{:S(2)}, u32[]{:S(2)}) collective-permute-start(bf16[16,10496]{1,0:T(8,128)(2,1)} %constant_dynamic-update-slice_fusion), channel_id=1, source_target_pairs={{0,16},{8,24},{16,0},{24,8},{1,17},{9,25},{17,1},{25,9},{2,18},{10... | collective-permute-start | bytes 1007624 | tf_op jit(solution)/shard_map/ppermute | solution.py:694
  442.0 16.3 %collective-permute-start.6 = (bf16[16,10496]{1,0:T(8,128)(2,1)}, bf16[16,10496]{1,0:T(8,128)(2,1)}, u32[]{:S(2)}, u32[]{:S(2)}) collective-permute-start(bf16[16,10496]{1,0:T(8,128)(2,1)} %constant_dynamic-update-slice_fusion), channel_id=1, source_target_pairs={{0,8},{8,0},{16,24},{24,16},{1,9},{9,1},{17,25},{25,17},{2,10},{10... | collective-permute-start | bytes 1007624 | tf_op jit(solution)/shard_map/ppermute | solution.py:694
  502.2 24.4 %all-to-all-start.1 = ((bf16[8,2,19648]{2,1,0:T(2,128)(2,1)}), bf16[8,2,19648]{2,1,0:T(2,128)(2,1)}, u32[]{:S(2)}, u32[]{:S(2)}) async-start(bf16[8,2,19648]{2,1,0:T(2,128)(2,1)} %reshape.214), calls=%async_computation.5 | async-start | bytes 1261568 | tf_op jit(solution)/shard_map/all_to_all | solution.py:311
  507.9 64.3 %reduce-scatter.11.cloned.1.call-start = ((), (), s32[]{:S(2)}) async-start(), calls=%async_computation.13 | async-start | bytes 4718592 | tf_op jit(solution)/shard_map/reduce_scatter | solution.py:447
  543.1 15.2 %collective-permute-start.9 = (bf16[2,41600]{1,0:T(2,128)(2,1)S(1)}, bf16[2,41600]{1,0:T(2,128)(2,1)S(1)}, u32[]{:S(2)}, u32[]{:S(2)}) collective-permute-start(bf16[2,41600]{1,0:T(2,128)(2,1)S(1)} %get-tuple-element.141), channel_id=1, source_target_pairs={{0,0},{1,4},{2,1},{3,5},{4,2},{5,6},{6,3},{7,7},{8,8},{9,12},{10,9... | collective-permute-start | bytes 499208 | tf_op jit(solution)/shard_map/ppermute | solution.py:338
  545.0 13.2 %collective-permute-start.10 = (bf16[2,41600]{1,0:T(2,128)(2,1)S(1)}, bf16[2,41600]{1,0:T(2,128)(2,1)S(1)}, u32[]{:S(2)}, u32[]{:S(2)}) collective-permute-start(bf16[2,41600]{1,0:T(2,128)(2,1)S(1)} %get-tuple-element.142), channel_id=1, source_target_pairs={{0,4},{1,0},{2,5},{3,1},{4,6},{5,2},{6,7},{7,3},{8,12},{9,8},{10,1... | collective-permute-start | bytes 499208 | tf_op jit(solution)/shard_map/ppermute | solution.py:338
  (115 other events, 1010.0 us)
Sparse Core Ops, SparseCore 0:
  9.6 52.7 all-gather.6
  64.0 48.4 all-gather.8
  154.4 48.2 reduce-scatter.4
  207.3 45.7 all-gather.10
  321.7 48.2 reduce-scatter.6
  372.1 49.1 reduce-scatter.8
  427.2 45.8 all-gather.12
  511.0 61.1 reduce-scatter.10
